TPU v7x, 32 devices: a whole 2x2x4 slice. The times are simulated.
32 devices in a mesh: dp: 4 (over y, x), fsdp: 8 (over z, core).
Axes of the slice: x: 2, y: 2, z: 4, core: 2. Of those that a mesh axis runs over, the one named last changes fastest.
Arguments:
- tokens: bfloat16 [8192, 2048], P(('dp', 'fsdp')), may hold values from -6 to 6
- seq_lengths: int32 [32], P(('dp', 'fsdp')), may hold values from 256 to 256, as said below
- w_qkv: bfloat16 [2048, 6144], P(('dp', 'fsdp')), may hold values from -0.125 to 0.125
- bias_q: bfloat16 [2048], P(('dp', 'fsdp')), may hold values from -3 to 3
- bias_v: bfloat16 [2048], P(('dp', 'fsdp')), may hold values from -3 to 3
- w_out: bfloat16 [2048, 2048], P(('dp', 'fsdp')), may hold values from -0.375 to 0.375
- bias_out: bfloat16 [2048], P(('dp', 'fsdp')), may hold values from -2 to 2
- ln1_gain: bfloat16 [2048], P(('dp', 'fsdp')), may hold values from 0.5 to 1.5
- ln1_bias: bfloat16 [2048], P(('dp', 'fsdp')), may hold values from -1.1953125 to 1.1953125
- w_up: bfloat16 [2048, 8192], P(('dp', 'fsdp')), may hold values from -0.125 to 0.125
- bias_up: bfloat16 [8192], P(('dp', 'fsdp')), may hold values from -3 to 3
- w_down: bfloat16 [8192, 2048], P(('dp', 'fsdp')), may hold values from -0.0625 to 0.0625
- bias_down: bfloat16 [2048], P(('dp', 'fsdp')), may hold values from -2 to 2
- ln2_gain: bfloat16 [2048], P(('dp', 'fsdp')), may hold values from 0.5 to 1.5
- ln2_bias: bfloat16 [2048], P(('dp', 'fsdp')), may hold values from -1.1953125 to 1.1953125
- cotangent: bfloat16 [8192, 2048], P(('dp', 'fsdp')), may hold values from -6 to 6
Outputs:
- output: bfloat16 [8192, 2048], P(('dp', 'fsdp'))
- grad_tokens: bfloat16 [8192, 2048], P(('dp', 'fsdp'))
- grad_w_qkv: float32 [2048, 6144], P(('dp', 'fsdp'))
- grad_bias_q: float32 [2048], P(('dp', 'fsdp'))
- grad_bias_v: float32 [2048], P(('dp', 'fsdp'))
- grad_w_out: float32 [2048, 2048], P(('dp', 'fsdp'))
- grad_bias_out: float32 [2048], P(('dp', 'fsdp'))
- grad_ln1_gain: float32 [2048], P(('dp', 'fsdp'))
- grad_ln1_bias: float32 [2048], P(('dp', 'fsdp'))
- grad_w_up: float32 [2048, 8192], P(('dp', 'fsdp'))
- grad_bias_up: float32 [8192], P(('dp', 'fsdp'))
- grad_w_down: float32 [8192, 2048], P(('dp', 'fsdp'))
- grad_bias_down: float32 [2048], P(('dp', 'fsdp'))
- grad_ln2_gain: float32 [2048], P(('dp', 'fsdp'))
- grad_ln2_bias: float32 [2048], P(('dp', 'fsdp'))
- clipped_qkv: bfloat16 [2048, 6144], P(('dp', 'fsdp'))
Inputs may be any that keep to these rules, and one draw needn't show every extreme that they name: `seq_lengths`: each device's sequence starts at slot 0; the rest of its 256 slots are padding. Every sequence fills all 256 slots of its device, so no slot is padding.
All inputs are finite; a program needn't handle non-finite values.
Results may differ from a plain program's by a relative error of at most 0.012.
Values may be sent and summed in bfloat16 or wider, within the bound.
A program may use at most 384 MiB of HBM per device.

v0:
```python
import functools

import jax
import jax.numpy as jnp
from jax import lax
from jax.experimental import pallas as pl
from jax.experimental.pallas import tpu as pltpu
from jax.sharding import PartitionSpec as P


HEAD_DIM = 64
EPS = 1e-05
CLIP_TAU = 5.0
MASKED = 1e35
F32 = jnp.float32
BF16 = jnp.bfloat16
SCALE = HEAD_DIM ** (-0.5)


def swap(value, axis, size, bit):
    return lax.ppermute(value, axis, [(i, i ^ bit) for i in range(size)])


def bits_of(size):
    return [1 << b for b in range(size.bit_length() - 1)]


def gather_path(block, size, bits):
    blocks = {0: block}
    for bit in bits:
        held = sorted(blocks)
        moved = swap(jnp.concatenate([blocks[r] for r in held], 0), "dp", size, bit)
        for place, r in enumerate(held):
            rows = block.shape[0]
            blocks[r ^ bit] = moved[place * rows : (place + 1) * rows]
    return blocks


def gather_dp(block, size):
    half = block.shape[0] // 2
    top = gather_path(block[:half], size, bits_of(size))
    low = gather_path(block[half:], size, bits_of(size)[::-1])
    parts = []
    for r in range(size):
        parts += [top[r], low[r]]
    return jnp.concatenate(parts, 0)


def scatter_path(blocks, size, bits):
    blocks = dict(blocks)
    for bit in bits:
        away = sorted(r for r in blocks if r & bit)
        rows = blocks[0].shape[0]
        sent = jnp.concatenate([blocks[r].astype(BF16) for r in away], 0)
        moved = swap(sent, "dp", size, bit)
        blocks = {
            r ^ bit: blocks[r ^ bit].astype(F32)
            + moved[place * rows : (place + 1) * rows].astype(F32)
            for place, r in enumerate(away)
        }
    return blocks[0]


def scatter_dp(partial, size):
    rows = partial.shape[0] // size
    half = rows // 2
    top = {r: partial[r * rows : r * rows + half] for r in range(size)}
    low = {r: partial[r * rows + half : (r + 1) * rows] for r in range(size)}
    return jnp.concatenate(
        [scatter_path(top, size, bits_of(size)), scatter_path(low, size, bits_of(size)[::-1])], 0
    )


def combine_all(value, sizes, join):
    for axis, size in sizes:
        for bit in bits_of(size):
            value = join(value, swap(value, axis, size, bit))
    return value


STEPS = 4
MESH_IDS = pl.DeviceIdType.MESH
PATHS = ((1, 2), (2, 1))


def neighbours():
    me = lax.axis_index("dp")
    near = {1: {"dp": me + 1 - 2 * (me % 2)}, 2: {"dp": (me + 2) % 4}}
    barrier = pltpu.get_barrier_semaphore()
    for bit in (1, 2):
        pl.semaphore_signal(barrier, inc=1, device_id=near[bit], device_id_type=MESH_IDS)
    pl.semaphore_wait(barrier, 2)
    return near


def remote(source, target, sems, index, where):
    return pltpu.make_async_remote_copy(
        src_ref=source, dst_ref=target, send_sem=sems.at[0, index], recv_sem=sems.at[1, index],
        device_id=where, device_id_type=MESH_IDS,
    )


def each_step(act):
    def run(step, carry):
        act(step)
        return carry

    lax.fori_loop(0, STEPS, run, 0)


class Gather:
    def __init__(self, out, sems, near):
        self.out, self.sems, self.near = out, sems, near
        self.rows = out.shape[0] // 4
        self.step_rows = self.rows // 2 // STEPS

    def span(self, block, path, step):
        start = block * self.rows + path * (self.rows // 2) + step * self.step_rows
        return pl.ds(pl.multiple_of(start, self.step_rows), self.step_rows)

    def copy(self, source, bit, path, step, kind):
        return remote(
            self.out.at[self.span(source, path, step)],
            self.out.at[self.span(source + bit, path, step)],
            self.sems, (path * 3 + kind) * STEPS + step, self.near[bit],
        )

    def send(self, path, step):
        first, second = PATHS[path]
        self.copy(0, first, path, step, 0).start()
        self.copy(0, second, path, step, 1).start()

    def forward(self, path, step):
        first, second = PATHS[path]
        self.copy(0, first, path, step, 0).wait_recv()
        self.copy(first, second, path, step, 2).start()

    def finish(self, path, step):
        first, second = PATHS[path]
        self.copy(0, first, path, step, 0).wait_send()
        self.copy(0, second, path, step, 1).wait()
        self.copy(first, second, path, step, 2).wait()


class Scatter:
    def __init__(self, partial, landing, passing, last, sems, near):
        self.partial, self.landing, self.passing, self.last = partial, landing, passing, last
        self.sems, self.near = sems, near
        self.rows = partial.shape[0] // 4
        self.step_rows = self.rows // 2 // STEPS

    def span(self, block, path, step):
        start = block * self.rows + path * (self.rows // 2) + step * self.step_rows
        return pl.ds(pl.multiple_of(start, self.step_rows), self.step_rows)

    def own(self, path, step):
        return self.span(0, path, step)

    def opening(self, path, step, kind):
        first, _ = PATHS[path]
        return remote(
            self.partial.at[self.span((first, 3)[kind], path, step)],
            self.landing.at[kind, self.own(path, step)],
            self.sems, (path * 3 + kind) * STEPS + step, self.near[first],
        )

    def closing(self, path, step):
        rows = self.own(path, step)
        return remote(
            self.passing.at[rows], self.last.at[rows], self.sems,
            (path * 3 + 2) * STEPS + step, self.near[PATHS[path][1]],
        )

    def begin(self, path, step):
        for kind in range(2):
            self.opening(path, step, kind).start()

    def relay(self, path, step):
        _, second = PATHS[path]
        self.opening(path, step, 1).wait_recv()
        rows = self.own(path, step)
        self.passing[rows] = (
            self.partial[self.span(second, path, step)].astype(F32)
            + self.landing[1, rows].astype(F32)
        ).astype(BF16)
        self.closing(path, step).start()

    def total(self, path, step):
        self.opening(path, step, 0).wait_recv()
        self.closing(path, step).wait_recv()
        rows = self.own(path, step)
        return (
            self.partial[self.span(0, path, step)].astype(F32)
            + self.landing[0, rows].astype(F32)
            + self.last[rows].astype(F32)
        )

    def finish(self, path, step):
        for kind in range(2):
            self.opening(path, step, kind).wait_send()
        self.closing(path, step).wait_send()


def row_norm(values):
    centred = values - jnp.mean(values, axis=-1, keepdims=True)
    inverse_std = lax.rsqrt(jnp.mean(centred * centred, axis=-1, keepdims=True) + EPS)
    return centred * inverse_std, inverse_std


def row_back(grad_norm, normed, inverse_std, gain):
    scaled = grad_norm * gain
    return inverse_std * (
        scaled
        - jnp.mean(scaled, axis=-1, keepdims=True)
        - normed * jnp.mean(scaled * normed, axis=-1, keepdims=True)
    )


def gather_two_kernel(one_ref, two_ref, out_one, out_two, sems):
    near = neighbours()
    jobs = []
    for k, (source, out) in enumerate(((one_ref, out_one), (two_ref, out_two))):
        out[: source.shape[0]] = source[...]
        jobs.append(Gather(out, sems.at[k], near))
    for job in jobs:
        each_step(lambda step, job=job: [job.send(path, step) for path in range(2)])
    for job in jobs:
        each_step(lambda step, job=job: [job.forward(path, step) for path in range(2)])
    for job in jobs:
        each_step(lambda step, job=job: [job.finish(path, step) for path in range(2)])


def exchange(scatter, gather, rows_of):
    each_step(lambda step: [scatter.begin(path, step) for path in range(2)])
    each_step(lambda step: [scatter.relay(path, step) for path in range(2)])

    def middle(step):
        for path in range(2):
            rows = scatter.own(path, step)
            gather.out[rows] = rows_of(rows, scatter.total(path, step))
            gather.send(path, step)

        @pl.when(step > 0)
        def _():
            for path in range(2):
                gather.forward(path, step - 1)

    each_step(middle)
    for path in range(2):
        gather.forward(path, STEPS - 1)
    each_step(lambda step: [scatter.finish(path, step) for path in range(2)])
    each_step(lambda step: [gather.finish(path, step) for path in range(2)])


def add_sums(sums_ref, values):
    for k, value in enumerate(values):
        sums_ref[k : k + 1] += jnp.sum(value, axis=0, keepdims=True)


def hidden_kernel(
    partial_ref, tokens_ref, params_ref, out_ref, hidden_ref, landing, passing, last, sems
):
    near = neighbours()

    def rows_of(rows, total):
        hidden = tokens_ref[rows].astype(F32) + total + params_ref[0:1]
        hidden_ref[rows] = hidden
        normed, _ = row_norm(hidden)
        return (normed * params_ref[1:2] + params_ref[2:3]).astype(BF16)

    exchange(
        Scatter(partial_ref, landing, passing, last, sems.at[0], near),
        Gather(out_ref, sems.at[1], near), rows_of,
    )


def branch_kernel(
    partial_ref, hidden_ref, cotangent_ref, params_ref, out_ref, grad_ref, sums_ref, landing,
    passing, last, sems,
):
    near = neighbours()
    sums_ref[...] = jnp.zeros_like(sums_ref)

    def rows_of(rows, total):
        normed, inverse_std = row_norm(hidden_ref[rows])
        upper = cotangent_ref[rows].astype(F32)
        grad = upper + row_back(total, normed, inverse_std, params_ref[1:2])
        grad_ref[rows] = grad
        branch = grad.astype(BF16)
        add_sums(sums_ref, (upper, total * normed, total, branch.astype(F32)))
        return branch

    exchange(
        Scatter(partial_ref, landing, passing, last, sems.at[0], near),
        Gather(out_ref, sems.at[1], near), rows_of,
    )


def last_kernel(
    first_ref, output_ref, tokens_ref, hidden_ref, grad_ref, params_ref, tokens_out, output_out,
    sums_ref, landing, passing, last, sems,
):
    near = neighbours()
    sums_ref[...] = jnp.zeros_like(sums_ref)
    first, second = (
        Scatter(ref, landing.at[k], passing.at[k], last.at[k], sems.at[k], near)
        for k, ref in enumerate((first_ref, output_ref))
    )

    def first_rows(path, step):
        rows = first.own(path, step)
        total = first.total(path, step)
        normed, inverse_std = row_norm(tokens_ref[rows].astype(F32))
        grad = grad_ref[rows] + row_back(total, normed, inverse_std, params_ref[0:1])
        tokens_out[rows] = grad.astype(BF16)
        add_sums(sums_ref, (total * normed, total))

    def second_rows(path, step):
        rows = second.own(path, step)
        total = second.total(path, step)
        output_out[rows] = (hidden_ref[rows] + total + params_ref[1:2]).astype(BF16)

    for job in (first, second):
        each_step(lambda step, job=job: [job.begin(path, step) for path in range(2)])
    for job in (first, second):
        each_step(lambda step, job=job: [job.relay(path, step) for path in range(2)])
    each_step(lambda step: [first_rows(path, step) for path in range(2)])
    each_step(lambda step: [second_rows(path, step) for path in range(2)])
    for job in (first, second):
        each_step(lambda step, job=job: [job.finish(path, step) for path in range(2)])


def call_exchange(kernel, number, jobs, scatters, outs, args):
    rows, width = args[0].shape if scatters else (4 * args[0].shape[0], args[0].shape[1])
    own = rows // 4
    room = []
    if scatters == 1:
        room = [(2, own, width), (own, width), (own, width)]
    if scatters == 2:
        room = [(2, 2, own, width), (2, own, width), (2, own, width)]
    return pl.pallas_call(
        kernel,
        in_specs=[pl.BlockSpec(memory_space=pltpu.VMEM)] * len(args),
        out_specs=[pl.BlockSpec(memory_space=pltpu.VMEM)] * len(outs),
        out_shape=[jax.ShapeDtypeStruct(shape, dtype) for shape, dtype in outs],
        scratch_shapes=[
            *(pltpu.VMEM(shape, BF16) for shape in room),
            pltpu.SemaphoreType.DMA((jobs, 2, 6 * STEPS)),
        ],
        compiler_params=pltpu.CompilerParams(
            collective_id=number, has_side_effects=True, vmem_limit_bytes=48 << 20
        ),
        cost_estimate=pl.CostEstimate(
            flops=rows * width, bytes_accessed=200 << 20, transcendentals=0
        ),
    )(*args)


def pair_span(offset, pair):
    return pl.ds(pl.multiple_of(offset + pair * 2 * HEAD_DIM, 2 * HEAD_DIM), 2 * HEAD_DIM)


def head_parts(ref, offset, pair):
    both = ref[:, pair_span(offset, pair)]
    return both[:, :HEAD_DIM], both[:, HEAD_DIM:]


def dot_nt(a, b):
    return lax.dot_general(a, b, (((1,), (1,)), ((), ())), preferred_element_type=F32)


def dot_tn(a, b):
    return lax.dot_general(a, b, (((0,), (0,)), ((), ())), preferred_element_type=F32)


def attend_kernel(slope_ref, distance_ref, qkv_ref, mixed_ref, top_ref):
    width = mixed_ref.shape[1]
    lane = lax.broadcasted_iota(jnp.int32, (8, 128), 1)

    def pair_step(pair, tops):
        distance = distance_ref[...]
        outs = []
        for t, (q, k, v) in enumerate(
            zip(*(head_parts(qkv_ref, part * width, pair) for part in range(3)))
        ):
            logits = dot_nt(q * jnp.asarray(SCALE, BF16), k)
            head_top = jnp.max(jnp.where(distance < MASKED, logits, -1e30))
            tops = jnp.where(lane == pair * 2 + t, head_top, tops)
            scores = logits - slope_ref[pair * 2 + t] * distance
            expos = jnp.exp(scores - jnp.max(scores, axis=-1, keepdims=True))
            probs = expos * (1.0 / jnp.sum(expos, axis=-1, keepdims=True))
            outs.append(jnp.dot(probs.astype(BF16), v, preferred_element_type=F32))
        mixed_ref[:, pair_span(0, pair)] = jnp.concatenate(outs, 1).astype(BF16)
        return tops

    pairs = width // HEAD_DIM // 2
    top_ref[...] = lax.fori_loop(0, pairs, pair_step, jnp.zeros((8, 128), F32))


def attend_back_kernel(slope_ref, distance_ref, qkv_ref, grad_ref, out_ref):
    width = grad_ref.shape[1]

    def pair_step(pair, carry):
        distance = distance_ref[...]
        outs = ([], [], [])
        parts = [head_parts(qkv_ref, part * width, pair) for part in range(3)]
        parts.append(head_parts(grad_ref, 0, pair))
        for t, (q, k, v, grad) in enumerate(zip(*parts)):
            low_q = q * jnp.asarray(SCALE, BF16)
            scores = dot_nt(low_q, k) - slope_ref[pair * 2 + t] * distance
            expos = jnp.exp(scores - jnp.max(scores, axis=-1, keepdims=True))
            probs = expos * (1.0 / jnp.sum(expos, axis=-1, keepdims=True))
            outs[2].append(dot_tn(probs.astype(BF16), grad))
            grad_probs = dot_nt(grad, v)
            inner = jnp.sum(grad_probs * probs, axis=-1, keepdims=True)
            grad_scores = (probs * (grad_probs - inner)).astype(BF16)
            outs[0].append(jnp.dot(grad_scores, k, preferred_element_type=F32) * SCALE)
            outs[1].append(dot_tn(grad_scores, low_q))
        for part in range(3):
            out_ref[:, pair_span(part * width, pair)] = jnp.concatenate(outs[part], 1).astype(BF16)
        return carry

    lax.fori_loop(0, width // HEAD_DIM // 2, pair_step, 0)


def attend(slopes, distance, qkv, length):
    rows, width = qkv.shape[0], qkv.shape[1] // 3
    blocks = rows // length
    mixed, tops = pl.pallas_call(
        attend_kernel,
        grid=(blocks,),
        in_specs=[
            pl.BlockSpec(memory_space=pltpu.SMEM),
            pl.BlockSpec((length, length), lambda b: (0, 0)),
            pl.BlockSpec((length, 3 * width), lambda b: (b, 0)),
        ],
        out_specs=[
            pl.BlockSpec((length, width), lambda b: (b, 0)),
            pl.BlockSpec((8, 128), lambda b: (b, 0)),
        ],
        out_shape=[
            jax.ShapeDtypeStruct((rows, width), BF16),
            jax.ShapeDtypeStruct((blocks * 8, 128), F32),
        ],
        cost_estimate=pl.CostEstimate(
            flops=4 * rows * length * width, bytes_accessed=8 * rows * width,
            transcendentals=rows * length * width // HEAD_DIM,
        ),
        name="attend",
    )(slopes, distance, qkv)
    return mixed, jnp.max(tops, axis=0)[: width // HEAD_DIM]


def attend_back(slopes, distance, qkv, grad, length):
    rows, width = grad.shape
    return pl.pallas_call(
        attend_back_kernel,
        grid=(rows // length,),
        in_specs=[
            pl.BlockSpec(memory_space=pltpu.SMEM),
            pl.BlockSpec((length, length), lambda b: (0, 0)),
            pl.BlockSpec((length, 3 * width), lambda b: (b, 0)),
            pl.BlockSpec((length, width), lambda b: (b, 0)),
        ],
        out_specs=pl.BlockSpec((length, 3 * width), lambda b: (b, 0)),
        out_shape=jax.ShapeDtypeStruct((rows, 3 * width), BF16),
        cost_estimate=pl.CostEstimate(
            flops=10 * rows * length * width, bytes_accessed=14 * rows * width,
            transcendentals=rows * length * width // HEAD_DIM,
        ),
        name="attend_back",
    )(slopes, distance, qkv, grad)


def norm_stats(values):
    row_mean = jnp.mean(values, axis=-1, keepdims=True)
    centred = values - row_mean
    inverse_std = lax.rsqrt(jnp.mean(centred * centred, axis=-1, keepdims=True) + EPS)
    return centred * inverse_std, inverse_std


def norm_back(grad_norm, normed, inverse_std, gain):
    scaled = grad_norm * gain
    return inverse_std * (
        scaled
        - jnp.mean(scaled, axis=-1, keepdims=True)
        - normed * jnp.mean(scaled * normed, axis=-1, keepdims=True)
    )


def dot(a, b):
    return jnp.dot(a, b, preferred_element_type=F32)


def layer(
    dp, fsdp, tokens, seq_lengths, w_qkv, bias_q, bias_v, w_out, bias_out, ln1_gain, ln1_bias,
    w_up, bias_up, w_down, bias_down, ln2_gain, ln2_bias, cotangent,
):
    length, width = tokens.shape
    shard = w_qkv.shape[0]
    ff = w_up.shape[1]
    heads = width // HEAD_DIM
    part, ff_part = width // dp, ff // dp
    local_heads = heads // dp
    spot, place = lax.axis_index("dp"), lax.axis_index("fsdp")
    rank = spot * fsdp + place
    both = (("fsdp", fsdp), ("dp", dp))

    full_small = (bias_out, ln1_gain, ln1_bias, bias_down, ln2_gain, ln2_bias)
    row = jnp.concatenate(full_small + (bias_q, bias_v, bias_up))[None]
    table = jnp.zeros((dp * fsdp, row.shape[1]), BF16)
    table = lax.dynamic_update_slice(table, row, (rank, 0))
    table = combine_all(table, both, jnp.add).astype(F32)
    small = [table[:, k * shard : (k + 1) * shard].reshape(1, width) for k in range(6)]
    out_b, gain1, shift1, down_b, gain2, shift2 = small
    mine = lax.dynamic_slice(table, (spot * fsdp, 0), (fsdp, row.shape[1]))[:, 6 * shard :]
    q_b, v_b = mine[:, :shard].reshape(1, part), mine[:, shard : 2 * shard].reshape(1, part)
    up_b = mine[:, 2 * shard :].reshape(1, ff_part)

    out_w = lax.all_gather(w_out, "fsdp", axis=0, tiled=True)
    cols = w_qkv.reshape(shard, 3, dp, part).transpose(0, 2, 1, 3).reshape(shard, 3 * width)
    cols = lax.all_to_all(cols, "dp", 1, 0, tiled=True).reshape(dp, shard, 3 * part)
    qkv_w = lax.all_gather(cols, "fsdp", axis=1, tiled=True).reshape(width, 3 * part)
    w_up, cols = lax.optimization_barrier((w_up, cols))
    ups = lax.all_to_all(w_up, "dp", 1, 0, tiled=True).reshape(dp, shard, ff_part)
    up_w = lax.all_gather(ups, "fsdp", axis=1, tiled=True).reshape(width, ff_part)
    down_w = lax.all_gather(w_down, "fsdp", axis=0, tiled=True)

    ranks = (spot * local_heads + 1 + jnp.arange(local_heads)).astype(F32)
    slopes = jnp.exp2(-8.0 * ranks / heads) * SCALE
    places = jnp.arange(length, dtype=jnp.int32)
    gap = places[:, None] - places[None, :]
    distance = jnp.where(gap >= 0, gap.astype(F32), MASKED)

    inputs = tokens.astype(F32)
    wide = (4 * length, width)
    narrow = (length, width)
    kernels = dp == 4 and length % (32 * STEPS) == 0
    ordered_tokens, ups, cols = lax.optimization_barrier((tokens, ups, cols))
    if kernels:
        all_tokens, grad_y = call_exchange(
            gather_two_kernel, 1, 2, 0, [(wide, BF16)] * 2,
            [ordered_tokens, cotangent],
        )
    else:
        all_tokens, grad_y = gather_dp(ordered_tokens, dp), gather_dp(cotangent, dp)
    normed_all, _ = norm_stats(all_tokens.astype(F32))
    first_in = (normed_all * gain1 + shift1).astype(BF16)
    biases = jnp.concatenate([q_b, jnp.zeros_like(q_b), v_b], 1)
    qkv = (dot(first_in, qkv_w) + biases).astype(BF16)
    mixed, tops = attend(slopes, distance, qkv, length)
    out_part = dot(mixed, out_w).astype(BF16)
    if kernels:
        second_in, hidden = call_exchange(
            hidden_kernel, 2, 2, 1, [(wide, BF16), (narrow, F32)],
            [out_part, tokens, jnp.concatenate([out_b, gain2, shift2], 0)],
        )
    else:
        hidden = inputs + scatter_dp(out_part, dp) + out_b
        normed2, inverse2 = norm_stats(hidden)
        second_in = gather_dp((normed2 * gain2 + shift2).astype(BF16), dp)

    upward = dot(second_in, up_w) + up_b
    cumulative = 0.5 * (1.0 + lax.erf(upward * (0.5**0.5)))
    active = (upward * cumulative).astype(BF16)
    slope = cumulative + upward * jnp.exp(-0.5 * upward * upward) * ((0.5 / jnp.pi) ** 0.5)
    active, slope = lax.optimization_barrier((active, slope.astype(BF16)))

    def reduce_rows(grad):
        return lax.psum_scatter(grad, "fsdp", scatter_dimension=0, tiled=True).astype(F32)

    def reduce_columns(grad):
        grad = grad.reshape(dp, fsdp * shard, grad.shape[1])
        grad = lax.psum_scatter(grad, "fsdp", scatter_dimension=1, tiled=True)
        return lax.all_to_all(
            grad.reshape(dp * shard, grad.shape[2]), "dp", 0, 1, tiled=True
        ).astype(F32)

    local_down = dot_tn(active, grad_y).astype(BF16)
    late_y, slope, _ = lax.optimization_barrier((grad_y, slope, local_down))
    grad_upward = (dot_nt(late_y, down_w) * slope).astype(BF16)
    grad_w_down = reduce_rows(local_down)
    local_up = dot_tn(second_in, grad_upward).astype(BF16)
    late_upward, _ = lax.optimization_barrier((grad_upward, local_up))
    second_part = dot_nt(late_upward, up_w).astype(BF16)
    grad_w_up = reduce_columns(local_up)
    if kernels:
        branch_all, grad_hidden, branch_sums = call_exchange(
            branch_kernel, 3, 2, 1, [(wide, BF16), (narrow, F32), ((8, width), F32)],
            [second_part, hidden, cotangent, jnp.concatenate([out_b, gain2], 0)],
        )
    else:
        grad_second = scatter_dp(second_part, dp)
        grad_hidden = cotangent.astype(F32) + norm_back(grad_second, normed2, inverse2, gain2)
        grad_branch = grad_hidden.astype(BF16)
        branch_all = gather_dp(grad_branch, dp)
        branch_sums = jnp.stack([
            jnp.sum(piece, axis=0)
            for piece in (
                cotangent.astype(F32), grad_second * normed2, grad_second,
                grad_branch.astype(F32),
            )
        ])

    grad_mixed = dot_nt(branch_all, out_w).astype(BF16)
    grad_proj = attend_back(slopes, distance, qkv, grad_mixed, length)
    local_qkv = dot_tn(first_in, grad_proj).astype(BF16)
    late_branch, late_active, late_proj, _ = lax.optimization_barrier(
        (branch_all, active, grad_proj, local_qkv)
    )
    grad_w_qkv = reduce_columns(local_qkv)
    grad_w_qkv = (
        grad_w_qkv.reshape(shard, dp, 3, part).transpose(0, 2, 1, 3).reshape(shard, 3 * width)
    )
    local_out = dot_tn(mixed, late_branch).astype(BF16)
    grad_w_out = reduce_rows(local_out)
    first_part = dot_nt(late_proj, qkv_w).astype(BF16)
    output_part = dot(late_active, down_w).astype(BF16)
    if kernels:
        grad_tokens, output, last_sums = call_exchange(
            last_kernel, 4, 2, 2, [(narrow, BF16), (narrow, BF16), ((8, width), F32)],
            [first_part, output_part, tokens, hidden, grad_hidden,
             jnp.concatenate([gain1, down_b], 0)],
        )
    else:
        grad_first = scatter_dp(first_part, dp)
        normed1, inverse1 = norm_stats(inputs)
        grad_tokens = grad_hidden + norm_back(grad_first, normed1, inverse1, gain1)
        output = hidden + scatter_dp(output_part, dp) + down_b
        last_sums = jnp.stack([jnp.sum(grad_first * normed1, axis=0), jnp.sum(grad_first, axis=0)])

    def spread(piece):
        wide = jnp.zeros((piece.shape[0] * dp,), F32)
        return lax.dynamic_update_slice(wide, piece, (spot * piece.shape[0],))

    def owned(total, start, size):
        step = size // (dp * fsdp)
        return lax.dynamic_slice(total, (start + rank * step,), (step,))

    early = jnp.concatenate([
        branch_sums[:4].reshape(4 * width),
        spread(jnp.sum(grad_upward.astype(F32), axis=0)),
        spread(jnp.sum(grad_proj[:, :part].astype(F32), axis=0)),
        spread(jnp.sum(grad_proj[:, 2 * part :].astype(F32), axis=0)),
    ])
    early = combine_all(early, both, jnp.add)
    late = combine_all(last_sums[:2].reshape(2 * width), both, jnp.add)

    head_top = jnp.full((heads,), -1e30, F32)
    head_top = lax.dynamic_update_slice(head_top, tops, (spot * local_heads,))
    head_top = combine_all(head_top, both, jnp.maximum)
    factor = jnp.sqrt(CLIP_TAU / jnp.maximum(head_top, CLIP_TAU))
    column = jnp.repeat(factor, HEAD_DIM)
    columns = jnp.concatenate([column, column, jnp.ones((width,), F32)])
    clipped = (w_qkv.astype(F32) * columns[None, :]).astype(BF16)
    return (
        output.astype(BF16),
        grad_tokens.astype(BF16),
        grad_w_qkv,
        owned(early, 4 * width + ff, width),
        owned(early, 5 * width + ff, width),
        grad_w_out,
        owned(early, 3 * width, width),
        owned(late, 0, width),
        owned(late, width, width),
        grad_w_up,
        owned(early, 4 * width, ff),
        grad_w_down,
        owned(early, 0, width),
        owned(early, width, width),
        owned(early, 2 * width, width),
        clipped,
    )


def solution(mesh):
    rows, flat = P(("dp", "fsdp"), None), P(("dp", "fsdp"))
    return jax.shard_map(
        functools.partial(layer, mesh.shape["dp"], mesh.shape["fsdp"]),
        mesh=mesh,
        in_specs=(
            rows, flat, rows, flat, flat, rows, flat, flat, flat, rows, flat, rows, flat, flat,
            flat, rows,
        ),
        out_specs=(
            rows, rows, rows, flat, flat, rows, flat, flat, flat, rows, flat, rows, flat, flat,
            flat, rows,
        ),
        check_vma=False,
    )
```

profile of v0, /device:TPU:0, one launch (start us, length us, event | category | flops | bytes accessed | tf_op | source)
XLA Modules:
  0.0 769.0 jit_solution(5850968501604893500)
XLA Ops:
  11.2 16.4 %all_to_all.52 = bf16[64,4,1536]{2,0,1:T(8,128)(2,1)} all-to-all(bf16[64,4,1536]{2,0,1:T(8,128)(2,1)S(1)} %all_to_all.40), channel_id=1, replica_groups=mesh['dp'=4,'fsdp'=8] {'dp'}, dimensions={1} | all-to-all | bytes 1572864 | tf_op jit(solution)/shard_map/all_to_all | solution.py:522
  28.7 15.5 %all_to_all.53 = bf16[64,4,2048]{2,0,1:T(8,128)(2,1)S(1)} all-to-all(bf16[64,4,2048]{2,0,1:T(8,128)(2,1)S(1)} %bitcast.64), channel_id=1, replica_groups=mesh['dp'=4,'fsdp'=8] {'dp'}, dimensions={1} | all-to-all | bytes 2097152 | tf_op jit(solution)/shard_map/all_to_all | solution.py:525
  50.1 8.0 %collective-permute-done.1 = bf16[32,768]{1,0:T(8,128)(2,1)S(1)} collective-permute-done((bf16[32,768]{1,0:T(8,128)(2,1)S(1)}, bf16[32,768]{1,0:T(8,128)(2,1)S(1)}, u32[]{:S(2)}, u32[]{:S(2)}) %collective-permute-start.1) | collective-permute-done | bytes 49184 | tf_op jit(solution)/shard_map/ppermute | solution.py:21
  58.6 8.8 %collective-permute-done.2 = bf16[32,768]{1,0:T(8,128)(2,1)S(1)} collective-permute-done((bf16[32,768]{1,0:T(8,128)(2,1)S(1)}, bf16[32,768]{1,0:T(8,128)(2,1)S(1)}, u32[]{:S(2)}, u32[]{:S(2)}) %collective-permute-start.2) | collective-permute-done | bytes 49184 | tf_op jit(solution)/shard_map/ppermute | solution.py:21
  77.2 73.0 %shard_map.270 = (bf16[1024,2048]{1,0:T(8,128)(2,1)}, bf16[1024,2048]{1,0:T(8,128)(2,1)}) custom-call(bf16[256,2048]{1,0:T(8,128)(2,1)S(1)} %copy-done, bf16[256,2048]{1,0:T(8,128)(2,1)S(1)} %copy-done.1), custom_call_target="tpu_custom_call" | custom-call | flops 2097152 | bytes 209715200 | tf_op jit(solution)/shard_map/pallas_call | solution.py:341
  155.0 11.9 %add_convert_fusion.qkv_ref = bf16[1024,1536]{1,0:T(8,128)(2,1)} fusion(bf16[2048,1536]{1,0:T(8,128)(2,1)} %bitcast.73, f32[1536]{0:T(1024)S(1)} %fusion.13, bf16[1024,2048]{1,0:T(8,128)(2,1)} %get-tuple-element.41, f32[2048]{0:T(1024)S(1)} %add.189, f32[2048]{0:T(1024)S(1)} %mul.100, f32[1024]{0:T(1024)S(1)} %add_rsqrt_fusion, ...), kind=kOutput, calls=%fused_computation.21 | convolution fusion | flops 6458179584 | bytes 13662208 | tf_op jit(solution)/shard_map/dot_general | solution.py:492
  167.0 17.8 %attend.1 = (bf16[1024,512]{1,0:T(8,128)(2,1)}, f32[32,128]{1,0:T(8,128)}) custom-call(f32[8]{0:T(128)} %exponential_multiply_fusion.slope_ref, f32[256,256]{1,0:T(8,128)} %convert_select_fusion.distance_ref, bf16[1024,1536]{1,0:T(8,128)(2,1)} %add_convert_fusion.qkv_ref), custom_call_target="tpu_custom_call" | custom-call | flops 536870912 | bytes 4194304 | tf_op jit(solution)/shard_map/attend/pallas_call | solution.py:429
  191.1 73.1 %shard_map.271 = (bf16[1024,2048]{1,0:T(8,128)(2,1)}, f32[256,2048]{1,0:T(8,128)S(1)}) custom-call(bf16[1024,2048]{1,0:T(8,128)(2,1)} %convolution_convert_fusion.6.partial_ref, bf16[256,2048]{1,0:T(8,128)(2,1)S(1)} %copy-done, f32[3,2048]{1,0:T(4,128)S(1)} %pad_maximum_fusion.1.params_ref), custom_call_target="tpu_custom_call" | custom-call | flops 2097152 | bytes 209715200 | tf_op jit(solution)/shard_map/pallas_call | solution.py:341
  264.2 11.4 %copy.42 = bf16[4,512,2048]{2,1,0:T(8,128)(2,1)} copy(bf16[4,512,2048]{2,0,1:T(4,128)(2,1)} %all-gather.9.cloned.1.call-done) | data formatting | bytes 16777216 | tf_op jit(solution)/shard_map/all_gather | solution.py:526
  275.5 16.6 %fusion.10 = (bf16[1024,2048]{1,0:T(8,128)(2,1)}, bf16[1024,2048]{1,0:T(8,128)(2,1)S(1)}) fusion(f32[2048]{0:T(1024)S(1)} %bitcast.72, bf16[1024,2048]{1,0:T(8,128)(2,1)} %get-tuple-element.43, bf16[2048,2048]{1,0:T(8,128)(2,1)} %bitcast.57), kind=kOutput, calls=%fused_computation.13 | convolution fusion | flops 8615100416 | bytes 20979712 | tf_op jit(solution)/shard_map/dot_general | solution.py:492
  294.1 11.9 %convolution_convert_fusion.2 = bf16[2048,2048]{1,0:T(8,128)(2,1)} fusion(bf16[1024,2048]{1,0:T(8,128)(2,1)S(1)} %get-tuple-element.52, bf16[1024,2048]{1,0:T(8,128)(2,1)S(1)} %copy-done.25), kind=kOutput, calls=%fused_computation.20 | convolution fusion | flops 8594128896 | bytes 16777216 | tf_op jit(solution)/shard_map/dot_general | solution.py:373
  306.0 13.3 %convert_reduce_fusion.1 = (f32[2048]{0:T(1024)S(1)}, bf16[1024,2048]{1,0:T(8,128)(2,1)S(1)}) fusion(bf16[1024,2048]{1,0:T(8,128)(2,1)} %get-tuple-element.47, bf16[1024,2048]{1,0:T(8,128)(2,1)} %get-tuple-element.46, bf16[2048,2048]{1,0:T(8,128)(2,1)} %all-gather.11.cloned.1.call-done), kind=kOutput, calls=%fused_computation.14 | convolution fusion | flops 8600418304 | bytes 20979712 | tf_op jit(solution)/shard_map/dot_general | solution.py:369
  319.4 11.3 %convolution_convert_fusion.1 = bf16[2048,2048]{1,0:T(8,128)(2,1)} fusion(bf16[1024,2048]{1,0:T(8,128)(2,1)S(1)} %copy-done.26, bf16[1024,2048]{1,0:T(8,128)(2,1)S(1)} %get-tuple-element.48), kind=kOutput, calls=%fused_computation.19 | convolution fusion | flops 8594128896 | bytes 16777216 | tf_op jit(solution)/shard_map/dot_general | solution.py:373
  330.7 10.4 %convolution_convert_fusion.5.partial_ref = bf16[1024,2048]{1,0:T(8,128)(2,1)} fusion(bf16[1024,2048]{1,0:T(8,128)(2,1)S(1)} %get-tuple-element.48, bf16[2048,2048]{1,0:T(8,128)(2,1)S(1)} %bitcast.60), kind=kOutput, calls=%fused_computation.24 | convolution fusion | flops 8592031744 | bytes 16777216 | tf_op jit(solution)/shard_map/dot_general | solution.py:369
  341.2 72.2 %shard_map.272 = (bf16[1024,2048]{1,0:T(8,128)(2,1)}, f32[256,2048]{1,0:T(8,128)S(1)}, f32[8,2048]{1,0:T(8,128)S(1)}) custom-call(bf16[1024,2048]{1,0:T(8,128)(2,1)} %convolution_convert_fusion.5.partial_ref, f32[256,2048]{1,0:T(8,128)S(1)} %get-tuple-element.49.hidden_ref, bf16[256,2048]{1,0:T(8,128)(2,1)S(1)} %copy-done.2, ...), custom_call_target="tpu_custom_call" | custom-call | flops 2097152 | bytes 209715200 | tf_op jit(solution)/shard_map/pallas_call | solution.py:341
  420.2 28.7 %attend_back.1 = bf16[1024,1536]{1,0:T(8,128)(2,1)} custom-call(f32[8]{0:T(128)} %exponential_multiply_fusion.slope_ref, f32[256,256]{1,0:T(8,128)} %convert_select_fusion.distance_ref, bf16[1024,1536]{1,0:T(8,128)(2,1)} %add_convert_fusion.qkv_ref, bf16[1024,512]{1,0:T(8,128)(2,1)} %convolution_convert_fusion.8.grad_ref), custom_call_target="tpu_custom_call" | custom-call | flops 1342177280 | bytes 7340032 | tf_op jit(solution)/shard_map/attend_back/pallas_call | solution.py:456
  448.9 11.8 %convolution_convert_fusion = bf16[2048,1536]{1,0:T(8,128)(2,1)} fusion(bf16[1024,1536]{1,0:T(8,128)(2,1)} %attend_back.1, bf16[1024,2048]{1,0:T(8,128)(2,1)} %get-tuple-element.41, f32[2048]{0:T(1024)S(1)} %add.189, f32[2048]{0:T(1024)S(1)} %mul.100, f32[1024]{0:T(1024)S(1)} %add_rsqrt_fusion, f32[1024]{0:T(1024)S(1)} %broadcast_multiply_fusion), kind=kOutput, calls=%fused_computation.18 | convolution fusion | flops 6458179584 | bytes 13656064 | tf_op jit(solution)/shard_map/dot_general | solution.py:373
  468.6 14.3 %convolution_convert_fusion.4.output_ref = bf16[1024,2048]{1,0:T(8,128)(2,1)} fusion(bf16[1024,2048]{1,0:T(8,128)(2,1)} %copy-done.28, bf16[2048,2048]{1,0:T(8,128)(2,1)} %all-gather.11.cloned.1.call-done), kind=kOutput, calls=%fused_computation.23 | convolution fusion | flops 8592031744 | bytes 16777216 | tf_op jit(solution)/shard_map/dot_general | solution.py:492
  482.9 11.0 %convolution_convert_fusion.3.first_ref = bf16[1024,2048]{1,0:T(8,128)(2,1)} fusion(bf16[1024,1536]{1,0:T(8,128)(2,1)S(1)} %copy-done.9, bf16[2048,1536]{1,0:T(8,128)(2,1)} %bitcast.74), kind=kOutput, calls=%fused_computation.22 | convolution fusion | flops 6444548096 | bytes 13631488 | tf_op jit(solution)/shard_map/dot_general | solution.py:369
  493.9 70.4 %shard_map.273 = (bf16[256,2048]{1,0:T(8,128)(2,1)S(1)}, bf16[256,2048]{1,0:T(8,128)(2,1)S(1)}, f32[8,2048]{1,0:T(8,128)S(1)}) custom-call(bf16[1024,2048]{1,0:T(8,128)(2,1)} %convolution_convert_fusion.3.first_ref, bf16[1024,2048]{1,0:T(8,128)(2,1)} %convolution_convert_fusion.4.output_ref, bf16[256,2048]{1,0:T(8,128)(2,1)S(1)} %copy-done, ...), custom_call_target="tpu_custom_call" | custom-call | flops 2097152 | bytes 209715200 | tf_op jit(solution)/shard_map/pallas_call | solution.py:341
  607.3 18.6 %reduce-scatter.9.cloned.1.call-done = bf16[4,64,2048]{2,1,0:T(8,128)(2,1)} async-done(((bf16[4,512,2048]{2,1,0:T(8,128)(2,1)}), bf16[4,64,2048]{2,1,0:T(8,128)(2,1)}) %reduce-scatter.9.cloned.1.call-update) | async-done | bytes 1048592 | tf_op jit(solution)/shard_map/reduce_scatter | solution.py:574
  634.2 10.0 %collective-permute-done.9 = f32[20480]{0:T(1024)S(1)} collective-permute-done((f32[20480]{0:T(1024)S(1)}, f32[20480]{0:T(1024)S(1)}, u32[]{:S(2)}, u32[]{:S(2)}) %collective-permute-start.9) | collective-permute-done | bytes 81952 | tf_op jit(solution)/shard_map/ppermute | solution.py:21
  645.5 18.1 %reduce-scatter.7.cloned.1.call-done = bf16[64,2048]{1,0:T(8,128)(2,1)} async-done(((bf16[512,2048]{1,0:T(8,128)(2,1)}), bf16[64,2048]{1,0:T(8,128)(2,1)}) %reduce-scatter.7.cloned.1.call-update) | async-done | bytes 262160 | tf_op jit(solution)/shard_map/reduce_scatter | solution.py:570
  674.9 79.0 %reduce-scatter.11.cloned.1.call-done = bf16[256,2048]{1,0:T(8,128)(2,1)} async-done(((bf16[2048,2048]{1,0:T(8,128)(2,1)}), bf16[256,2048]{1,0:T(8,128)(2,1)}) %reduce-scatter.11.cloned.1.call-update) | async-done | bytes 1048592 | tf_op jit(solution)/shard_map/reduce_scatter | solution.py:570
  (216 shorter events, 120.2 us)
Async XLA Ops:
  7.2 147.9 %all-gather.5.cloned.1.call-start = ((), (), s32[]{:S(2)}) async-start(), calls=%async_computation.8 | async-start | bytes 7077888 | tf_op jit(solution)/shard_map/all_gather | solution.py:523
  27.6 157.2 %all-gather.7.cloned.1.call-start = ((), (), s32[]{:S(2)}) async-start(), calls=%async_computation.9 | async-start | bytes 2359296 | tf_op jit(solution)/shard_map/all_gather | solution.py:520
  28.4 235.8 %all-gather.9.cloned.1.call-start = ((), (), s32[]{:S(2)}) async-start(), calls=%async_computation.10 | async-start | bytes 9437184 | tf_op jit(solution)/shard_map/all_gather | solution.py:526
  46.0 260.0 %all-gather.11.cloned.1.call-start = ((), (), s32[]{:S(2)}) async-start(), calls=%async_computation.11 | async-start | bytes 9437184 | tf_op jit(solution)/shard_map/all_gather | solution.py:527
  46.5 539.8 %reduce-scatter.5.cloned.1.call-start = ((), (), s32[]{:S(2)}) async-start(), calls=%async_computation.12 | async-start | bytes 7077888 | tf_op jit(solution)/shard_map/reduce_scatter | solution.py:574
  48.4 9.6 %collective-permute-start.1 = (bf16[32,768]{1,0:T(8,128)(2,1)S(1)}, bf16[32,768]{1,0:T(8,128)(2,1)S(1)}, u32[]{:S(2)}, u32[]{:S(2)}) collective-permute-start(bf16[32,768]{1,0:T(8,128)(2,1)S(1)} %add.184), channel_id=1, source_target_pairs={{0,2},{1,3},{2,0},{3,1},{4,6},{5,7},{6,4},{7,5},{8,10},{9,11},{10,... | collective-permute-start | bytes 147464 | tf_op jit(solution)/shard_map/ppermute | solution.py:21
  58.1 9.3 %collective-permute-start.2 = (bf16[32,768]{1,0:T(8,128)(2,1)S(1)}, bf16[32,768]{1,0:T(8,128)(2,1)S(1)}, u32[]{:S(2)}, u32[]{:S(2)}) collective-permute-start(bf16[32,768]{1,0:T(8,128)(2,1)S(1)} %add.185), channel_id=1, source_target_pairs={{0,4},{1,5},{2,6},{3,7},{4,0},{5,1},{6,2},{7,3},{8,12},{9,13},{10,... | collective-permute-start | bytes 147464 | tf_op jit(solution)/shard_map/ppermute | solution.py:21
  67.4 4.2 collective-permute-start.3
  460.7 165.2 %reduce-scatter.9.cloned.1.call-start = ((), (), s32[]{:S(2)}) async-start(), calls=%async_computation.14 | async-start | bytes 9437184 | tf_op jit(solution)/shard_map/reduce_scatter | solution.py:574
  461.3 202.3 %reduce-scatter.7.cloned.1.call-start = ((), (), s32[]{:S(2)}) async-start(), calls=%async_computation.13 | async-start | bytes 2359296 | tf_op jit(solution)/shard_map/reduce_scatter | solution.py:570
  467.6 286.3 %reduce-scatter.11.cloned.1.call-start = ((), (), s32[]{:S(2)}) async-start(), calls=%async_computation.15 | async-start | bytes 9437184 | tf_op jit(solution)/shard_map/reduce_scatter | solution.py:570
  567.6 22.2 %collective-permute-start.5 = (f32[20480]{0:T(1024)S(1)}, f32[20480]{0:T(1024)S(1)}, u32[]{:S(2)}, u32[]{:S(2)}) collective-permute-start(f32[20480]{0:T(1024)S(1)} %pad_maximum_fusion), channel_id=1, source_target_pairs={{0,1},{1,0},{2,3},{3,2},{4,5},{5,4},{6,7},{7,6},{8,9},{9,8},{10,11... | collective-permute-start | bytes 245768 | tf_op jit(solution)/shard_map/ppermute | solution.py:21
  568.2 15.2 %collective-permute-start.11 = (f32[4096]{0:T(1024)S(1)}, f32[4096]{0:T(1024)S(1)}, u32[]{:S(2)}, u32[]{:S(2)}) collective-permute-start(f32[4096]{0:T(1024)S(1)} %add.212), channel_id=1, source_target_pairs={{0,2},{1,3},{2,0},{3,1},{4,6},{5,7},{6,4},{7,5},{8,10},{9,11},{10,... | collective-permute-start | bytes 49160 | tf_op jit(solution)/shard_map/ppermute | solution.py:21
  573.2 6.3 collective-permute-start.17
  583.1 6.8 collective-permute-start.19
  583.3 6.8 collective-permute-start.12
  586.3 21.0 %all-to-all-start.2 = ((bf16[4,64,1536]{2,1,0:T(8,128)(2,1)}), bf16[4,64,1536]{2,1,0:T(8,128)(2,1)S(1)}, u32[]{:S(2)}, u32[]{:S(2)}) async-start(bf16[4,64,1536]{2,1,0:T(8,128)(2,1)} %reduce-scatter.5.cloned.1.call-done), calls=%async_computation.3 | async-start | bytes 1572864 | tf_op jit(solution)/shard_map/all_to_all | solution.py:575
  589.9 6.5 collective-permute-start.6
  590.2 8.4 %collective-permute-start.13 = (f32[4096]{0:T(1024)S(1)}, f32[4096]{0:T(1024)S(1)}, u32[]{:S(2)}, u32[]{:S(2)}) collective-permute-start(f32[4096]{0:T(1024)S(1)} %add.214), channel_id=1, source_target_pairs={{0,8},{8,0},{16,24},{24,16},{1,9},{9,1},{17,25},{25,17},{2,10},{10... | collective-permute-start | bytes 49160 | tf_op jit(solution)/shard_map/ppermute | solution.py:21
  596.3 8.9 %collective-permute-start.7 = (f32[20480]{0:T(1024)S(1)}, f32[20480]{0:T(1024)S(1)}, u32[]{:S(2)}, u32[]{:S(2)}) collective-permute-start(f32[20480]{0:T(1024)S(1)} %add.205), channel_id=1, source_target_pairs={{0,4},{1,5},{2,6},{3,7},{4,0},{5,1},{6,2},{7,3},{8,12},{9,13},{10,... | collective-permute-start | bytes 245768 | tf_op jit(solution)/shard_map/ppermute | solution.py:21
  598.5 33.0 %collective-permute-start.14 = (f32[4096]{0:T(1024)S(1)}, f32[4096]{0:T(1024)S(1)}, u32[]{:S(2)}, u32[]{:S(2)}) collective-permute-start(f32[4096]{0:T(1024)S(1)} %add.215), channel_id=1, source_target_pairs={{0,16},{8,24},{16,0},{24,8},{1,17},{9,25},{17,1},{25,9},{2,18},{10... | collective-permute-start | bytes 49160 | tf_op jit(solution)/shard_map/ppermute | solution.py:21
  605.3 26.2 %collective-permute-start.8 = (f32[20480]{0:T(1024)S(1)}, f32[20480]{0:T(1024)S(1)}, u32[]{:S(2)}, u32[]{:S(2)}) collective-permute-start(f32[20480]{0:T(1024)S(1)} %add.206), channel_id=1, source_target_pairs={{0,8},{8,0},{16,24},{24,16},{1,9},{9,1},{17,25},{25,17},{2,10},{10... | collective-permute-start | bytes 245768 | tf_op jit(solution)/shard_map/ppermute | solution.py:21
  625.9 130.7 %all-to-all-start.3 = ((bf16[4,64,2048]{2,1,0:T(8,128)(2,1)}), bf16[4,64,2048]{2,1,0:T(8,128)(2,1)}, u32[]{:S(2)}, u32[]{:S(2)}) async-start(bf16[4,64,2048]{2,1,0:T(8,128)(2,1)} %reduce-scatter.9.cloned.1.call-done), calls=%async_computation.6 | async-start | bytes 2097152 | tf_op jit(solution)/shard_map/all_to_all | solution.py:575
  631.5 12.7 %collective-permute-start.9 = (f32[20480]{0:T(1024)S(1)}, f32[20480]{0:T(1024)S(1)}, u32[]{:S(2)}, u32[]{:S(2)}) collective-permute-start(f32[20480]{0:T(1024)S(1)} %add.207), channel_id=1, source_target_pairs={{0,16},{8,24},{16,0},{24,8},{1,17},{9,25},{17,1},{25,9},{2,18},{10... | collective-permute-start | bytes 245768 | tf_op jit(solution)/shard_map/ppermute | solution.py:21
  (37 other events, 624.9 us)
Sparse Core Ops, SparseCore 0:
  27.7 66.4 all-gather.4
  95.8 27.7 all-gather.6
  125.8 81.4 all-gather.8
  208.7 80.5 all-gather.10
  460.8 70.6 reduce-scatter.4
  533.7 92.2 reduce-scatter.8
  628.8 34.7 reduce-scatter.6
  665.9 87.9 reduce-scatter.10
where the time goes:
time: 773 us; the launch traced here: 769 us
  Pallas kernels  335 us (43%)
  waiting for transfers between devices  171 us (22%)
  matrix products  131 us (17%)
  local copies, waits for them, and re-layouts  39.5 us (5%)
  blocking collectives  31.9 us (4%)
  starting transfers between devices  30.8 us (4%)
  between operations  15.3 us (2%)
  other arithmetic  14.7 us (2%)
    pallas_call x4, Pallas kernels, call_exchange(): pl.pallas_call(kernel, in_specs=[pl.BlockSpec(memory_space=pltpu.VMEM)] *...  289 us
    reduce_scatter x2, waiting for transfers between devices, reduce_rows(): lax.psum_scatter(grad, 'fsdp', scatter_dimension=0, tiled=True).astype(F32)  97.1 us
    ppermute x20, waiting for transfers between devices, swap(): return lax.ppermute(value, axis, [(i, i ^ bit) for i in range(size)])  52.8 us
    dot_general x4, matrix products, dot(): return jnp.dot(a, b, preferred_element_type=F32)  49.1 us
    dot_general x4, matrix products, dot_tn(): lax.dot_general(a, b, (((0,), (0,)), ((), ())), preferred_element_type=F32)  41.2 us
    dot_general x4, matrix products, dot_nt(): lax.dot_general(a, b, (((1,), (1,)), ((), ())), preferred_element_type=F32)  40.4 us
    pallas_call x1, Pallas kernels, attend_back(): pl.pallas_call(attend_back_kernel, grid=(rows // length,), in_specs=[pl.B...  28.7 us
    ppermute x20, starting transfers between devices, swap(): return lax.ppermute(value, axis, [(i, i ^ bit) for i in range(size)])  22.4 us
  transfers between devices with their start and end apart: 30, of which 16 were waited for; matrix products, arithmetic and copies ran while one was open for 15% of the time, Pallas kernels for 30%

commit v1 on v0

--- a/solution.py
+++ b/solution.py
@@ -83,14 +83,20 @@
 PATHS = ((1, 2), (2, 1))
 
 
-def neighbours():
-    me = lax.axis_index("dp")
-    near = {1: {"dp": me + 1 - 2 * (me % 2)}, 2: {"dp": (me + 2) % 4}}
+def flipped(axis, bit):
+    me = lax.axis_index(axis)
+    return {axis: me + bit - 2 * bit * ((me // bit) % 2)}
+
+
+def neighbours(fsdp=1):
+    near = {bit: flipped("dp", bit) for bit in (1, 2)}
+    partners = [near[1], near[2]] + [flipped("fsdp", bit) for bit in bits_of(fsdp)]
+    greeted = partners if fsdp > 1 else [near[1], near[2]]
     barrier = pltpu.get_barrier_semaphore()
-    for bit in (1, 2):
-        pl.semaphore_signal(barrier, inc=1, device_id=near[bit], device_id_type=MESH_IDS)
-    pl.semaphore_wait(barrier, 2)
-    return near
+    for where in greeted:
+        pl.semaphore_signal(barrier, inc=1, device_id=where, device_id_type=MESH_IDS)
+    pl.semaphore_wait(barrier, len(greeted))
+    return near, partners
 
 
 def remote(source, target, sems, index, where):
@@ -216,22 +222,39 @@
     )
 
 
-def gather_two_kernel(one_ref, two_ref, out_one, out_two, sems):
-    near = neighbours()
+def double_all(held, landing, sems, partners, join, stages=None):
+    for stage in stages or range(len(partners)):
+        where = partners[stage]
+        copy = remote(held.at[stage], landing.at[stage], sems, stage, where)
+        copy.start()
+        copy.wait()
+        held[stage + 1] = join(held[stage], landing[stage])
+
+
+def gather_two_kernel(
+    fsdp, one_ref, two_ref, table_ref, out_one, out_two, table_out, held, landing, sems, small_sems
+):
+    near, partners = neighbours(fsdp)
     jobs = []
     for k, (source, out) in enumerate(((one_ref, out_one), (two_ref, out_two))):
         out[: source.shape[0]] = source[...]
         jobs.append(Gather(out, sems.at[k], near))
+    held[0] = table_ref[...]
+    double_all(held, landing, small_sems, partners, jnp.add, range(2))
     for job in jobs:
         each_step(lambda step, job=job: [job.send(path, step) for path in range(2)])
+    double_all(held, landing, small_sems, partners, jnp.add, range(2, len(partners)))
+    table_out[...] = held[len(partners)]
     for job in jobs:
         each_step(lambda step, job=job: [job.forward(path, step) for path in range(2)])
     for job in jobs:
         each_step(lambda step, job=job: [job.finish(path, step) for path in range(2)])
 
 
-def exchange(scatter, gather, rows_of):
+def exchange(scatter, gather, rows_of, beside=None):
     each_step(lambda step: [scatter.begin(path, step) for path in range(2)])
+    if beside is not None:
+        beside()
     each_step(lambda step: [scatter.relay(path, step) for path in range(2)])
 
     def middle(step):
@@ -252,15 +275,16 @@
     each_step(lambda step: [gather.finish(path, step) for path in range(2)])
 
 
-def add_sums(sums_ref, values):
+def add_sums(sums_ref, values, start=0):
     for k, value in enumerate(values):
-        sums_ref[k : k + 1] += jnp.sum(value, axis=0, keepdims=True)
+        row = start + k
+        sums_ref[row : row + 1] += jnp.sum(value, axis=0, keepdims=True)
 
 
 def hidden_kernel(
     partial_ref, tokens_ref, params_ref, out_ref, hidden_ref, landing, passing, last, sems
 ):
-    near = neighbours()
+    near, _ = neighbours()
 
     def rows_of(rows, total):
         hidden = tokens_ref[rows].astype(F32) + total + params_ref[0:1]
@@ -275,10 +299,16 @@
 
 
 def branch_kernel(
-    partial_ref, hidden_ref, cotangent_ref, params_ref, out_ref, grad_ref, sums_ref, landing,
-    passing, last, sems,
+    partial_ref, hidden_ref, cotangent_ref, params_ref, active_ref, weight_ref, out_ref, grad_ref,
+    sums_ref, output_ref, landing, passing, last, active, weight, copy_sems, sems,
 ):
-    near = neighbours()
+    copies = [
+        pltpu.make_async_copy(active_ref, active, copy_sems.at[0]),
+        pltpu.make_async_copy(weight_ref, weight, copy_sems.at[1]),
+    ]
+    for copy in copies:
+        copy.start()
+    near, _ = neighbours()
     sums_ref[...] = jnp.zeros_like(sums_ref)
 
     def rows_of(rows, total):
@@ -290,18 +320,34 @@
         add_sums(sums_ref, (upper, total * normed, total, branch.astype(F32)))
         return branch
 
+    def output_tile(tile, carry):
+        columns = pl.ds(pl.multiple_of(tile * 256, 256), 256)
+        output_ref[:, columns] = dot(active[...], weight[:, columns]).astype(BF16)
+        return carry
+
+    def beside():
+        for copy in copies:
+            copy.wait()
+        lax.fori_loop(0, output_ref.shape[1] // 256, output_tile, 0)
+
     exchange(
         Scatter(partial_ref, landing, passing, last, sems.at[0], near),
-        Gather(out_ref, sems.at[1], near), rows_of,
-    )
+        Gather(out_ref, sems.at[1], near), rows_of, beside,
+    )
+
+
+def sum_or_top(a, b):
+    row = lax.broadcasted_iota(jnp.int32, a.shape, 0)
+    return jnp.where(row < a.shape[0] - 1, a + b, jnp.maximum(a, b))
 
 
 def last_kernel(
-    first_ref, output_ref, tokens_ref, hidden_ref, grad_ref, params_ref, tokens_out, output_out,
-    sums_ref, landing, passing, last, sems,
+    fsdp, first_ref, output_ref, tokens_ref, hidden_ref, grad_ref, params_ref, small_ref,
+    tokens_out, output_out, small_out, sums_out, landing, passing, last, held, small_landing,
+    sums, sums_landing, sems, small_sems,
 ):
-    near = neighbours()
-    sums_ref[...] = jnp.zeros_like(sums_ref)
+    near, partners = neighbours(fsdp)
+    sums[0] = jnp.zeros_like(sums_out)
     first, second = (
         Scatter(ref, landing.at[k], passing.at[k], last.at[k], sems.at[k], near)
         for k, ref in enumerate((first_ref, output_ref))
@@ -313,24 +359,29 @@
         normed, inverse_std = row_norm(tokens_ref[rows].astype(F32))
         grad = grad_ref[rows] + row_back(total, normed, inverse_std, params_ref[0:1])
         tokens_out[rows] = grad.astype(BF16)
-        add_sums(sums_ref, (total * normed, total))
+        add_sums(sums.at[0], (total * normed, total))
 
     def second_rows(path, step):
         rows = second.own(path, step)
         total = second.total(path, step)
         output_out[rows] = (hidden_ref[rows] + total + params_ref[1:2]).astype(BF16)
 
+    held[0] = small_ref[...]
     for job in (first, second):
         each_step(lambda step, job=job: [job.begin(path, step) for path in range(2)])
+    double_all(held, small_landing, small_sems.at[0], partners, sum_or_top)
+    small_out[...] = held[len(partners)]
     for job in (first, second):
         each_step(lambda step, job=job: [job.relay(path, step) for path in range(2)])
     each_step(lambda step: [first_rows(path, step) for path in range(2)])
+    double_all(sums, sums_landing, small_sems.at[1], partners, jnp.add)
+    sums_out[...] = sums[len(partners)]
     each_step(lambda step: [second_rows(path, step) for path in range(2)])
     for job in (first, second):
         each_step(lambda step, job=job: [job.finish(path, step) for path in range(2)])
 
 
-def call_exchange(kernel, number, jobs, scatters, outs, args):
+def call_exchange(kernel, number, jobs, scatters, outs, args, extra=(), stages=0, unplaced=0):
     rows, width = args[0].shape if scatters else (4 * args[0].shape[0], args[0].shape[1])
     own = rows // 4
     room = []
@@ -340,12 +391,15 @@
         room = [(2, 2, own, width), (2, own, width), (2, own, width)]
     return pl.pallas_call(
         kernel,
-        in_specs=[pl.BlockSpec(memory_space=pltpu.VMEM)] * len(args),
+        in_specs=[pl.BlockSpec(memory_space=pltpu.VMEM)] * (len(args) - unplaced)
+        + [pl.BlockSpec(memory_space=pl.ANY)] * unplaced,
         out_specs=[pl.BlockSpec(memory_space=pltpu.VMEM)] * len(outs),
         out_shape=[jax.ShapeDtypeStruct(shape, dtype) for shape, dtype in outs],
         scratch_shapes=[
             *(pltpu.VMEM(shape, BF16) for shape in room),
+            *extra,
             pltpu.SemaphoreType.DMA((jobs, 2, 6 * STEPS)),
+            *([pltpu.SemaphoreType.DMA(stages)] if stages else []),
         ],
         compiler_params=pltpu.CompilerParams(
             collective_id=number, has_side_effects=True, vmem_limit_bytes=48 << 20
@@ -357,7 +411,7 @@
 
 
 def pair_span(offset, pair):
-    return pl.ds(pl.multiple_of(offset + pair * 2 * HEAD_DIM, 2 * HEAD_DIM), 2 * HEAD_DIM)
+    return pl.ds(offset + pair * 2 * HEAD_DIM, 2 * HEAD_DIM)
 
 
 def head_parts(ref, offset, pair):
@@ -377,8 +431,9 @@
     width = mixed_ref.shape[1]
     lane = lax.broadcasted_iota(jnp.int32, (8, 128), 1)
 
-    def pair_step(pair, tops):
-        distance = distance_ref[...]
+    distance = distance_ref[...]
+    tops = jnp.zeros((8, 128), F32)
+    for pair in range(width // HEAD_DIM // 2):
         outs = []
         for t, (q, k, v) in enumerate(
             zip(*(head_parts(qkv_ref, part * width, pair) for part in range(3)))
@@ -391,17 +446,14 @@
             probs = expos * (1.0 / jnp.sum(expos, axis=-1, keepdims=True))
             outs.append(jnp.dot(probs.astype(BF16), v, preferred_element_type=F32))
         mixed_ref[:, pair_span(0, pair)] = jnp.concatenate(outs, 1).astype(BF16)
-        return tops
-
-    pairs = width // HEAD_DIM // 2
-    top_ref[...] = lax.fori_loop(0, pairs, pair_step, jnp.zeros((8, 128), F32))
+    top_ref[...] = tops
 
 
 def attend_back_kernel(slope_ref, distance_ref, qkv_ref, grad_ref, out_ref):
     width = grad_ref.shape[1]
 
-    def pair_step(pair, carry):
-        distance = distance_ref[...]
+    distance = distance_ref[...]
+    for pair in range(width // HEAD_DIM // 2):
         outs = ([], [], [])
         parts = [head_parts(qkv_ref, part * width, pair) for part in range(3)]
         parts.append(head_parts(grad_ref, 0, pair))
@@ -418,9 +470,6 @@
             outs[1].append(dot_tn(grad_scores, low_q))
         for part in range(3):
             out_ref[:, pair_span(part * width, pair)] = jnp.concatenate(outs[part], 1).astype(BF16)
-        return carry
-
-    lax.fori_loop(0, width // HEAD_DIM // 2, pair_step, 0)
 
 
 def attend(slopes, distance, qkv, length):
@@ -506,17 +555,6 @@
     rank = spot * fsdp + place
     both = (("fsdp", fsdp), ("dp", dp))
 
-    full_small = (bias_out, ln1_gain, ln1_bias, bias_down, ln2_gain, ln2_bias)
-    row = jnp.concatenate(full_small + (bias_q, bias_v, bias_up))[None]
-    table = jnp.zeros((dp * fsdp, row.shape[1]), BF16)
-    table = lax.dynamic_update_slice(table, row, (rank, 0))
-    table = combine_all(table, both, jnp.add).astype(F32)
-    small = [table[:, k * shard : (k + 1) * shard].reshape(1, width) for k in range(6)]
-    out_b, gain1, shift1, down_b, gain2, shift2 = small
-    mine = lax.dynamic_slice(table, (spot * fsdp, 0), (fsdp, row.shape[1]))[:, 6 * shard :]
-    q_b, v_b = mine[:, :shard].reshape(1, part), mine[:, shard : 2 * shard].reshape(1, part)
-    up_b = mine[:, 2 * shard :].reshape(1, ff_part)
-
     out_w = lax.all_gather(w_out, "fsdp", axis=0, tiled=True)
     cols = w_qkv.reshape(shard, 3, dp, part).transpose(0, 2, 1, 3).reshape(shard, 3 * width)
     cols = lax.all_to_all(cols, "dp", 1, 0, tiled=True).reshape(dp, shard, 3 * part)
@@ -525,6 +563,32 @@
     ups = lax.all_to_all(w_up, "dp", 1, 0, tiled=True).reshape(dp, shard, ff_part)
     up_w = lax.all_gather(ups, "fsdp", axis=1, tiled=True).reshape(width, ff_part)
     down_w = lax.all_gather(w_down, "fsdp", axis=0, tiled=True)
+    late_tokens, _ = lax.optimization_barrier((tokens, ups))
+
+    full_small = (bias_out, ln1_gain, ln1_bias, bias_down, ln2_gain, ln2_bias)
+    row = jnp.concatenate(full_small + (bias_q, bias_v, bias_up))[None]
+    table = jnp.zeros((dp * fsdp, row.shape[1]), BF16)
+    table = lax.dynamic_update_slice(table, row, (rank, 0))
+    wide = (4 * length, width)
+    narrow = (length, width)
+    kernels = dp == 4 and length % (32 * STEPS) == 0 and ff == dp * width
+    stages = len(bits_of(fsdp)) + 2
+    if kernels:
+        all_tokens, grad_y, table = call_exchange(
+            functools.partial(gather_two_kernel, fsdp), 1, 2, 0,
+            [(wide, BF16), (wide, BF16), (table.shape, BF16)], [late_tokens, cotangent, table],
+            (pltpu.VMEM((stages + 1,) + table.shape, BF16), pltpu.VMEM((stages,) + table.shape, BF16)),
+            (2, stages),
+        )
+    else:
+        all_tokens, grad_y = gather_dp(late_tokens, dp), gather_dp(cotangent, dp)
+        table = combine_all(table, both, jnp.add)
+    table = table.astype(F32)
+    small = [table[:, k * shard : (k + 1) * shard].reshape(1, width) for k in range(6)]
+    out_b, gain1, shift1, down_b, gain2, shift2 = small
+    mine = lax.dynamic_slice(table, (spot * fsdp, 0), (fsdp, row.shape[1]))[:, 6 * shard :]
+    q_b, v_b = mine[:, :shard].reshape(1, part), mine[:, shard : 2 * shard].reshape(1, part)
+    up_b = mine[:, 2 * shard :].reshape(1, ff_part)
 
     ranks = (spot * local_heads + 1 + jnp.arange(local_heads)).astype(F32)
     slopes = jnp.exp2(-8.0 * ranks / heads) * SCALE
@@ -533,17 +597,6 @@
     distance = jnp.where(gap >= 0, gap.astype(F32), MASKED)
 
     inputs = tokens.astype(F32)
-    wide = (4 * length, width)
-    narrow = (length, width)
-    kernels = dp == 4 and length % (32 * STEPS) == 0
-    ordered_tokens, ups, cols = lax.optimization_barrier((tokens, ups, cols))
-    if kernels:
-        all_tokens, grad_y = call_exchange(
-            gather_two_kernel, 1, 2, 0, [(wide, BF16)] * 2,
-            [ordered_tokens, cotangent],
-        )
-    else:
-        all_tokens, grad_y = gather_dp(ordered_tokens, dp), gather_dp(cotangent, dp)
     normed_all, _ = norm_stats(all_tokens.astype(F32))
     first_in = (normed_all * gain1 + shift1).astype(BF16)
     biases = jnp.concatenate([q_b, jnp.zeros_like(q_b), v_b], 1)
@@ -571,7 +624,9 @@
 
     def reduce_columns(grad):
         grad = grad.reshape(dp, fsdp * shard, grad.shape[1])
-        grad = lax.psum_scatter(grad, "fsdp", scatter_dimension=1, tiled=True)
+        return lax.psum_scatter(grad, "fsdp", scatter_dimension=1, tiled=True)
+
+    def exchange_columns(grad):
         return lax.all_to_all(
             grad.reshape(dp * shard, grad.shape[2]), "dp", 0, 1, tiled=True
         ).astype(F32)
@@ -583,11 +638,15 @@
     local_up = dot_tn(second_in, grad_upward).astype(BF16)
     late_upward, _ = lax.optimization_barrier((grad_upward, local_up))
     second_part = dot_nt(late_upward, up_w).astype(BF16)
-    grad_w_up = reduce_columns(local_up)
+    scattered_up = reduce_columns(local_up)
     if kernels:
-        branch_all, grad_hidden, branch_sums = call_exchange(
-            branch_kernel, 3, 2, 1, [(wide, BF16), (narrow, F32), ((8, width), F32)],
-            [second_part, hidden, cotangent, jnp.concatenate([out_b, gain2], 0)],
+        branch_all, grad_hidden, branch_sums, output_part = call_exchange(
+            branch_kernel, 3, 2, 1,
+            [(wide, BF16), (narrow, F32), ((8, width), F32), (wide, BF16)],
+            [second_part, hidden, cotangent, jnp.concatenate([out_b, gain2], 0), active, down_w],
+            (pltpu.VMEM(active.shape, BF16), pltpu.VMEM(down_w.shape, BF16),
+             pltpu.SemaphoreType.DMA((2,))),
+            unplaced=2,
         )
     else:
         grad_second = scatter_dp(second_part, dp)
@@ -605,50 +664,61 @@
     grad_mixed = dot_nt(branch_all, out_w).astype(BF16)
     grad_proj = attend_back(slopes, distance, qkv, grad_mixed, length)
     local_qkv = dot_tn(first_in, grad_proj).astype(BF16)
-    late_branch, late_active, late_proj, _ = lax.optimization_barrier(
-        (branch_all, active, grad_proj, local_qkv)
-    )
-    grad_w_qkv = reduce_columns(local_qkv)
+    late_branch, late_proj, _ = lax.optimization_barrier((branch_all, grad_proj, local_qkv))
+    grad_w_qkv = exchange_columns(reduce_columns(local_qkv))
     grad_w_qkv = (
         grad_w_qkv.reshape(shard, dp, 3, part).transpose(0, 2, 1, 3).reshape(shard, 3 * width)
     )
     local_out = dot_tn(mixed, late_branch).astype(BF16)
     grad_w_out = reduce_rows(local_out)
     first_part = dot_nt(late_proj, qkv_w).astype(BF16)
-    output_part = dot(late_active, down_w).astype(BF16)
+    if not kernels:
+        output_part = dot(active, down_w).astype(BF16)
+
+    def spread(piece, size, fill=0.0):
+        return lax.dynamic_update_slice(
+            jnp.full((size,), fill, F32), piece, (spot * piece.shape[0],)
+        )
+
+    up_sum = jnp.sum(grad_upward.astype(F32), axis=0)
+    q_sum = jnp.sum(grad_proj[:, :part].astype(F32), axis=0)
+    v_sum = jnp.sum(grad_proj[:, 2 * part :].astype(F32), axis=0)
+    small = jnp.concatenate([
+        branch_sums[:4].reshape(4 * width), spread(up_sum, ff), spread(q_sum, width),
+        spread(v_sum, width), jnp.zeros((5 * width,), F32), spread(tops, width, -1e30),
+    ]).reshape(-1, width)
     if kernels:
-        grad_tokens, output, last_sums = call_exchange(
-            last_kernel, 4, 2, 2, [(narrow, BF16), (narrow, BF16), ((8, width), F32)],
+        first_part, scattered_up = lax.optimization_barrier((first_part, scattered_up))
+        sums = (8, width)
+        grad_tokens, output, small, sums = call_exchange(
+            functools.partial(last_kernel, fsdp), 4, 2, 2,
+            [(narrow, BF16), (narrow, BF16), (small.shape, F32), (sums, F32)],
             [first_part, output_part, tokens, hidden, grad_hidden,
-             jnp.concatenate([gain1, down_b], 0)],
-        )
+             jnp.concatenate([gain1, down_b], 0), small],
+            (pltpu.VMEM((stages + 1,) + small.shape, F32),
+             pltpu.VMEM((stages,) + small.shape, F32),
+             pltpu.VMEM((stages + 1,) + sums, F32), pltpu.VMEM((stages,) + sums, F32)),
+            (2, 2, stages),
+        )
+        sums = sums[:2]
     else:
         grad_first = scatter_dp(first_part, dp)
         normed1, inverse1 = norm_stats(inputs)
         grad_tokens = grad_hidden + norm_back(grad_first, normed1, inverse1, gain1)
         output = hidden + scatter_dp(output_part, dp) + down_b
-        last_sums = jnp.stack([jnp.sum(grad_first * normed1, axis=0), jnp.sum(grad_first, axis=0)])
-
-    def spread(piece):
-        wide = jnp.zeros((piece.shape[0] * dp,), F32)
-        return lax.dynamic_update_slice(wide, piece, (spot * piece.shape[0],))
-
-    def owned(total, start, size):
-        step = size // (dp * fsdp)
-        return lax.dynamic_slice(total, (start + rank * step,), (step,))
-
-    early = jnp.concatenate([
-        branch_sums[:4].reshape(4 * width),
-        spread(jnp.sum(grad_upward.astype(F32), axis=0)),
-        spread(jnp.sum(grad_proj[:, :part].astype(F32), axis=0)),
-        spread(jnp.sum(grad_proj[:, 2 * part :].astype(F32), axis=0)),
-    ])
-    early = combine_all(early, both, jnp.add)
-    late = combine_all(last_sums[:2].reshape(2 * width), both, jnp.add)
-
-    head_top = jnp.full((heads,), -1e30, F32)
-    head_top = lax.dynamic_update_slice(head_top, tops, (spot * local_heads,))
-    head_top = combine_all(head_top, both, jnp.maximum)
+        sums = jnp.stack([jnp.sum(grad_first * normed1, axis=0), jnp.sum(grad_first, axis=0)])
+        small = combine_all(small, both, sum_or_top)
+        sums = combine_all(sums, both, jnp.add)
+    grad_w_up = exchange_columns(scattered_up)
+    ups_at = 4 + ff // width
+    owned = lax.dynamic_slice(small, (0, rank * shard), (small.shape[0], shard))
+    owned_late = lax.dynamic_slice(sums, (0, rank * shard), (2, shard))
+    ff_shard = ff // (dp * fsdp)
+    owned_up = lax.dynamic_slice(
+        small[4:ups_at].reshape(ff), (rank * ff_shard,), (ff_shard,)
+    )
+
+    head_top = small[-1, :heads]
     factor = jnp.sqrt(CLIP_TAU / jnp.maximum(head_top, CLIP_TAU))
     column = jnp.repeat(factor, HEAD_DIM)
     columns = jnp.concatenate([column, column, jnp.ones((width,), F32)])
@@ -657,18 +727,18 @@
         output.astype(BF16),
         grad_tokens.astype(BF16),
         grad_w_qkv,
-        owned(early, 4 * width + ff, width),
-        owned(early, 5 * width + ff, width),
+        owned[ups_at],
+        owned[ups_at + 1],
         grad_w_out,
-        owned(early, 3 * width, width),
-        owned(late, 0, width),
-        owned(late, width, width),
+        owned[3],
+        owned_late[0],
+        owned_late[1],
         grad_w_up,
-        owned(early, 4 * width, ff),
+        owned_up,
         grad_w_down,
-        owned(early, 0, width),
-        owned(early, width, width),
-        owned(early, 2 * width, width),
+        owned[0],
+        owned[1],
+        owned[2],
         clipped,
     )
 

time: 773 us -> 793 us (1.026)
  Pallas kernels: 335 us -> 385 us
  starting transfers between devices: 30.8 us -> 8.64 us
  matrix products: 131 us -> 117 us
    reduce_scatter x2, waiting for transfers between devices: 18.6 us -> 121 us  [reduce_columns(): return lax.psum_scatter(grad, 'fsdp', scatter_dimension=1, tiled=True)]
    reduce_scatter x2, waiting for transfers between devices: 97.1 us -> 32.5 us  [reduce_rows(): lax.psum_scatter(grad, 'fsdp', scatter_dimension=0, tiled=True).astype(F32)]
    pallas_call x4, Pallas kernels: 289 us -> 351 us  [call_exchange(): pl.pallas_call(kernel, in_specs=[pl.BlockSpec(memory_space=pltpu.VMEM)] *...]
    ppermute x20 -> x0, waiting for transfers between devices: 52.8 us -> none  [swap(): return lax.ppermute(value, axis, [(i, i ^ bit) for i in range(size)])]
    ppermute x20 -> x0, starting transfers between devices: 22.4 us -> none  [swap(): return lax.ppermute(value, axis, [(i, i ^ bit) for i in range(size)])]
    dot_general x4 -> x3, matrix products: 49.1 us -> 34.9 us  [dot(): return jnp.dot(a, b, preferred_element_type=F32)]
    all_gather x1, waiting for transfers between devices: 0.01 us -> 9.77 us  [layer(): down_w = lax.all_gather(w_down, 'fsdp', axis=0, tiled=True)]
  transfers between devices with their start and end apart: 30 -> 10, of which waited for: 16 -> 5; matrix products, arithmetic and copies ran while one was open for 15% -> 14% of each run, Pallas kernels for 30% -> 36%
where the time goes in v1:
time: 793 us; the launch traced here: 789 us
  Pallas kernels  385 us (49%)
  waiting for transfers between devices  173 us (22%)
  matrix products  117 us (15%)
  local copies, waits for them, and re-layouts  42.1 us (5%)
  blocking collectives  31.9 us (4%)
  other arithmetic  17 us (2%)
  between operations  15 us (2%)
  starting transfers between devices  8.64 us (1%)
    pallas_call x4, Pallas kernels, call_exchange(): pl.pallas_call(kernel, in_specs=[pl.BlockSpec(memory_space=pltpu.VMEM)] *...  351 us
    reduce_scatter x2, waiting for transfers between devices, reduce_columns(): return lax.psum_scatter(grad, 'fsdp', scatter_dimension=1, tiled=True)  121 us
    dot_general x4, matrix products, dot_tn(): lax.dot_general(a, b, (((0,), (0,)), ((), ())), preferred_element_type=F32)  41.3 us
    dot_general x4, matrix products, dot_nt(): lax.dot_general(a, b, (((1,), (1,)), ((), ())), preferred_element_type=F32)  40.5 us
    dot_general x3, matrix products, dot(): return jnp.dot(a, b, preferred_element_type=F32)  34.9 us
    reduce_scatter x2, waiting for transfers between devices, reduce_rows(): lax.psum_scatter(grad, 'fsdp', scatter_dimension=0, tiled=True).astype(F32)  32.5 us
    pallas_call x1, Pallas kernels, attend_back(): pl.pallas_call(attend_back_kernel, grid=(rows // length,), in_specs=[pl.B...  22.2 us
    all_to_all x1, blocking collectives, layer(): lax.all_to_all(cols, 'dp', 1, 0, tiled=True).reshape(dp, shard, 3 * part)  16.4 us
  transfers between devices with their start and end apart: 10, of which 5 were waited for; matrix products, arithmetic and copies ran while one was open for 14% of the time, Pallas kernels for 36%

profile of v1, /device:TPU:0, one launch (start us, length us, event | category | flops | bytes accessed | tf_op | source)
XLA Modules:
  0.0 789.1 jit_solution(15572354020834581058)
XLA Ops:
  11.2 16.4 %all_to_all.52 = bf16[64,4,1536]{2,0,1:T(8,128)(2,1)} all-to-all(bf16[64,4,1536]{2,0,1:T(8,128)(2,1)S(1)} %all_to_all.40), channel_id=1, replica_groups=mesh['dp'=4,'fsdp'=8] {'dp'}, dimensions={1} | all-to-all | bytes 1572864 | tf_op jit(solution)/shard_map/all_to_all | solution.py:560
  28.7 15.5 %all_to_all.53 = bf16[64,4,2048]{2,0,1:T(8,128)(2,1)S(1)} all-to-all(bf16[64,4,2048]{2,0,1:T(8,128)(2,1)S(1)} %bitcast.80), channel_id=1, replica_groups=mesh['dp'=4,'fsdp'=8] {'dp'}, dimensions={1} | all-to-all | bytes 2097152 | tf_op jit(solution)/shard_map/all_to_all | solution.py:563
  48.3 79.8 %shard_map.270 = (bf16[1024,2048]{1,0:T(8,128)(2,1)}, bf16[1024,2048]{1,0:T(8,128)(2,1)}, bf16[32,768]{1,0:T(8,128)(2,1)S(1)}) custom-call(bf16[256,2048]{1,0:T(8,128)(2,1)S(1)} %copy-done, bf16[256,2048]{1,0:T(8,128)(2,1)S(1)} %copy-done.1, bf16[32,768]{1,0:T(8,128)(2,1)S(1)} %dynamic_update_slice.15.table_ref), custom_call_target="tpu_custom_call" | custom-call | flops 2097152 | bytes 209715200 | tf_op jit(solution)/shard_map/pallas_call | solution.py:392
  134.7 11.9 %add_convert_fusion.qkv_ref = bf16[1024,1536]{1,0:T(8,128)(2,1)} fusion(bf16[2048,1536]{1,0:T(8,128)(2,1)} %bitcast.87, f32[1536]{0:T(1024)S(1)} %fusion.13, bf16[1024,2048]{1,0:T(8,128)(2,1)} %get-tuple-element.45, f32[2048]{0:T(1024)S(1)} %add.100, f32[2048]{0:T(1024)S(1)} %mul.94, f32[1024]{0:T(1024)S(1)} %add_rsqrt_fusion, ...), kind=kOutput, calls=%fused_computation.21 | convolution fusion | flops 6458179584 | bytes 13662208 | tf_op jit(solution)/shard_map/dot_general | solution.py:541
  146.6 11.6 %attend.1 = (bf16[1024,512]{1,0:T(8,128)(2,1)}, f32[32,128]{1,0:T(8,128)}) custom-call(f32[8]{0:T(128)} %exponential_multiply_fusion.slope_ref, f32[256,256]{1,0:T(8,128)} %convert_select_fusion.distance_ref, bf16[1024,1536]{1,0:T(8,128)(2,1)} %add_convert_fusion.qkv_ref), custom_call_target="tpu_custom_call" | custom-call | flops 536870912 | bytes 4194304 | tf_op jit(solution)/shard_map/attend/pallas_call | solution.py:478
  158.2 6.3 convolution_convert_fusion.5.partial_ref
  164.4 73.0 %shard_map.271 = (bf16[1024,2048]{1,0:T(8,128)(2,1)}, f32[256,2048]{1,0:T(8,128)S(1)}) custom-call(bf16[1024,2048]{1,0:T(8,128)(2,1)} %convolution_convert_fusion.5.partial_ref, bf16[256,2048]{1,0:T(8,128)(2,1)S(1)} %copy-done, f32[3,2048]{1,0:T(4,128)S(1)} %pad_maximum_fusion.params_ref), custom_call_target="tpu_custom_call" | custom-call | flops 2097152 | bytes 209715200 | tf_op jit(solution)/shard_map/pallas_call | solution.py:392
  237.5 11.4 %copy.42 = bf16[4,512,2048]{2,1,0:T(8,128)(2,1)} copy(bf16[4,512,2048]{2,0,1:T(4,128)(2,1)} %all-gather.9.cloned.1.call-done) | data formatting | bytes 16777216 | tf_op jit(solution)/shard_map/all_gather | solution.py:564
  248.9 16.7 %fusion.10 = (bf16[1024,2048]{1,0:T(8,128)(2,1)}, bf16[1024,2048]{1,0:T(8,128)(2,1)S(1)}) fusion(f32[2048]{0:T(1024)S(1)} %bitcast.86, bf16[1024,2048]{1,0:T(8,128)(2,1)} %get-tuple-element.48, bf16[2048,2048]{1,0:T(8,128)(2,1)} %bitcast.73), kind=kOutput, calls=%fused_computation.13 | convolution fusion | flops 8615100416 | bytes 20979712 | tf_op jit(solution)/shard_map/dot_general | solution.py:541
  267.6 11.9 %convolution_convert_fusion.2 = bf16[2048,2048]{1,0:T(8,128)(2,1)} fusion(bf16[1024,2048]{1,0:T(8,128)(2,1)S(1)} %get-tuple-element.50.active_ref, bf16[1024,2048]{1,0:T(8,128)(2,1)S(1)} %copy-done.24), kind=kOutput, calls=%fused_computation.20 | convolution fusion | flops 8594128896 | bytes 16777216 | tf_op jit(solution)/shard_map/dot_general | solution.py:427
  279.5 9.8 %all-gather.11.cloned.1.call-done.weight_ref = bf16[2048,2048]{1,0:T(8,128)(2,1)} async-done(((bf16[256,2048]{1,0:T(8,128)(2,1)}), bf16[2048,2048]{1,0:T(8,128)(2,1)}) %all-gather.11.cloned.1.call-update) | async-done | bytes 8388624 | tf_op jit(solution)/shard_map/all_gather | solution.py:565
  289.3 13.3 %convert_reduce_fusion.1 = (f32[2048]{0:T(1024)S(1)}, bf16[1024,2048]{1,0:T(8,128)(2,1)S(1)}) fusion(bf16[1024,2048]{1,0:T(8,128)(2,1)} %get-tuple-element.52, bf16[1024,2048]{1,0:T(8,128)(2,1)} %get-tuple-element.51, bf16[2048,2048]{1,0:T(8,128)(2,1)} %all-gather.11.cloned.1.call-done.weight_ref), kind=kOutput, calls=%fused_computation.14 | convolution fusion | flops 8600418304 | bytes 20979712 | tf_op jit(solution)/shard_map/dot_general | solution.py:423
  302.7 11.3 %convolution_convert_fusion.1 = bf16[2048,2048]{1,0:T(8,128)(2,1)} fusion(bf16[1024,2048]{1,0:T(8,128)(2,1)S(1)} %copy-done.25, bf16[1024,2048]{1,0:T(8,128)(2,1)S(1)} %get-tuple-element.53), kind=kOutput, calls=%fused_computation.19 | convolution fusion | flops 8594128896 | bytes 16777216 | tf_op jit(solution)/shard_map/dot_general | solution.py:427
  314.0 10.4 %convolution_convert_fusion.4.partial_ref = bf16[1024,2048]{1,0:T(8,128)(2,1)} fusion(bf16[1024,2048]{1,0:T(8,128)(2,1)S(1)} %get-tuple-element.53, bf16[2048,2048]{1,0:T(8,128)(2,1)S(1)} %bitcast.76), kind=kOutput, calls=%fused_computation.23 | convolution fusion | flops 8592031744 | bytes 16777216 | tf_op jit(solution)/shard_map/dot_general | solution.py:423
  324.5 77.8 %shard_map.272 = (bf16[1024,2048]{1,0:T(8,128)(2,1)}, f32[256,2048]{1,0:T(8,128)S(1)}, f32[8,2048]{1,0:T(8,128)S(1)}, bf16[1024,2048]{1,0:T(8,128)(2,1)}) custom-call(bf16[1024,2048]{1,0:T(8,128)(2,1)} %convolution_convert_fusion.4.partial_ref, f32[256,2048]{1,0:T(8,128)S(1)} %get-tuple-element.54.hidden_ref, bf16[256,2048]{1,0:T(8,128)(2,1)S(1)} %copy-done.2, ...), custom_call_target="tpu_custom_call" | custom-call | flops 2097152 | bytes 209715200 | tf_op jit(solution)/shard_map/pallas_call | solution.py:392
  409.2 22.2 %attend_back.1 = bf16[1024,1536]{1,0:T(8,128)(2,1)} custom-call(f32[8]{0:T(128)} %exponential_multiply_fusion.slope_ref, f32[256,256]{1,0:T(8,128)} %convert_select_fusion.distance_ref, bf16[1024,1536]{1,0:T(8,128)(2,1)} %add_convert_fusion.qkv_ref, bf16[1024,512]{1,0:T(8,128)(2,1)} %convolution_convert_fusion.7.grad_ref), custom_call_target="tpu_custom_call" | custom-call | flops 1342177280 | bytes 7340032 | tf_op jit(solution)/shard_map/attend_back/pallas_call | solution.py:505
  431.4 11.8 %convolution_convert_fusion = bf16[2048,1536]{1,0:T(8,128)(2,1)} fusion(bf16[1024,1536]{1,0:T(8,128)(2,1)} %attend_back.1, bf16[1024,2048]{1,0:T(8,128)(2,1)} %get-tuple-element.45, f32[2048]{0:T(1024)S(1)} %add.100, f32[2048]{0:T(1024)S(1)} %mul.94, f32[1024]{0:T(1024)S(1)} %add_rsqrt_fusion, f32[1024]{0:T(1024)S(1)} %broadcast_multiply_fusion), kind=kOutput, calls=%fused_computation.18 | convolution fusion | flops 6458179584 | bytes 13656064 | tf_op jit(solution)/shard_map/dot_general | solution.py:427
  443.5 6.2 convolution_convert_fusion.6
  453.9 11.2 %convolution_convert_fusion.3.first_ref = bf16[1024,2048]{1,0:T(8,128)(2,1)} fusion(bf16[1024,1536]{1,0:T(8,128)(2,1)} %attend_back.1, bf16[2048,1536]{1,0:T(8,128)(2,1)} %bitcast.88), kind=kOutput, calls=%fused_computation.22 | convolution fusion | flops 6444548096 | bytes 13631488 | tf_op jit(solution)/shard_map/dot_general | solution.py:423
  465.1 45.6 %reduce-scatter.7.cloned.1.call-done = bf16[4,64,1536]{2,1,0:T(8,128)(2,1)} async-done(((bf16[4,512,1536]{2,1,0:T(8,128)(2,1)}), bf16[4,64,1536]{2,1,0:T(8,128)(2,1)}) %reduce-scatter.7.cloned.1.call-update) | async-done | bytes 786448 | tf_op jit(solution)/shard_map/reduce_scatter | solution.py:627
  515.4 32.5 %reduce-scatter.9.cloned.1.call-done = bf16[64,2048]{1,0:T(8,128)(2,1)} async-done(((bf16[512,2048]{1,0:T(8,128)(2,1)}), bf16[64,2048]{1,0:T(8,128)(2,1)}) %reduce-scatter.9.cloned.1.call-update) | async-done | bytes 262160 | tf_op jit(solution)/shard_map/reduce_scatter | solution.py:623
  563.1 75.3 %reduce-scatter.5.cloned.1.call-done = bf16[4,64,2048]{2,1,0:T(8,128)(2,1)} async-done(((bf16[4,512,2048]{2,1,0:T(8,128)(2,1)}), bf16[4,64,2048]{2,1,0:T(8,128)(2,1)}) %reduce-scatter.5.cloned.1.call-update) | async-done | bytes 1048592 | tf_op jit(solution)/shard_map/reduce_scatter | solution.py:627
  638.4 120.2 %shard_map.273 = (bf16[256,2048]{1,0:T(8,128)(2,1)S(1)}, bf16[256,2048]{1,0:T(8,128)(2,1)S(1)}, f32[16,2048]{1,0:T(8,128)S(1)}, f32[8,2048]{1,0:T(8,128)S(1)}) custom-call(bf16[1024,2048]{1,0:T(8,128)(2,1)} %convolution_convert_fusion.3.first_ref, bf16[1024,2048]{1,0:T(8,128)(2,1)} %get-tuple-element.58.output_ref, bf16[256,2048]{1,0:T(8,128)(2,1)S(1)} %copy-done, ...), custom_call_target="tpu_custom_call" | custom-call | flops 2097152 | bytes 209715200 | tf_op jit(solution)/shard_map/pallas_call | solution.py:392
  771.0 7.3 all-to-all-done.3
  (159 shorter events, 64.6 us)
Async XLA Ops:
  7.2 21.2 %copy-start.10 = (bf16[64,8192]{1,0:T(8,128)(2,1)S(1)}, bf16[64,8192]{1,0:T(8,128)(2,1)}, u32[]{:S(2)}) copy-start(bf16[64,8192]{1,0:T(8,128)(2,1)} %param.24) | copy-start | bytes 3145732
  7.2 127.5 %all-gather.5.cloned.1.call-start = ((), (), s32[]{:S(2)}) async-start(), calls=%async_computation.8 | async-start | bytes 7077888 | tf_op jit(solution)/shard_map/all_gather | solution.py:561
  27.6 130.5 %all-gather.7.cloned.1.call-start = ((), (), s32[]{:S(2)}) async-start(), calls=%async_computation.9 | async-start | bytes 2359296 | tf_op jit(solution)/shard_map/all_gather | solution.py:558
  28.4 209.1 %all-gather.9.cloned.1.call-start = ((), (), s32[]{:S(2)}) async-start(), calls=%async_computation.10 | async-start | bytes 9437184 | tf_op jit(solution)/shard_map/all_gather | solution.py:564
  28.4 18.2 %copy-start.15 = (bf16[64]{0:T(256)(128)(2,1)S(1)}, bf16[64]{0:T(256)(128)(2,1)}, u32[]{:S(2)}) copy-start(bf16[64]{0:T(256)(128)(2,1)} %param.21) | copy-start | bytes 388
  28.4 18.2 %copy-start.16 = (bf16[64]{0:T(256)(128)(2,1)S(1)}, bf16[64]{0:T(256)(128)(2,1)}, u32[]{:S(2)}) copy-start(bf16[64]{0:T(256)(128)(2,1)} %param.22) | copy-start | bytes 388
  28.4 18.2 %copy-start.17 = (bf16[64]{0:T(256)(128)(2,1)S(1)}, bf16[64]{0:T(256)(128)(2,1)}, u32[]{:S(2)}) copy-start(bf16[64]{0:T(256)(128)(2,1)} %param.23) | copy-start | bytes 388
  28.5 18.2 %copy-start.18 = (bf16[64]{0:T(256)(128)(2,1)S(1)}, bf16[64]{0:T(256)(128)(2,1)}, u32[]{:S(2)}) copy-start(bf16[64]{0:T(256)(128)(2,1)} %param.27) | copy-start | bytes 388
  28.5 18.2 %copy-start.19 = (bf16[64]{0:T(256)(128)(2,1)S(1)}, bf16[64]{0:T(256)(128)(2,1)}, u32[]{:S(2)}) copy-start(bf16[64]{0:T(256)(128)(2,1)} %param.28) | copy-start | bytes 388
  28.5 18.2 %copy-start.20 = (bf16[64]{0:T(256)(128)(2,1)S(1)}, bf16[64]{0:T(256)(128)(2,1)}, u32[]{:S(2)}) copy-start(bf16[64]{0:T(256)(128)(2,1)} %param.29) | copy-start | bytes 388
  28.5 18.2 %copy-start.21 = (bf16[64]{0:T(256)(128)(2,1)S(1)}, bf16[64]{0:T(256)(128)(2,1)}, u32[]{:S(2)}) copy-start(bf16[64]{0:T(256)(128)(2,1)} %param.18) | copy-start | bytes 388
  28.5 18.2 %copy-start.22 = (bf16[64]{0:T(256)(128)(2,1)S(1)}, bf16[64]{0:T(256)(128)(2,1)}, u32[]{:S(2)}) copy-start(bf16[64]{0:T(256)(128)(2,1)} %param.19) | copy-start | bytes 388
  28.5 19.8 %copy-start = (bf16[256,2048]{1,0:T(8,128)(2,1)S(1)}, bf16[256,2048]{1,0:T(8,128)(2,1)}, u32[]{:S(2)}) copy-start(bf16[256,2048]{1,0:T(8,128)(2,1)} %tokens_ref.3) | copy-start | bytes 3145732
  28.5 19.8 %copy-start.1 = (bf16[256,2048]{1,0:T(8,128)(2,1)S(1)}, bf16[256,2048]{1,0:T(8,128)(2,1)}, u32[]{:S(2)}) copy-start(bf16[256,2048]{1,0:T(8,128)(2,1)} %cotangent_ref.1) | copy-start | bytes 3145732
  46.0 243.4 %all-gather.11.cloned.1.call-start = ((), (), s32[]{:S(2)}) async-start(), calls=%async_computation.11 | async-start | bytes 9437184 | tf_op jit(solution)/shard_map/all_gather | solution.py:565
  46.5 464.1 %reduce-scatter.7.cloned.1.call-start = ((), (), s32[]{:S(2)}) async-start(), calls=%async_computation.13 | async-start | bytes 7077888 | tf_op jit(solution)/shard_map/reduce_scatter | solution.py:627
  248.9 18.7 %copy-start.24 = (bf16[1024,2048]{1,0:T(8,128)(2,1)S(1)}, bf16[1024,2048]{1,0:T(8,128)(2,1)}, u32[]{:S(2)}) copy-start(bf16[1024,2048]{1,0:T(8,128)(2,1)} %get-tuple-element.51) | copy-start | bytes 12582916
  289.3 24.7 %slice-start = ((s8[8388608]{0:T(1024)(128)(4,1)}), s8[4194304]{0:T(1024)(128)(4,1)S(1)}, s32[]{:S(2)}) async-start(s8[8388608]{0:T(1024)(128)(4,1)} %bitcast.74), calls=%async_computation.16 | async-start | bytes 8388608
  324.5 79.2 %copy-start.26 = (bf16[512,2048]{1,0:T(8,128)(2,1)S(1)}, bf16[512,2048]{1,0:T(8,128)(2,1)}, u32[]{:S(2)}) copy-start(bf16[512,2048]{1,0:T(8,128)(2,1)} %all-gather.7.cloned.1.call-done) | copy-start | bytes 6291460
  443.2 104.7 %reduce-scatter.9.cloned.1.call-start = ((), (), s32[]{:S(2)}) async-start(), calls=%async_computation.14 | async-start | bytes 2359296 | tf_op jit(solution)/shard_map/reduce_scatter | solution.py:623
  449.7 188.7 %reduce-scatter.5.cloned.1.call-start = ((), (), s32[]{:S(2)}) async-start(), calls=%async_computation.12 | async-start | bytes 9437184 | tf_op jit(solution)/shard_map/reduce_scatter | solution.py:627
  450.5 317.0 %reduce-scatter.11.cloned.1.call-start = ((), (), s32[]{:S(2)}) async-start(), calls=%async_computation.15 | async-start | bytes 9437184 | tf_op jit(solution)/shard_map/reduce_scatter | solution.py:623
  510.6 39.1 %all-to-all-start.2 = ((bf16[4,64,1536]{2,1,0:T(8,128)(2,1)}), bf16[4,64,1536]{2,1,0:T(8,128)(2,1)}, u32[]{:S(2)}, u32[]{:S(2)}) async-start(bf16[4,64,1536]{2,1,0:T(8,128)(2,1)} %reduce-scatter.7.cloned.1.call-done), calls=%async_computation.4 | async-start | bytes 1572864 | tf_op jit(solution)/shard_map/all_to_all | solution.py:630
  760.8 17.5 %all-to-all-start.3 = ((bf16[4,64,2048]{2,1,0:T(8,128)(2,1)}), bf16[4,64,2048]{2,1,0:T(8,128)(2,1)S(1)}, u32[]{:S(2)}, u32[]{:S(2)}) async-start(bf16[4,64,2048]{2,1,0:T(8,128)(2,1)} %reduce-scatter.5.cloned.1.call-done), calls=%async_computation.6 | async-start | bytes 2097152 | tf_op jit(solution)/shard_map/all_to_all | solution.py:630
  (15 other events, 90.3 us)
Sparse Core Ops, SparseCore 0:
  27.7 66.4 all-gather.4
  95.8 27.8 all-gather.6
  125.8 81.4 all-gather.8
  208.8 80.5 all-gather.10
  443.3 67.2 reduce-scatter.6
  513.4 34.5 reduce-scatter.8
  550.2 88.1 reduce-scatter.4
  640.7 93.6 reduce-scatter.10

commit v2 on v1

--- a/solution.py
+++ b/solution.py
@@ -342,12 +342,11 @@
 
 
 def last_kernel(
-    fsdp, first_ref, output_ref, tokens_ref, hidden_ref, grad_ref, params_ref, small_ref,
-    tokens_out, output_out, small_out, sums_out, landing, passing, last, held, small_landing,
-    sums, sums_landing, sems, small_sems,
+    first_ref, output_ref, tokens_ref, hidden_ref, grad_ref, params_ref, tokens_out, output_out,
+    sums_out, landing, passing, last, sems,
 ):
-    near, partners = neighbours(fsdp)
-    sums[0] = jnp.zeros_like(sums_out)
+    near, _ = neighbours()
+    sums_out[...] = jnp.zeros_like(sums_out)
     first, second = (
         Scatter(ref, landing.at[k], passing.at[k], last.at[k], sems.at[k], near)
         for k, ref in enumerate((first_ref, output_ref))
@@ -359,23 +358,18 @@
         normed, inverse_std = row_norm(tokens_ref[rows].astype(F32))
         grad = grad_ref[rows] + row_back(total, normed, inverse_std, params_ref[0:1])
         tokens_out[rows] = grad.astype(BF16)
-        add_sums(sums.at[0], (total * normed, total))
+        add_sums(sums_out, (total * normed, total))
 
     def second_rows(path, step):
         rows = second.own(path, step)
         total = second.total(path, step)
         output_out[rows] = (hidden_ref[rows] + total + params_ref[1:2]).astype(BF16)
 
-    held[0] = small_ref[...]
     for job in (first, second):
         each_step(lambda step, job=job: [job.begin(path, step) for path in range(2)])
-    double_all(held, small_landing, small_sems.at[0], partners, sum_or_top)
-    small_out[...] = held[len(partners)]
     for job in (first, second):
         each_step(lambda step, job=job: [job.relay(path, step) for path in range(2)])
     each_step(lambda step: [first_rows(path, step) for path in range(2)])
-    double_all(sums, sums_landing, small_sems.at[1], partners, jnp.add)
-    sums_out[...] = sums[len(partners)]
     each_step(lambda step: [second_rows(path, step) for path in range(2)])
     for job in (first, second):
         each_step(lambda step, job=job: [job.finish(path, step) for path in range(2)])
@@ -683,36 +677,28 @@
     up_sum = jnp.sum(grad_upward.astype(F32), axis=0)
     q_sum = jnp.sum(grad_proj[:, :part].astype(F32), axis=0)
     v_sum = jnp.sum(grad_proj[:, 2 * part :].astype(F32), axis=0)
-    small = jnp.concatenate([
-        branch_sums[:4].reshape(4 * width), spread(up_sum, ff), spread(q_sum, width),
-        spread(v_sum, width), jnp.zeros((5 * width,), F32), spread(tops, width, -1e30),
-    ]).reshape(-1, width)
     if kernels:
         first_part, scattered_up = lax.optimization_barrier((first_part, scattered_up))
-        sums = (8, width)
-        grad_tokens, output, small, sums = call_exchange(
-            functools.partial(last_kernel, fsdp), 4, 2, 2,
-            [(narrow, BF16), (narrow, BF16), (small.shape, F32), (sums, F32)],
+        grad_tokens, output, sums = call_exchange(
+            last_kernel, 4, 2, 2, [(narrow, BF16), (narrow, BF16), ((8, width), F32)],
             [first_part, output_part, tokens, hidden, grad_hidden,
-             jnp.concatenate([gain1, down_b], 0), small],
-            (pltpu.VMEM((stages + 1,) + small.shape, F32),
-             pltpu.VMEM((stages,) + small.shape, F32),
-             pltpu.VMEM((stages + 1,) + sums, F32), pltpu.VMEM((stages,) + sums, F32)),
-            (2, 2, stages),
-        )
-        sums = sums[:2]
+             jnp.concatenate([gain1, down_b], 0)],
+        )
     else:
         grad_first = scatter_dp(first_part, dp)
         normed1, inverse1 = norm_stats(inputs)
         grad_tokens = grad_hidden + norm_back(grad_first, normed1, inverse1, gain1)
         output = hidden + scatter_dp(output_part, dp) + down_b
         sums = jnp.stack([jnp.sum(grad_first * normed1, axis=0), jnp.sum(grad_first, axis=0)])
-        small = combine_all(small, both, sum_or_top)
-        sums = combine_all(sums, both, jnp.add)
+    small = jnp.concatenate([
+        branch_sums[:4].reshape(4 * width), spread(up_sum, ff), spread(q_sum, width),
+        spread(v_sum, width), sums[:2].reshape(2 * width), spread(tops, width, -1e30),
+    ]).reshape(-1, width)
     grad_w_up = exchange_columns(scattered_up)
+    small, grad_w_up = lax.optimization_barrier((small, grad_w_up))
+    small = combine_all(small, both, sum_or_top)
     ups_at = 4 + ff // width
     owned = lax.dynamic_slice(small, (0, rank * shard), (small.shape[0], shard))
-    owned_late = lax.dynamic_slice(sums, (0, rank * shard), (2, shard))
     ff_shard = ff // (dp * fsdp)
     owned_up = lax.dynamic_slice(
         small[4:ups_at].reshape(ff), (rank * ff_shard,), (ff_shard,)
@@ -731,8 +717,8 @@
         owned[ups_at + 1],
         grad_w_out,
         owned[3],
-        owned_late[0],
-        owned_late[1],
+        owned[ups_at + 2],
+        owned[ups_at + 3],
         grad_w_up,
         owned_up,
         grad_w_down,

time: 793 us -> 666 us (0.84)
  waiting for transfers between devices: 173 us -> 79.8 us
  Pallas kernels: 385 us -> 346 us
    reduce_scatter x2, waiting for transfers between devices: 121 us -> 0.01 us  [reduce_columns(): return lax.psum_scatter(grad, 'fsdp', scatter_dimension=1, tiled=True)]
    pallas_call x4, Pallas kernels: 351 us -> 313 us  [call_exchange(): pl.pallas_call(kernel, in_specs=[pl.BlockSpec(memory_space=pltpu.VMEM)] *...]
    ppermute x0 -> x5, waiting for transfers between devices: none -> 22.1 us  [swap(): return lax.ppermute(value, axis, [(i, i ^ bit) for i in range(size)])]
    reduce_scatter x2, waiting for transfers between devices: 32.5 us -> 46 us  [reduce_rows(): lax.psum_scatter(grad, 'fsdp', scatter_dimension=0, tiled=True).astype(F32)]
  transfers between devices with their start and end apart: 10 -> 15, of which waited for: 5 -> 6; matrix products, arithmetic and copies ran while one was open for 14% -> 21% of each run, Pallas kernels for 36% -> 52%
where the time goes in v2:
time: 666 us; the launch traced here: 662 us
  Pallas kernels  346 us (52%)
  matrix products  121 us (18%)
  waiting for transfers between devices  79.8 us (12%)
  local copies, waits for them, and re-layouts  39.5 us (6%)
  blocking collectives  31.9 us (5%)
  other arithmetic  16.3 us (2%)
  between operations  15 us (2%)
  starting transfers between devices  12.5 us (2%)
    pallas_call x4, Pallas kernels, call_exchange(): pl.pallas_call(kernel, in_specs=[pl.BlockSpec(memory_space=pltpu.VMEM)] *...  313 us
    reduce_scatter x2, waiting for transfers between devices, reduce_rows(): lax.psum_scatter(grad, 'fsdp', scatter_dimension=0, tiled=True).astype(F32)  46 us
    dot_general x4, matrix products, dot_nt(): lax.dot_general(a, b, (((1,), (1,)), ((), ())), preferred_element_type=F32)  44.2 us
    dot_general x4, matrix products, dot_tn(): lax.dot_general(a, b, (((0,), (0,)), ((), ())), preferred_element_type=F32)  41.6 us
    dot_general x3, matrix products, dot(): return jnp.dot(a, b, preferred_element_type=F32)  34.9 us
    pallas_call x1, Pallas kernels, attend_back(): pl.pallas_call(attend_back_kernel, grid=(rows // length,), in_specs=[pl.B...  22.2 us
    ppermute x5, waiting for transfers between devices, swap(): return lax.ppermute(value, axis, [(i, i ^ bit) for i in range(size)])  22.1 us
    all_to_all x1, blocking collectives, layer(): lax.all_to_all(cols, 'dp', 1, 0, tiled=True).reshape(dp, shard, 3 * part)  16.4 us
  transfers between devices with their start and end apart: 15, of which 6 were waited for; matrix products, arithmetic and copies ran while one was open for 21% of the time, Pallas kernels for 52%

profile of v2, /device:TPU:0, one launch (start us, length us, event | category | flops | bytes accessed | tf_op | source)
XLA Modules:
  0.0 662.1 jit_solution(8730984959157064137)
XLA Ops:
  11.2 16.4 %all_to_all.52 = bf16[64,4,1536]{2,0,1:T(8,128)(2,1)} all-to-all(bf16[64,4,1536]{2,0,1:T(8,128)(2,1)S(1)} %all_to_all.40), channel_id=1, replica_groups=mesh['dp'=4,'fsdp'=8] {'dp'}, dimensions={1} | all-to-all | bytes 1572864 | tf_op jit(solution)/shard_map/all_to_all | solution.py:554
  28.7 15.5 %all_to_all.53 = bf16[64,4,2048]{2,0,1:T(8,128)(2,1)S(1)} all-to-all(bf16[64,4,2048]{2,0,1:T(8,128)(2,1)S(1)} %bitcast.81), channel_id=1, replica_groups=mesh['dp'=4,'fsdp'=8] {'dp'}, dimensions={1} | all-to-all | bytes 2097152 | tf_op jit(solution)/shard_map/all_to_all | solution.py:557
  48.3 79.9 %shard_map.270 = (bf16[1024,2048]{1,0:T(8,128)(2,1)}, bf16[1024,2048]{1,0:T(8,128)(2,1)}, bf16[32,768]{1,0:T(8,128)(2,1)S(1)}) custom-call(bf16[256,2048]{1,0:T(8,128)(2,1)S(1)} %copy-done, bf16[256,2048]{1,0:T(8,128)(2,1)S(1)} %copy-done.1, bf16[32,768]{1,0:T(8,128)(2,1)S(1)} %dynamic_update_slice.15.table_ref), custom_call_target="tpu_custom_call" | custom-call | flops 2097152 | bytes 209715200 | tf_op jit(solution)/shard_map/pallas_call | solution.py:386
  134.7 11.9 %add_convert_fusion.qkv_ref = bf16[1024,1536]{1,0:T(8,128)(2,1)} fusion(bf16[2048,1536]{1,0:T(8,128)(2,1)} %bitcast.89, f32[1536]{0:T(1024)S(1)} %fusion.13, bf16[1024,2048]{1,0:T(8,128)(2,1)} %get-tuple-element.46, f32[2048]{0:T(1024)S(1)} %add.114, f32[2048]{0:T(1024)S(1)} %mul.93, f32[1024]{0:T(1024)S(1)} %add_rsqrt_fusion, ...), kind=kOutput, calls=%fused_computation.21 | convolution fusion | flops 6458179584 | bytes 13662208 | tf_op jit(solution)/shard_map/dot_general | solution.py:535
  146.7 11.6 %attend.1 = (bf16[1024,512]{1,0:T(8,128)(2,1)}, f32[32,128]{1,0:T(8,128)}) custom-call(f32[8]{0:T(128)} %exponential_multiply_fusion.slope_ref, f32[256,256]{1,0:T(8,128)} %convert_select_fusion.distance_ref, bf16[1024,1536]{1,0:T(8,128)(2,1)} %add_convert_fusion.qkv_ref), custom_call_target="tpu_custom_call" | custom-call | flops 536870912 | bytes 4194304 | tf_op jit(solution)/shard_map/attend/pallas_call | solution.py:472
  158.2 6.3 convolution_convert_fusion.5.partial_ref
  164.5 73.1 %shard_map.271 = (bf16[1024,2048]{1,0:T(8,128)(2,1)}, f32[256,2048]{1,0:T(8,128)S(1)}) custom-call(bf16[1024,2048]{1,0:T(8,128)(2,1)} %convolution_convert_fusion.5.partial_ref, bf16[256,2048]{1,0:T(8,128)(2,1)S(1)} %copy-done, f32[3,2048]{1,0:T(4,128)S(1)} %pad_maximum_fusion.params_ref), custom_call_target="tpu_custom_call" | custom-call | flops 2097152 | bytes 209715200 | tf_op jit(solution)/shard_map/pallas_call | solution.py:386
  237.6 11.4 %copy.42 = bf16[4,512,2048]{2,1,0:T(8,128)(2,1)} copy(bf16[4,512,2048]{2,0,1:T(4,128)(2,1)} %all-gather.9.cloned.1.call-done) | data formatting | bytes 16777216 | tf_op jit(solution)/shard_map/all_gather | solution.py:558
  249.1 16.7 %fusion.10 = (bf16[1024,2048]{1,0:T(8,128)(2,1)}, bf16[1024,2048]{1,0:T(8,128)(2,1)S(1)}) fusion(f32[2048]{0:T(1024)S(1)} %bitcast.88, bf16[1024,2048]{1,0:T(8,128)(2,1)} %get-tuple-element.49, bf16[2048,2048]{1,0:T(8,128)(2,1)} %bitcast.76), kind=kOutput, calls=%fused_computation.13 | convolution fusion | flops 8615100416 | bytes 20979712 | tf_op jit(solution)/shard_map/dot_general | solution.py:535
  267.8 11.9 %convolution_convert_fusion.2 = bf16[2048,2048]{1,0:T(8,128)(2,1)} fusion(bf16[1024,2048]{1,0:T(8,128)(2,1)S(1)} %get-tuple-element.51.active_ref, bf16[1024,2048]{1,0:T(8,128)(2,1)S(1)} %copy-done.25), kind=kOutput, calls=%fused_computation.20 | convolution fusion | flops 8594128896 | bytes 16777216 | tf_op jit(solution)/shard_map/dot_general | solution.py:421
  279.7 9.6 %all-gather.11.cloned.1.call-done.weight_ref = bf16[2048,2048]{1,0:T(8,128)(2,1)} async-done(((bf16[256,2048]{1,0:T(8,128)(2,1)}), bf16[2048,2048]{1,0:T(8,128)(2,1)}) %all-gather.11.cloned.1.call-update) | async-done | bytes 8388624 | tf_op jit(solution)/shard_map/all_gather | solution.py:559
  289.3 13.3 %convert_reduce_fusion.1 = (f32[2048]{0:T(1024)S(1)}, bf16[1024,2048]{1,0:T(8,128)(2,1)S(1)}) fusion(bf16[1024,2048]{1,0:T(8,128)(2,1)} %get-tuple-element.53, bf16[1024,2048]{1,0:T(8,128)(2,1)} %get-tuple-element.52, bf16[2048,2048]{1,0:T(8,128)(2,1)} %all-gather.11.cloned.1.call-done.weight_ref), kind=kOutput, calls=%fused_computation.14 | convolution fusion | flops 8600418304 | bytes 20979712 | tf_op jit(solution)/shard_map/dot_general | solution.py:417
  302.7 11.5 %convolution_convert_fusion.1 = bf16[2048,2048]{1,0:T(8,128)(2,1)} fusion(bf16[1024,2048]{1,0:T(8,128)(2,1)S(1)} %copy-done.26, bf16[1024,2048]{1,0:T(8,128)(2,1)S(1)} %get-tuple-element.54), kind=kOutput, calls=%fused_computation.19 | convolution fusion | flops 8594128896 | bytes 16777216 | tf_op jit(solution)/shard_map/dot_general | solution.py:421
  314.3 14.2 %convolution_convert_fusion.4.partial_ref = bf16[1024,2048]{1,0:T(8,128)(2,1)} fusion(bf16[1024,2048]{1,0:T(8,128)(2,1)} %copy-done.28, bf16[2048,2048]{1,0:T(8,128)(2,1)} %bitcast.77), kind=kOutput, calls=%fused_computation.23 | convolution fusion | flops 8592031744 | bytes 16777216 | tf_op jit(solution)/shard_map/dot_general | solution.py:417
  328.4 77.8 %shard_map.272 = (bf16[1024,2048]{1,0:T(8,128)(2,1)}, f32[256,2048]{1,0:T(8,128)S(1)}, f32[8,2048]{1,0:T(8,128)S(1)}, bf16[1024,2048]{1,0:T(8,128)(2,1)}) custom-call(bf16[1024,2048]{1,0:T(8,128)(2,1)} %convolution_convert_fusion.4.partial_ref, f32[256,2048]{1,0:T(8,128)S(1)} %get-tuple-element.55.hidden_ref, bf16[256,2048]{1,0:T(8,128)(2,1)S(1)} %copy-done.2, ...), custom_call_target="tpu_custom_call" | custom-call | flops 2097152 | bytes 209715200 | tf_op jit(solution)/shard_map/pallas_call | solution.py:386
  407.6 5.5 convolution_convert_fusion.7.grad_ref
  413.1 22.2 %attend_back.1 = bf16[1024,1536]{1,0:T(8,128)(2,1)} custom-call(f32[8]{0:T(128)} %exponential_multiply_fusion.slope_ref, f32[256,256]{1,0:T(8,128)} %convert_select_fusion.distance_ref, bf16[1024,1536]{1,0:T(8,128)(2,1)} %add_convert_fusion.qkv_ref, bf16[1024,512]{1,0:T(8,128)(2,1)} %convolution_convert_fusion.7.grad_ref), custom_call_target="tpu_custom_call" | custom-call | flops 1342177280 | bytes 7340032 | tf_op jit(solution)/shard_map/attend_back/pallas_call | solution.py:499
  435.3 12.0 %convolution_convert_fusion = bf16[2048,1536]{1,0:T(8,128)(2,1)} fusion(bf16[1024,1536]{1,0:T(8,128)(2,1)} %attend_back.1, bf16[1024,2048]{1,0:T(8,128)(2,1)} %get-tuple-element.46, f32[2048]{0:T(1024)S(1)} %add.114, f32[2048]{0:T(1024)S(1)} %mul.93, f32[1024]{0:T(1024)S(1)} %add_rsqrt_fusion, f32[1024]{0:T(1024)S(1)} %broadcast_multiply_fusion), kind=kOutput, calls=%fused_computation.18 | convolution fusion | flops 6458179584 | bytes 13656064 | tf_op jit(solution)/shard_map/dot_general | solution.py:421
  447.4 6.2 convolution_convert_fusion.6
  457.5 11.2 %convolution_convert_fusion.3.first_ref = bf16[1024,2048]{1,0:T(8,128)(2,1)} fusion(bf16[1024,1536]{1,0:T(8,128)(2,1)} %attend_back.1, bf16[2048,1536]{1,0:T(8,128)(2,1)} %bitcast.90), kind=kOutput, calls=%fused_computation.22 | convolution fusion | flops 6444548096 | bytes 13631488 | tf_op jit(solution)/shard_map/dot_general | solution.py:417
  473.0 81.9 %shard_map.273 = (bf16[256,2048]{1,0:T(8,128)(2,1)S(1)}, bf16[256,2048]{1,0:T(8,128)(2,1)S(1)}, f32[8,2048]{1,0:T(8,128)S(1)}) custom-call(bf16[1024,2048]{1,0:T(8,128)(2,1)} %convolution_convert_fusion.3.first_ref, bf16[1024,2048]{1,0:T(8,128)(2,1)} %get-tuple-element.59.output_ref, bf16[256,2048]{1,0:T(8,128)(2,1)S(1)} %copy-done, ...), custom_call_target="tpu_custom_call" | custom-call | flops 2097152 | bytes 209715200 | tf_op jit(solution)/shard_map/pallas_call | solution.py:386
  561.4 9.0 %collective-permute-done.1 = f32[13,2048]{1,0:T(8,128)S(1)} collective-permute-done((f32[13,2048]{1,0:T(8,128)S(1)}, f32[13,2048]{1,0:T(8,128)S(1)}, u32[]{:S(2)}, u32[]{:S(2)}) %collective-permute-start.1) | collective-permute-done | bytes 106528 | tf_op jit(solution)/shard_map/ppermute | solution.py:21
  575.3 10.0 %collective-permute-done.2 = f32[13,2048]{1,0:T(8,128)S(1)} collective-permute-done((f32[13,2048]{1,0:T(8,128)S(1)}, f32[13,2048]{1,0:T(8,128)S(1)}, u32[]{:S(2)}, u32[]{:S(2)}) %collective-permute-start.2) | collective-permute-done | bytes 106528 | tf_op jit(solution)/shard_map/ppermute | solution.py:21
  601.7 46.0 %reduce-scatter.11.cloned.1.call-done = bf16[256,2048]{1,0:T(8,128)(2,1)} async-done(((bf16[2048,2048]{1,0:T(8,128)(2,1)}), bf16[256,2048]{1,0:T(8,128)(2,1)}) %reduce-scatter.11.cloned.1.call-update) | async-done | bytes 1048592 | tf_op jit(solution)/shard_map/reduce_scatter | solution.py:617
  (174 shorter events, 62.0 us)
Async XLA Ops:
  7.2 21.2 %copy-start.11 = (bf16[64,8192]{1,0:T(8,128)(2,1)S(1)}, bf16[64,8192]{1,0:T(8,128)(2,1)}, u32[]{:S(2)}) copy-start(bf16[64,8192]{1,0:T(8,128)(2,1)} %param.24) | copy-start | bytes 3145732
  7.2 127.5 %all-gather.5.cloned.1.call-start = ((), (), s32[]{:S(2)}) async-start(), calls=%async_computation.8 | async-start | bytes 7077888 | tf_op jit(solution)/shard_map/all_gather | solution.py:555
  27.6 130.6 %all-gather.7.cloned.1.call-start = ((), (), s32[]{:S(2)}) async-start(), calls=%async_computation.9 | async-start | bytes 2359296 | tf_op jit(solution)/shard_map/all_gather | solution.py:552
  28.4 209.3 %all-gather.9.cloned.1.call-start = ((), (), s32[]{:S(2)}) async-start(), calls=%async_computation.10 | async-start | bytes 9437184 | tf_op jit(solution)/shard_map/all_gather | solution.py:558
  28.4 18.2 %copy-start.16 = (bf16[64]{0:T(256)(128)(2,1)S(1)}, bf16[64]{0:T(256)(128)(2,1)}, u32[]{:S(2)}) copy-start(bf16[64]{0:T(256)(128)(2,1)} %param.21) | copy-start | bytes 388
  28.5 19.8 %copy-start = (bf16[256,2048]{1,0:T(8,128)(2,1)S(1)}, bf16[256,2048]{1,0:T(8,128)(2,1)}, u32[]{:S(2)}) copy-start(bf16[256,2048]{1,0:T(8,128)(2,1)} %tokens_ref.3) | copy-start | bytes 3145732
  28.5 19.8 %copy-start.1 = (bf16[256,2048]{1,0:T(8,128)(2,1)S(1)}, bf16[256,2048]{1,0:T(8,128)(2,1)}, u32[]{:S(2)}) copy-start(bf16[256,2048]{1,0:T(8,128)(2,1)} %cotangent_ref.1) | copy-start | bytes 3145732
  46.0 243.4 %all-gather.11.cloned.1.call-start = ((), (), s32[]{:S(2)}) async-start(), calls=%async_computation.11 | async-start | bytes 9437184 | tf_op jit(solution)/shard_map/all_gather | solution.py:559
  46.5 422.2 %reduce-scatter.5.cloned.1.call-start = ((), (), s32[]{:S(2)}) async-start(), calls=%async_computation.12 | async-start | bytes 9437184 | tf_op jit(solution)/shard_map/reduce_scatter | solution.py:621
  249.1 18.8 %copy-start.25 = (bf16[1024,2048]{1,0:T(8,128)(2,1)S(1)}, bf16[1024,2048]{1,0:T(8,128)(2,1)}, u32[]{:S(2)}) copy-start(bf16[1024,2048]{1,0:T(8,128)(2,1)} %get-tuple-element.52) | copy-start | bytes 12582916
  314.2 257.3 %reduce-scatter.7.cloned.1.call-start = ((), (), s32[]{:S(2)}) async-start(), calls=%async_computation.13 | async-start | bytes 7077888 | tf_op jit(solution)/shard_map/reduce_scatter | solution.py:621
  328.4 79.1 %copy-start.27 = (bf16[512,2048]{1,0:T(8,128)(2,1)S(1)}, bf16[512,2048]{1,0:T(8,128)(2,1)}, u32[]{:S(2)}) copy-start(bf16[512,2048]{1,0:T(8,128)(2,1)} %all-gather.7.cloned.1.call-done) | copy-start | bytes 6291460
  447.3 139.6 %reduce-scatter.9.cloned.1.call-start = ((), (), s32[]{:S(2)}) async-start(), calls=%async_computation.14 | async-start | bytes 2359296 | tf_op jit(solution)/shard_map/reduce_scatter | solution.py:617
  453.6 194.1 %reduce-scatter.11.cloned.1.call-start = ((), (), s32[]{:S(2)}) async-start(), calls=%async_computation.15 | async-start | bytes 9437184 | tf_op jit(solution)/shard_map/reduce_scatter | solution.py:617
  468.7 88.2 %all-to-all-start.3 = ((bf16[4,64,2048]{2,1,0:T(8,128)(2,1)}), bf16[4,64,2048]{2,1,0:T(8,128)(2,1)}, u32[]{:S(2)}, u32[]{:S(2)}) async-start(bf16[4,64,2048]{2,1,0:T(8,128)(2,1)} %reduce-scatter.5.cloned.1.call-done), calls=%async_computation.5 | async-start | bytes 2097152 | tf_op jit(solution)/shard_map/all_to_all | solution.py:624
  559.9 1.3 collective-permute-start
  561.3 9.1 %collective-permute-start.1 = (f32[13,2048]{1,0:T(8,128)S(1)}, f32[13,2048]{1,0:T(8,128)S(1)}, u32[]{:S(2)}, u32[]{:S(2)}) collective-permute-start(f32[13,2048]{1,0:T(8,128)S(1)} %maximum_select_fusion.4), channel_id=1, source_target_pairs={{0,2},{1,3},{2,0},{3,1},{4,6},{5,7},{6,4},{7,5},{8,10},{9,11},{10,... | collective-permute-start | bytes 319496 | tf_op jit(solution)/shard_map/ppermute | solution.py:21
  570.5 14.8 %collective-permute-start.2 = (f32[13,2048]{1,0:T(8,128)S(1)}, f32[13,2048]{1,0:T(8,128)S(1)}, u32[]{:S(2)}, u32[]{:S(2)}) collective-permute-start(f32[13,2048]{1,0:T(8,128)S(1)} %maximum_select_fusion.3), channel_id=1, source_target_pairs={{0,4},{1,5},{2,6},{3,7},{4,0},{5,1},{6,2},{7,3},{8,12},{9,13},{10,... | collective-permute-start | bytes 319496 | tf_op jit(solution)/shard_map/ppermute | solution.py:21
  571.5 20.5 %all-to-all-start.2 = ((bf16[4,64,1536]{2,1,0:T(8,128)(2,1)}), bf16[4,64,1536]{2,1,0:T(8,128)(2,1)S(1)}, u32[]{:S(2)}, u32[]{:S(2)}) async-start(bf16[4,64,1536]{2,1,0:T(8,128)(2,1)} %reduce-scatter.7.cloned.1.call-done), calls=%async_computation.4 | async-start | bytes 1572864 | tf_op jit(solution)/shard_map/all_to_all | solution.py:624
  585.4 5.0 collective-permute-start.3
  590.5 60.0 %collective-permute-start.4 = (f32[13,2048]{1,0:T(8,128)S(1)}, f32[13,2048]{1,0:T(8,128)S(1)}, u32[]{:S(2)}, u32[]{:S(2)}) collective-permute-start(f32[13,2048]{1,0:T(8,128)S(1)} %maximum_select_fusion.1), channel_id=1, source_target_pairs={{0,16},{8,24},{16,0},{24,8},{1,17},{9,25},{17,1},{25,9},{2,18},{10... | collective-permute-start | bytes 319496 | tf_op jit(solution)/shard_map/ppermute | solution.py:21
  598.3 52.4 %copy-start.10 = (bf16[64,6144]{1,0:T(8,128)(2,1)S(1)}, bf16[64,6144]{1,0:T(8,128)(2,1)}, u32[]{:S(2)}) copy-start(bf16[64,6144]{1,0:T(8,128)(2,1)} %param.17) | copy-start | bytes 2359300
  598.3 54.7 %copy-start.7 = (bf16[256,2048]{1,0:T(8,128)(2,1)S(1)}, bf16[256,2048]{1,0:T(8,128)(2,1)}, u32[]{:S(2)}) copy-start(bf16[256,2048]{1,0:T(8,128)(2,1)} %copy-done.6) | copy-start | bytes 3145732
  601.7 52.3 %copy-start.5 = (bf16[256,2048]{1,0:T(8,128)(2,1)S(1)}, bf16[256,2048]{1,0:T(8,128)(2,1)}, u32[]{:S(2)}) copy-start(bf16[256,2048]{1,0:T(8,128)(2,1)} %copy-done.4) | copy-start | bytes 3145732
  (20 other events, 201.7 us)
Sparse Core Ops, SparseCore 0:
  27.7 66.4 all-gather.4
  95.8 27.8 all-gather.6
  125.8 81.4 all-gather.8
  208.8 80.5 all-gather.10
  314.3 88.0 reduce-scatter.4
  447.4 67.2 reduce-scatter.6
  517.1 34.5 reduce-scatter.8
  554.0 93.6 reduce-scatter.10

commit v3 on v2

--- a/solution.py
+++ b/solution.py
@@ -83,15 +83,22 @@
 PATHS = ((1, 2), (2, 1))
 
 
-def flipped(axis, bit):
+def flipped(axis, mask):
     me = lax.axis_index(axis)
-    return {axis: me + bit - 2 * bit * ((me // bit) % 2)}
-
-
-def neighbours(fsdp=1):
+    there = me
+    for bit in bits_of(2 ** mask.bit_length()):
+        if mask & bit:
+            there = there + bit - 2 * bit * ((me // bit) % 2)
+    return {axis: there}
+
+
+def neighbours(fsdp=1, every=False):
     near = {bit: flipped("dp", bit) for bit in (1, 2)}
     partners = [near[1], near[2]] + [flipped("fsdp", bit) for bit in bits_of(fsdp)]
     greeted = partners if fsdp > 1 else [near[1], near[2]]
+    if every:
+        greeted = [flipped("dp", mask) for mask in (1, 2, 3)]
+        greeted += [flipped("fsdp", mask) for mask in range(1, fsdp)]
     barrier = pltpu.get_barrier_semaphore()
     for where in greeted:
         pl.semaphore_signal(barrier, inc=1, device_id=where, device_id_type=MESH_IDS)
@@ -341,12 +348,164 @@
     return jnp.where(row < a.shape[0] - 1, a + b, jnp.maximum(a, b))
 
 
+class LineSum:
+    def __init__(self, grad, merged, down, up, sems, size):
+        self.grad, self.merged, self.flows, self.sems = grad, merged, (down, up), sems
+        self.chips, self.chunks = size // 2, grad.shape[0]
+        place = lax.axis_index("fsdp")
+        self.chip, self.core = place // 2, place % 2
+        self.next = ({"fsdp": place - 2}, {"fsdp": place + 2})
+
+    def core_copy(self, piece):
+        return remote(
+            self.grad.at[:, piece * 2 + 1 - self.core], self.merged.at[piece], self.sems, piece,
+            flipped("fsdp", 1),
+        )
+
+    def begin(self):
+        for piece in range(self.chips):
+            self.core_copy(piece).start()
+
+    def each_chunk(self, act):
+        if self.chunks == 1:
+            return act(0)
+
+        def run(chunk, carry):
+            act(chunk)
+            return carry
+
+        return lax.fori_loop(0, self.chunks, run, 0)
+
+    def merge(self):
+        for piece in range(self.chips):
+            self.core_copy(piece).wait_recv()
+
+            def add(chunk, piece=piece):
+                self.merged[piece, chunk] = (
+                    self.merged[piece, chunk].astype(F32)
+                    + self.grad[chunk, piece * 2 + self.core].astype(F32)
+                ).astype(BF16)
+
+            self.each_chunk(add)
+
+    def hop(self, flow, step, chunk, source):
+        index = self.chips + (flow * (self.chips - 1) + step - 1) * self.chunks + chunk
+        return remote(
+            source, self.flows[flow].at[step - 1, chunk], self.sems, index, self.next[flow]
+        )
+
+    def landed(self, flow, step, chunk):
+        return self.hop(flow, step, chunk, self.flows[flow].at[step - 1, chunk])
+
+    def ends(self, flow):
+        return self.chip == (self.chips - 1, 0)[flow]
+
+    def receives(self, flow, step):
+        far = (self.chips - 1 - self.chip, self.chip)[flow]
+        return (far >= 1) & (far <= step)
+
+    def sends(self, flow, step):
+        far = (self.chips - 1 - self.chip, self.chip)[flow]
+        return far <= step - 1
+
+    def piece(self, flow, step):
+        return self.chip + (step - self.chips + 1, self.chips - 1 - step)[flow]
+
+    def open(self, step):
+        for flow in range(2):
+            piece = (step - 1, self.chips - step)[flow]
+
+            @pl.when(self.ends(flow))
+            def _(flow=flow, piece=piece):
+                self.each_chunk(
+                    lambda chunk: self.hop(
+                        flow, step, chunk, self.merged.at[piece, chunk]
+                    ).start()
+                )
+
+    def relay(self, step):
+        def one(chunk):
+            for flow in range(2):
+
+                @pl.when(self.receives(flow, step))
+                def _(flow=flow):
+                    self.landed(flow, step, chunk).wait_recv()
+                    held = self.flows[flow]
+                    held[step - 1, chunk] = (
+                        held[step - 1, chunk].astype(F32)
+                        + self.merged[self.piece(flow, step), chunk].astype(F32)
+                    ).astype(BF16)
+                    self.hop(flow, step + 1, chunk, held.at[step - 1, chunk]).start()
+
+        self.each_chunk(one)
+
+    def total(self, out, chunk):
+        step = self.chips - 1
+        out[chunk] = self.merged[self.chip, chunk].astype(F32)
+        for flow in range(2):
+
+            @pl.when(self.receives(flow, step))
+            def _(flow=flow):
+                self.landed(flow, step, chunk).wait_recv()
+                out[chunk] += self.flows[flow][step - 1, chunk].astype(F32)
+
+    def finish(self):
+        for piece in range(self.chips):
+            self.core_copy(piece).wait_send()
+        for flow in range(2):
+            for step in range(1, self.chips):
+
+                @pl.when(self.sends(flow, step))
+                def _(flow=flow, step=step):
+                    self.each_chunk(lambda chunk: self.landed(flow, step, chunk).wait_send())
+
+
+class Across:
+    def __init__(self, source, landing, sems):
+        self.source, self.landing, self.sems = source, landing, sems
+        self.me = lax.axis_index("dp")
+
+    def copy(self, chunk, slot):
+        return pltpu.make_async_remote_copy(
+            src_ref=self.source.at[chunk], dst_ref=self.landing.at[slot],
+            send_sem=self.sems.at[0, chunk], recv_sem=self.sems.at[1, slot],
+            device_id={"dp": chunk}, device_id_type=MESH_IDS,
+        )
+
+    def send(self, chunk):
+        @pl.when(self.me != chunk)
+        def _():
+            self.copy(chunk, self.me).start()
+
+        @pl.when(self.me == chunk)
+        def _():
+            self.landing[chunk] = self.source[chunk]
+
+    def receive(self, slot):
+        @pl.when(self.me != slot)
+        def _():
+            self.copy(slot, slot).wait_recv()
+
+    def finish(self, chunk):
+        @pl.when(self.me != chunk)
+        def _():
+            self.copy(chunk, self.me).wait_send()
+
+
 def last_kernel(
-    first_ref, output_ref, tokens_ref, hidden_ref, grad_ref, params_ref, tokens_out, output_out,
-    sums_out, landing, passing, last, sems,
+    fsdp, first_ref, output_ref, tokens_ref, hidden_ref, grad_ref, params_ref, small_ref, qkv_ref,
+    out_ref, up_ref, tokens_out, output_out, small_out, qkv_out, out_out, up_out, landing,
+    passing, last, held, small_landing, sums, qkv_merged, qkv_down, qkv_up, out_merged, out_down,
+    out_up, qkv_total, qkv_low, qkv_in, up_in, qkv_sems, out_sems, across_sems, sems, small_sems,
 ):
-    near, _ = neighbours()
-    sums_out[...] = jnp.zeros_like(sums_out)
+    near, partners = neighbours(fsdp, True)
+    dp, part = qkv_ref.shape[0], qkv_ref.shape[3] // 3
+    lines = (
+        LineSum(qkv_ref, qkv_merged, qkv_down, qkv_up, qkv_sems, fsdp),
+        LineSum(out_ref, out_merged, out_down, out_up, out_sems, fsdp),
+    )
+    up_across = Across(up_ref, up_in, across_sems.at[0])
+    qkv_across = Across(qkv_low, qkv_in, across_sems.at[1])
     first, second = (
         Scatter(ref, landing.at[k], passing.at[k], last.at[k], sems.at[k], near)
         for k, ref in enumerate((first_ref, output_ref))
@@ -358,21 +517,62 @@
         normed, inverse_std = row_norm(tokens_ref[rows].astype(F32))
         grad = grad_ref[rows] + row_back(total, normed, inverse_std, params_ref[0:1])
         tokens_out[rows] = grad.astype(BF16)
-        add_sums(sums_out, (total * normed, total))
+        add_sums(sums, (total * normed, total), 2)
 
     def second_rows(path, step):
         rows = second.own(path, step)
         total = second.total(path, step)
         output_out[rows] = (hidden_ref[rows] + total + params_ref[1:2]).astype(BF16)
 
+    for line in lines:
+        line.begin()
     for job in (first, second):
         each_step(lambda step, job=job: [job.begin(path, step) for path in range(2)])
-    for job in (first, second):
-        each_step(lambda step, job=job: [job.relay(path, step) for path in range(2)])
+    for chunk in range(dp):
+        up_across.send(chunk)
+    sums[...] = jnp.zeros_like(sums)
+    for line in lines:
+        line.merge()
+    for step in range(1, fsdp // 2):
+        for line in lines:
+            line.open(step)
+    each_step(lambda step: [first.relay(path, step) for path in range(2)])
+    for line in lines:
+        line.relay(1)
+    each_step(lambda step: [second.relay(path, step) for path in range(2)])
+    for step in range(2, fsdp // 2 - 1):
+        for line in lines:
+            line.relay(step)
     each_step(lambda step: [first_rows(path, step) for path in range(2)])
     each_step(lambda step: [second_rows(path, step) for path in range(2)])
+    held[0, :8] = small_ref[:8]
+    held[0, 8:] = small_ref[8:] + sums[...]
+    double_all(held, small_landing, small_sems, partners, sum_or_top, range(2))
+    for chunk in range(dp):
+        lines[0].total(qkv_total, chunk)
+        qkv_low[chunk] = qkv_total[chunk].astype(BF16)
+        qkv_across.send(chunk)
+    lines[1].total(out_out, 0)
+    double_all(held, small_landing, small_sems, partners, sum_or_top, range(2, len(partners)))
+    small_out[...] = held[len(partners)]
+    columns = up_ref.shape[2]
+    for slot in range(dp):
+        up_across.receive(slot)
+        up_out[:, slot * columns : (slot + 1) * columns] = up_in[slot].astype(F32)
+    for slot in range(dp):
+        qkv_across.receive(slot)
+        for third in range(3):
+            start = (third * dp + slot) * part
+            qkv_out[:, start : start + part] = qkv_in[
+                slot, :, third * part : (third + 1) * part
+            ].astype(F32)
     for job in (first, second):
         each_step(lambda step, job=job: [job.finish(path, step) for path in range(2)])
+    for line in lines:
+        line.finish()
+    for chunk in range(dp):
+        up_across.finish(chunk)
+        qkv_across.finish(chunk)
 
 
 def call_exchange(kernel, number, jobs, scatters, outs, args, extra=(), stages=0, unplaced=0):
@@ -396,7 +596,7 @@
             *([pltpu.SemaphoreType.DMA(stages)] if stages else []),
         ],
         compiler_params=pltpu.CompilerParams(
-            collective_id=number, has_side_effects=True, vmem_limit_bytes=48 << 20
+            collective_id=number, has_side_effects=True, vmem_limit_bytes=60 << 20
         ),
         cost_estimate=pl.CostEstimate(
             flops=rows * width, bytes_accessed=200 << 20, transcendentals=0
@@ -565,7 +765,7 @@
     table = lax.dynamic_update_slice(table, row, (rank, 0))
     wide = (4 * length, width)
     narrow = (length, width)
-    kernels = dp == 4 and length % (32 * STEPS) == 0 and ff == dp * width
+    kernels = dp == 4 and fsdp == 8 and length % (32 * STEPS) == 0 and ff == dp * width
     stages = len(bits_of(fsdp)) + 2
     if kernels:
         all_tokens, grad_y, table = call_exchange(
@@ -659,12 +859,13 @@
     grad_proj = attend_back(slopes, distance, qkv, grad_mixed, length)
     local_qkv = dot_tn(first_in, grad_proj).astype(BF16)
     late_branch, late_proj, _ = lax.optimization_barrier((branch_all, grad_proj, local_qkv))
-    grad_w_qkv = exchange_columns(reduce_columns(local_qkv))
-    grad_w_qkv = (
-        grad_w_qkv.reshape(shard, dp, 3, part).transpose(0, 2, 1, 3).reshape(shard, 3 * width)
-    )
     local_out = dot_tn(mixed, late_branch).astype(BF16)
-    grad_w_out = reduce_rows(local_out)
+    if not kernels:
+        grad_w_qkv = exchange_columns(reduce_columns(local_qkv))
+        grad_w_qkv = (
+            grad_w_qkv.reshape(shard, dp, 3, part).transpose(0, 2, 1, 3).reshape(shard, 3 * width)
+        )
+        grad_w_out = reduce_rows(local_out)
     first_part = dot_nt(late_proj, qkv_w).astype(BF16)
     if not kernels:
         output_part = dot(active, down_w).astype(BF16)
@@ -678,25 +879,53 @@
     q_sum = jnp.sum(grad_proj[:, :part].astype(F32), axis=0)
     v_sum = jnp.sum(grad_proj[:, 2 * part :].astype(F32), axis=0)
     if kernels:
-        first_part, scattered_up = lax.optimization_barrier((first_part, scattered_up))
-        grad_tokens, output, sums = call_exchange(
-            last_kernel, 4, 2, 2, [(narrow, BF16), (narrow, BF16), ((8, width), F32)],
+        small = jnp.concatenate([
+            branch_sums[:4].reshape(4 * width), spread(up_sum, ff), spread(q_sum, width),
+            spread(v_sum, width), jnp.zeros((5 * width,), F32), spread(tops, width, -1e30),
+        ]).reshape(-1, width)
+
+        def room(grad):
+            chips, piece = fsdp // 2, (grad.shape[0],) + grad.shape[2:]
+            return tuple(
+                pltpu.VMEM((count,) + piece, BF16) for count in (chips, chips - 1, chips - 1)
+            )
+
+        def line_sems(grad):
+            chips = fsdp // 2
+            return pltpu.SemaphoreType.DMA((2, chips + 2 * (chips - 1) * grad.shape[0]))
+
+        qkv_grad = local_qkv.reshape(dp, fsdp, shard, 3 * part)
+        out_grad = local_out.reshape(1, fsdp, shard, width)
+        grad_tokens, output, small, grad_w_qkv, grad_w_out, grad_w_up = call_exchange(
+            functools.partial(last_kernel, fsdp), 4, 2, 2,
+            [(narrow, BF16), (narrow, BF16), (small.shape, F32), (w_qkv.shape, F32),
+             ((1, shard, width), F32), (w_up.shape, F32)],
             [first_part, output_part, tokens, hidden, grad_hidden,
-             jnp.concatenate([gain1, down_b], 0)],
-        )
+             jnp.concatenate([gain1, down_b], 0), small, qkv_grad, out_grad,
+             scattered_up.reshape(dp, shard, ff_part)],
+            (
+                pltpu.VMEM((stages + 1,) + small.shape, F32),
+                pltpu.VMEM((stages,) + small.shape, F32), pltpu.VMEM((8, width), F32),
+                *room(qkv_grad), *room(out_grad),
+                pltpu.VMEM((dp, shard, 3 * part), F32), pltpu.VMEM((dp, shard, 3 * part), BF16),
+                pltpu.VMEM((dp, shard, 3 * part), BF16), pltpu.VMEM((dp, shard, ff_part), BF16),
+                line_sems(qkv_grad), line_sems(out_grad), pltpu.SemaphoreType.DMA((2, 2, dp)),
+            ),
+            (2, stages),
+        )
+        grad_w_out = grad_w_out[0]
     else:
         grad_first = scatter_dp(first_part, dp)
         normed1, inverse1 = norm_stats(inputs)
         grad_tokens = grad_hidden + norm_back(grad_first, normed1, inverse1, gain1)
         output = hidden + scatter_dp(output_part, dp) + down_b
-        sums = jnp.stack([jnp.sum(grad_first * normed1, axis=0), jnp.sum(grad_first, axis=0)])
-    small = jnp.concatenate([
-        branch_sums[:4].reshape(4 * width), spread(up_sum, ff), spread(q_sum, width),
-        spread(v_sum, width), sums[:2].reshape(2 * width), spread(tops, width, -1e30),
-    ]).reshape(-1, width)
-    grad_w_up = exchange_columns(scattered_up)
-    small, grad_w_up = lax.optimization_barrier((small, grad_w_up))
-    small = combine_all(small, both, sum_or_top)
+        sums = (jnp.sum(grad_first * normed1, axis=0), jnp.sum(grad_first, axis=0))
+        small = jnp.concatenate([
+            branch_sums[:4].reshape(4 * width), spread(up_sum, ff), spread(q_sum, width),
+            spread(v_sum, width), *sums, jnp.zeros((3 * width,), F32), spread(tops, width, -1e30),
+        ]).reshape(-1, width)
+        grad_w_up = exchange_columns(scattered_up)
+        small = combine_all(small, both, sum_or_top)
     ups_at = 4 + ff // width
     owned = lax.dynamic_slice(small, (0, rank * shard), (small.shape[0], shard))
     ff_shard = ff // (dp * fsdp)

time: 666 us -> 613 us (0.920)
  waiting for transfers between devices: 79.8 us -> 6.98 us
  Pallas kernels: 346 us -> 386 us
  starting transfers between devices: 12.5 us -> 0.24 us
    reduce_scatter x2 -> x1, waiting for transfers between devices: 46 us -> 0.01 us  [reduce_rows(): lax.psum_scatter(grad, 'fsdp', scatter_dimension=0, tiled=True).astype(F32)]
    pallas_call x4, Pallas kernels: 313 us -> 352 us  [call_exchange(): pl.pallas_call(kernel, in_specs=[pl.BlockSpec(memory_space=pltpu.VMEM)] *...]
    ppermute x5 -> x0, waiting for transfers between devices: 22.1 us -> none  [swap(): return lax.ppermute(value, axis, [(i, i ^ bit) for i in range(size)])]
    reshape x3 -> x0, local copies, waits for them, and re-layouts: 8.35 us -> none  [layer(): grad_w_qkv.reshape(shard, dp, 3, part).transpose(0, 2, 1, 3)]
    all_to_all x2 -> x0, starting transfers between devices: 7.99 us -> none  [exchange_columns(): lax.all_to_all(grad.reshape(dp * shard, grad.shape[2]), 'dp', 0, 1, tiled...]
  transfers between devices with their start and end apart: 15 -> 6, of which waited for: 6 -> 1; matrix products, arithmetic and copies ran while one was open for 21% -> 21% of each run, Pallas kernels for 52% -> 63%
where the time goes in v3:
time: 613 us; the launch traced here: 609 us
  Pallas kernels  386 us (63%)
  matrix products  122 us (20%)
  local copies, waits for them, and re-layouts  34.3 us (6%)
  blocking collectives  31.8 us (5%)
  between operations  14.8 us (2%)
  other arithmetic  13.7 us (2%)
  waiting for transfers between devices  6.98 us (1%)
    pallas_call x4, Pallas kernels, call_exchange(): pl.pallas_call(kernel, in_specs=[pl.BlockSpec(memory_space=pltpu.VMEM)] *...  352 us
    dot_general x4, matrix products, dot_nt(): lax.dot_general(a, b, (((1,), (1,)), ((), ())), preferred_element_type=F32)  44.7 us
    dot_general x4, matrix products, dot_tn(): lax.dot_general(a, b, (((0,), (0,)), ((), ())), preferred_element_type=F32)  42.1 us
    dot_general x3, matrix products, dot(): return jnp.dot(a, b, preferred_element_type=F32)  34.9 us
    pallas_call x1, Pallas kernels, attend_back(): pl.pallas_call(attend_back_kernel, grid=(rows // length,), in_specs=[pl.B...  22.2 us
    all_to_all x1, blocking collectives, layer(): lax.all_to_all(cols, 'dp', 1, 0, tiled=True).reshape(dp, shard, 3 * part)  16.4 us
    all_to_all x1, blocking collectives, layer(): lax.all_to_all(w_up, 'dp', 1, 0, tiled=True).reshape(dp, shard, ff_part)  15.4 us
  transfers between devices with their start and end apart: 6, of which 1 were waited for; matrix products, arithmetic and copies ran while one was open for 21% of the time, Pallas kernels for 63%

profile of v3, /device:TPU:0, one launch (start us, length us, event | category | flops | bytes accessed | tf_op | source)
XLA Modules:
  0.0 609.1 jit_solution(8444170606936555168)
XLA Ops:
  11.2 16.4 %all_to_all.32 = bf16[64,4,1536]{2,0,1:T(8,128)(2,1)} all-to-all(bf16[64,4,1536]{2,0,1:T(8,128)(2,1)S(1)} %all_to_all.24), channel_id=1, replica_groups=mesh['dp'=4,'fsdp'=8] {'dp'}, dimensions={1} | all-to-all | bytes 1572864 | tf_op jit(solution)/shard_map/all_to_all | solution.py:754
  28.6 15.4 %all_to_all.33 = bf16[64,4,2048]{2,0,1:T(8,128)(2,1)S(1)} all-to-all(bf16[64,4,2048]{2,0,1:T(8,128)(2,1)S(1)} %bitcast.70), channel_id=1, replica_groups=mesh['dp'=4,'fsdp'=8] {'dp'}, dimensions={1} | all-to-all | bytes 2097152 | tf_op jit(solution)/shard_map/all_to_all | solution.py:757
  48.2 81.4 %shard_map.270 = (bf16[1024,2048]{1,0:T(8,128)(2,1)}, bf16[1024,2048]{1,0:T(8,128)(2,1)}, bf16[32,768]{1,0:T(8,128)(2,1)}) custom-call(bf16[256,2048]{1,0:T(8,128)(2,1)} %tokens_ref.3, bf16[256,2048]{1,0:T(8,128)(2,1)} %cotangent_ref.1, bf16[32,768]{1,0:T(8,128)(2,1)} %copy-done.9), custom_call_target="tpu_custom_call" | custom-call | flops 2097152 | bytes 209715200 | tf_op jit(solution)/shard_map/pallas_call | solution.py:586
  132.6 3.6 convert_reduce_fusion
  138.9 11.9 %add_convert_fusion.qkv_ref = bf16[1024,1536]{1,0:T(8,128)(2,1)} fusion(bf16[2048,1536]{1,0:T(8,128)(2,1)} %bitcast.78, f32[1536]{0:T(1024)S(1)} %fusion.13, bf16[1024,2048]{1,0:T(8,128)(2,1)} %get-tuple-element.45, f32[2048]{0:T(1024)S(1)} %add.95, f32[2048]{0:T(1024)S(1)} %mul.93, f32[1024]{0:T(1024)S(1)} %add_rsqrt_fusion, ...), kind=kOutput, calls=%fused_computation.21 | convolution fusion | flops 6458179584 | bytes 13662208 | tf_op jit(solution)/shard_map/dot_general | solution.py:735
  150.7 11.6 %attend.1 = (bf16[1024,512]{1,0:T(8,128)(2,1)}, f32[32,128]{1,0:T(8,128)}) custom-call(f32[8]{0:T(128)} %exponential_multiply_fusion.slope_ref, f32[256,256]{1,0:T(8,128)} %convert_select_fusion.distance_ref, bf16[1024,1536]{1,0:T(8,128)(2,1)} %add_convert_fusion.qkv_ref), custom_call_target="tpu_custom_call" | custom-call | flops 536870912 | bytes 4194304 | tf_op jit(solution)/shard_map/attend/pallas_call | solution.py:672
  162.3 6.3 %convolution_convert_fusion.5.partial_ref = bf16[1024,2048]{1,0:T(8,128)(2,1)} fusion(bf16[1024,512]{1,0:T(8,128)(2,1)} %get-tuple-element.47, bf16[512,2048]{1,0:T(8,128)(2,1)} %all-gather.7.cloned.1.call-done), kind=kOutput, calls=%fused_computation.24 | convolution fusion | flops 2149580800 | bytes 7340032 | tf_op jit(solution)/shard_map/dot_general | solution.py:735
  168.6 73.5 %shard_map.271 = (bf16[1024,2048]{1,0:T(8,128)(2,1)}, f32[256,2048]{1,0:T(8,128)}) custom-call(bf16[1024,2048]{1,0:T(8,128)(2,1)} %convolution_convert_fusion.5.partial_ref, bf16[256,2048]{1,0:T(8,128)(2,1)} %tokens_ref.3, f32[3,2048]{1,0:T(4,128)} %pad_maximum_fusion.params_ref), custom_call_target="tpu_custom_call" | custom-call | flops 2097152 | bytes 209715200 | tf_op jit(solution)/shard_map/pallas_call | solution.py:586
  242.1 11.3 %copy.37 = bf16[4,512,2048]{2,1,0:T(8,128)(2,1)} copy(bf16[4,512,2048]{2,0,1:T(4,128)(2,1)} %all-gather.9.cloned.1.call-done) | data formatting | bytes 16777216 | tf_op jit(solution)/shard_map/all_gather | solution.py:758
  253.5 16.7 %fusion.10 = (bf16[1024,2048]{1,0:T(8,128)(2,1)}, bf16[1024,2048]{1,0:T(8,128)(2,1)S(1)}) fusion(f32[2048]{0:T(1024)S(1)} %bitcast.77, bf16[1024,2048]{1,0:T(8,128)(2,1)} %get-tuple-element.48, bf16[2048,2048]{1,0:T(8,128)(2,1)} %bitcast.65), kind=kOutput, calls=%fused_computation.13 | convolution fusion | flops 8615100416 | bytes 20979712 | tf_op jit(solution)/shard_map/dot_general | solution.py:735
  272.2 11.9 %convolution_convert_fusion.2 = bf16[2048,2048]{1,0:T(8,128)(2,1)} fusion(bf16[1024,2048]{1,0:T(8,128)(2,1)S(1)} %get-tuple-element.50.active_ref, bf16[1024,2048]{1,0:T(8,128)(2,1)S(1)} %copy-done.21), kind=kOutput, calls=%fused_computation.20 | convolution fusion | flops 8594128896 | bytes 16777216 | tf_op jit(solution)/shard_map/dot_general | solution.py:621
  284.1 5.2 all-gather.11.cloned.1.call-done.weight_ref
  289.3 13.3 %convert_reduce_fusion.1 = (f32[2048]{0:T(1024)S(1)}, bf16[1024,2048]{1,0:T(8,128)(2,1)S(1)}) fusion(bf16[1024,2048]{1,0:T(8,128)(2,1)} %get-tuple-element.52, bf16[1024,2048]{1,0:T(8,128)(2,1)} %get-tuple-element.51, bf16[2048,2048]{1,0:T(8,128)(2,1)} %all-gather.11.cloned.1.call-done.weight_ref), kind=kOutput, calls=%fused_computation.14 | convolution fusion | flops 8600418304 | bytes 20979712 | tf_op jit(solution)/shard_map/dot_general | solution.py:617
  302.6 11.5 %convolution_convert_fusion.1 = bf16[2048,2048]{1,0:T(8,128)(2,1)} fusion(bf16[1024,2048]{1,0:T(8,128)(2,1)S(1)} %copy-done.22, bf16[1024,2048]{1,0:T(8,128)(2,1)S(1)} %get-tuple-element.53), kind=kOutput, calls=%fused_computation.19 | convolution fusion | flops 8594128896 | bytes 16777216 | tf_op jit(solution)/shard_map/dot_general | solution.py:621
  316.3 14.8 %convolution_convert_fusion.4.partial_ref = bf16[1024,2048]{1,0:T(8,128)(2,1)} fusion(bf16[1024,2048]{1,0:T(8,128)(2,1)} %copy-done.24, bf16[2048,2048]{1,0:T(8,128)(2,1)} %bitcast.66), kind=kOutput, calls=%fused_computation.23 | convolution fusion | flops 8592031744 | bytes 16777216 | tf_op jit(solution)/shard_map/dot_general | solution.py:617
  331.2 79.5 %shard_map.272 = (bf16[1024,2048]{1,0:T(8,128)(2,1)}, f32[256,2048]{1,0:T(8,128)}, f32[8,2048]{1,0:T(8,128)}, bf16[1024,2048]{1,0:T(8,128)(2,1)}) custom-call(bf16[1024,2048]{1,0:T(8,128)(2,1)} %convolution_convert_fusion.4.partial_ref, f32[256,2048]{1,0:T(8,128)} %get-tuple-element.54.hidden_ref, bf16[256,2048]{1,0:T(8,128)(2,1)} %cotangent_ref.1, ...), custom_call_target="tpu_custom_call" | custom-call | flops 2097152 | bytes 209715200 | tf_op jit(solution)/shard_map/pallas_call | solution.py:586
  410.6 5.5 convolution_convert_fusion.7.grad_ref
  416.2 22.2 %attend_back.1 = bf16[1024,1536]{1,0:T(8,128)(2,1)} custom-call(f32[8]{0:T(128)} %exponential_multiply_fusion.slope_ref, f32[256,256]{1,0:T(8,128)} %convert_select_fusion.distance_ref, bf16[1024,1536]{1,0:T(8,128)(2,1)} %add_convert_fusion.qkv_ref, bf16[1024,512]{1,0:T(8,128)(2,1)} %convolution_convert_fusion.7.grad_ref), custom_call_target="tpu_custom_call" | custom-call | flops 1342177280 | bytes 7340032 | tf_op jit(solution)/shard_map/attend_back/pallas_call | solution.py:699
  438.4 12.4 %convolution_convert_fusion = bf16[2048,1536]{1,0:T(8,128)(2,1)} fusion(bf16[1024,1536]{1,0:T(8,128)(2,1)} %attend_back.1, bf16[1024,2048]{1,0:T(8,128)(2,1)} %get-tuple-element.45, f32[2048]{0:T(1024)S(1)} %add.95, f32[2048]{0:T(1024)S(1)} %mul.93, f32[1024]{0:T(1024)S(1)} %add_rsqrt_fusion, f32[1024]{0:T(1024)S(1)} %broadcast_multiply_fusion), kind=kOutput, calls=%fused_computation.18 | convolution fusion | flops 6458179584 | bytes 13656064 | tf_op jit(solution)/shard_map/dot_general | solution.py:621
  452.8 6.2 %convolution_convert_fusion.6 = bf16[512,2048]{1,0:T(8,128)(2,1)} fusion(bf16[1024,512]{1,0:T(8,128)(2,1)} %get-tuple-element.47, bf16[1024,2048]{1,0:T(8,128)(2,1)} %get-tuple-element.61), kind=kOutput, calls=%fused_computation.25 | convolution fusion | flops 2148532224 | bytes 7340032 | tf_op jit(solution)/shard_map/dot_general | solution.py:621
  459.1 11.0 %convolution_convert_fusion.3.first_ref = bf16[1024,2048]{1,0:T(8,128)(2,1)} fusion(bf16[1024,1536]{1,0:T(8,128)(2,1)S(1)} %copy-done.1, bf16[2048,1536]{1,0:T(8,128)(2,1)} %bitcast.79), kind=kOutput, calls=%fused_computation.22 | convolution fusion | flops 6444548096 | bytes 13631488 | tf_op jit(solution)/shard_map/dot_general | solution.py:617
  470.1 117.5 %shard_map.273 = (bf16[256,2048]{1,0:T(8,128)(2,1)}, bf16[256,2048]{1,0:T(8,128)(2,1)}, f32[16,2048]{1,0:T(8,128)}, f32[64,6144]{1,0:T(8,128)}, f32[1,64,2048]{2,1,0:T(8,128)}, /*index=5*/f32[64,8192]{1,0:T(8,128)}) custom-call(bf16[1024,2048]{1,0:T(8,128)(2,1)} %convolution_convert_fusion.3.first_ref, bf16[1024,2048]{1,0:T(8,128)(2,1)} %get-tuple-element.57.output_ref, ...), custom_call_target="tpu_custom_call" | custom-call | flops 2097152 | bytes 209715200 | tf_op jit(solution)/shard_map/pallas_call | solution.py:586
  592.5 2.8 convert_element_type.95
  595.3 2.5 copy.61
  (134 shorter events, 29.9 us)
Async XLA Ops:
  7.2 21.2 %copy-start.6 = (bf16[64,8192]{1,0:T(8,128)(2,1)S(1)}, bf16[64,8192]{1,0:T(8,128)(2,1)}, u32[]{:S(2)}) copy-start(bf16[64,8192]{1,0:T(8,128)(2,1)} %param.24) | copy-start | bytes 3145732
  7.2 131.7 %all-gather.5.cloned.1.call-start = ((), (), s32[]{:S(2)}) async-start(), calls=%async_computation.4 | async-start | bytes 7077888 | tf_op jit(solution)/shard_map/all_gather | solution.py:755
  27.6 134.7 %all-gather.7.cloned.1.call-start = ((), (), s32[]{:S(2)}) async-start(), calls=%async_computation.5 | async-start | bytes 2359296 | tf_op jit(solution)/shard_map/all_gather | solution.py:752
  28.4 213.8 %all-gather.9.cloned.1.call-start = ((), (), s32[]{:S(2)}) async-start(), calls=%async_computation.6 | async-start | bytes 9437184 | tf_op jit(solution)/shard_map/all_gather | solution.py:758
  28.4 18.0 %copy-start.12 = (bf16[64]{0:T(256)(128)(2,1)S(1)}, bf16[64]{0:T(256)(128)(2,1)}, u32[]{:S(2)}) copy-start(bf16[64]{0:T(256)(128)(2,1)} %param.21) | copy-start | bytes 388
  28.4 18.0 %copy-start.13 = (bf16[64]{0:T(256)(128)(2,1)S(1)}, bf16[64]{0:T(256)(128)(2,1)}, u32[]{:S(2)}) copy-start(bf16[64]{0:T(256)(128)(2,1)} %param.22) | copy-start | bytes 388
  28.4 18.0 %copy-start.14 = (bf16[64]{0:T(256)(128)(2,1)S(1)}, bf16[64]{0:T(256)(128)(2,1)}, u32[]{:S(2)}) copy-start(bf16[64]{0:T(256)(128)(2,1)} %param.23) | copy-start | bytes 388
  28.5 18.0 %copy-start.15 = (bf16[64]{0:T(256)(128)(2,1)S(1)}, bf16[64]{0:T(256)(128)(2,1)}, u32[]{:S(2)}) copy-start(bf16[64]{0:T(256)(128)(2,1)} %param.27) | copy-start | bytes 388
  28.5 18.0 %copy-start.16 = (bf16[64]{0:T(256)(128)(2,1)S(1)}, bf16[64]{0:T(256)(128)(2,1)}, u32[]{:S(2)}) copy-start(bf16[64]{0:T(256)(128)(2,1)} %param.28) | copy-start | bytes 388
  28.5 18.0 %copy-start.17 = (bf16[64]{0:T(256)(128)(2,1)S(1)}, bf16[64]{0:T(256)(128)(2,1)}, u32[]{:S(2)}) copy-start(bf16[64]{0:T(256)(128)(2,1)} %param.29) | copy-start | bytes 388
  28.5 18.0 %copy-start.18 = (bf16[64]{0:T(256)(128)(2,1)S(1)}, bf16[64]{0:T(256)(128)(2,1)}, u32[]{:S(2)}) copy-start(bf16[64]{0:T(256)(128)(2,1)} %param.18) | copy-start | bytes 388
  28.5 18.0 %copy-start.19 = (bf16[64]{0:T(256)(128)(2,1)S(1)}, bf16[64]{0:T(256)(128)(2,1)}, u32[]{:S(2)}) copy-start(bf16[64]{0:T(256)(128)(2,1)} %param.19) | copy-start | bytes 388
  28.5 18.0 %copy-start.20 = (bf16[256]{0:T(256)(128)(2,1)S(1)}, bf16[256]{0:T(256)(128)(2,1)}, u32[]{:S(2)}) copy-start(bf16[256]{0:T(256)(128)(2,1)} %param.25) | copy-start | bytes 1540
  45.8 243.5 %all-gather.11.cloned.1.call-start = ((), (), s32[]{:S(2)}) async-start(), calls=%async_computation.7 | async-start | bytes 9437184 | tf_op jit(solution)/shard_map/all_gather | solution.py:759
  46.4 423.7 %reduce-scatter.3.cloned.1.call-start = ((), (), s32[]{:S(2)}) async-start(), calls=%async_computation.8 | async-start | bytes 9437184 | tf_op jit(solution)/shard_map/reduce_scatter | solution.py:821
  253.5 18.7 %copy-start.21 = (bf16[1024,2048]{1,0:T(8,128)(2,1)S(1)}, bf16[1024,2048]{1,0:T(8,128)(2,1)}, u32[]{:S(2)}) copy-start(bf16[1024,2048]{1,0:T(8,128)(2,1)} %get-tuple-element.51) | copy-start | bytes 12582916
  289.3 13.4 %copy-start.22 = (bf16[1024,2048]{1,0:T(8,128)(2,1)S(1)}, bf16[1024,2048]{1,0:T(8,128)(2,1)}, u32[]{:S(2)}) copy-start(bf16[1024,2048]{1,0:T(8,128)(2,1)} %get-tuple-element.48) | copy-start | bytes 12582916
  302.6 11.5 %copy-start.24 = (bf16[1024,2048]{1,0:T(8,128)(2,1)}, bf16[1024,2048]{1,0:T(8,128)(2,1)S(1)}, u32[]{:S(2)}) copy-start(bf16[1024,2048]{1,0:T(8,128)(2,1)S(1)} %get-tuple-element.53) | copy-start | bytes 12582916
  314.2 278.3 %reduce-scatter.5.cloned.1.call-start = ((), (), s32[]{:S(2)}) async-start(), calls=%async_computation.9 | async-start | bytes 9437184 | tf_op jit(solution)/shard_map/reduce_scatter | solution.py:817
  331.2 79.5 %copy-start.23 = (bf16[512,2048]{1,0:T(8,128)(2,1)S(1)}, bf16[512,2048]{1,0:T(8,128)(2,1)}, u32[]{:S(2)}) copy-start(bf16[512,2048]{1,0:T(8,128)(2,1)} %all-gather.7.cloned.1.call-done) | copy-start | bytes 6291460
  438.4 12.4 %copy-start.10 = (f32[8,2048]{1,0:T(8,128)S(1)}, f32[8,2048]{1,0:T(8,128)}, u32[]{:S(2)}) copy-start(f32[8,2048]{1,0:T(8,128)} %get-tuple-element.59) | copy-start | bytes 196612
  438.4 12.5 %copy-start.1 = (bf16[1024,1536]{1,0:T(8,128)(2,1)S(1)}, bf16[1024,1536]{1,0:T(8,128)(2,1)}, u32[]{:S(2)}) copy-start(bf16[1024,1536]{1,0:T(8,128)(2,1)} %attend_back.1) | copy-start | bytes 9437188
  470.1 121.4 %copy-start.3 = (bf16[64,6144]{1,0:T(8,128)(2,1)S(1)}, bf16[64,6144]{1,0:T(8,128)(2,1)}, u32[]{:S(2)}) copy-start(bf16[64,6144]{1,0:T(8,128)(2,1)} %param.17) | copy-start | bytes 2359300
  587.6 10.2 %copy-start.7 = (bf16[256,2048]{1,0:T(8,128)(2,1)S(1)}, bf16[256,2048]{1,0:T(8,128)(2,1)}, u32[]{:S(2)}) copy-start(bf16[256,2048]{1,0:T(8,128)(2,1)} %get-tuple-element.107) | copy-start | bytes 3145732
  (7 other events, 26.9 us)
Sparse Core Ops, SparseCore 0:
  27.7 66.4 all-gather.4
  95.8 27.7 all-gather.6
  125.8 81.4 all-gather.8
  208.7 80.5 all-gather.10
  314.3 88.0 reduce-scatter.2
  404.5 88.9 reduce-scatter.4

commit v4 on v3

--- a/solution.py
+++ b/solution.py
@@ -229,13 +229,27 @@
     )
 
 
-def double_all(held, landing, sems, partners, join, stages=None):
-    for stage in stages or range(len(partners)):
-        where = partners[stage]
-        copy = remote(held.at[stage], landing.at[stage], sems, stage, where)
-        copy.start()
-        copy.wait()
-        held[stage + 1] = join(held[stage], landing[stage])
+class Doubling:
+    def __init__(self, held, landing, sems, partners, join):
+        self.held, self.landing, self.sems = held, landing, sems
+        self.partners, self.join = partners, join
+
+    def copy(self, stage):
+        return remote(
+            self.held.at[stage], self.landing.at[stage], self.sems, stage, self.partners[stage]
+        )
+
+    def start(self, stage):
+        self.copy(stage).start()
+
+    def end(self, stage):
+        self.copy(stage).wait()
+        self.held[stage + 1] = self.join(self.held[stage], self.landing[stage])
+
+    def run(self, *stages):
+        for stage in stages:
+            self.start(stage)
+            self.end(stage)
 
 
 def gather_two_kernel(
@@ -247,10 +261,11 @@
         out[: source.shape[0]] = source[...]
         jobs.append(Gather(out, sems.at[k], near))
     held[0] = table_ref[...]
-    double_all(held, landing, small_sems, partners, jnp.add, range(2))
+    small = Doubling(held, landing, small_sems, partners, jnp.add)
+    small.run(0, 1)
     for job in jobs:
         each_step(lambda step, job=job: [job.send(path, step) for path in range(2)])
-    double_all(held, landing, small_sems, partners, jnp.add, range(2, len(partners)))
+    small.run(*range(2, len(partners)))
     table_out[...] = held[len(partners)]
     for job in jobs:
         each_step(lambda step, job=job: [job.forward(path, step) for path in range(2)])
@@ -349,8 +364,9 @@
 
 
 class LineSum:
-    def __init__(self, grad, merged, down, up, sems, size):
+    def __init__(self, grad, own, merged, down, up, own_sems, sems, size):
         self.grad, self.merged, self.flows, self.sems = grad, merged, (down, up), sems
+        self.own, self.own_sems = own, own_sems
         self.chips, self.chunks = size // 2, grad.shape[0]
         place = lax.axis_index("fsdp")
         self.chip, self.core = place // 2, place % 2
@@ -362,9 +378,15 @@
             flipped("fsdp", 1),
         )
 
+    def own_copy(self, piece):
+        return pltpu.make_async_copy(
+            self.grad.at[:, piece * 2 + self.core], self.own.at[piece], self.own_sems.at[piece]
+        )
+
     def begin(self):
         for piece in range(self.chips):
             self.core_copy(piece).start()
+            self.own_copy(piece).start()
 
     def each_chunk(self, act):
         if self.chunks == 1:
@@ -379,11 +401,12 @@
     def merge(self):
         for piece in range(self.chips):
             self.core_copy(piece).wait_recv()
+            self.own_copy(piece).wait()
 
             def add(chunk, piece=piece):
                 self.merged[piece, chunk] = (
                     self.merged[piece, chunk].astype(F32)
-                    + self.grad[chunk, piece * 2 + self.core].astype(F32)
+                    + self.own[piece, chunk].astype(F32)
                 ).astype(BF16)
 
             self.each_chunk(add)
@@ -493,19 +516,30 @@
 
 
 def last_kernel(
-    fsdp, first_ref, output_ref, tokens_ref, hidden_ref, grad_ref, params_ref, small_ref, qkv_ref,
-    out_ref, up_ref, tokens_out, output_out, small_out, qkv_out, out_out, up_out, landing,
-    passing, last, held, small_landing, sums, qkv_merged, qkv_down, qkv_up, out_merged, out_down,
-    out_up, qkv_total, qkv_low, qkv_in, up_in, qkv_sems, out_sems, across_sems, sems, small_sems,
+    fsdp, first_ref, params_ref, small_ref, up_ref, output_any, tokens_any, hidden_any, grad_any,
+    qkv_ref, out_ref, tokens_out, output_out, small_out, qkv_out, out_out, up_out, landing,
+    passing, last, held, small_landing, sums, output_ref, tokens_ref, hidden_ref, grad_ref,
+    qkv_own, qkv_merged, qkv_down, qkv_up, out_own, out_merged, out_down, out_up, qkv_total,
+    qkv_low, qkv_in, up_in, copy_sems, qkv_own_sems, out_own_sems, qkv_sems, out_sems,
+    across_sems, sems, small_sems,
 ):
+    copies = [
+        pltpu.make_async_copy(source, target, copy_sems.at[k])
+        for k, (source, target) in enumerate((
+            (output_any, output_ref), (tokens_any, tokens_ref), (hidden_any, hidden_ref),
+            (grad_any, grad_ref),
+        ))
+    ]
     near, partners = neighbours(fsdp, True)
     dp, part = qkv_ref.shape[0], qkv_ref.shape[3] // 3
+    chips = fsdp // 2
     lines = (
-        LineSum(qkv_ref, qkv_merged, qkv_down, qkv_up, qkv_sems, fsdp),
-        LineSum(out_ref, out_merged, out_down, out_up, out_sems, fsdp),
+        LineSum(qkv_ref, qkv_own, qkv_merged, qkv_down, qkv_up, qkv_own_sems, qkv_sems, fsdp),
+        LineSum(out_ref, out_own, out_merged, out_down, out_up, out_own_sems, out_sems, fsdp),
     )
     up_across = Across(up_ref, up_in, across_sems.at[0])
     qkv_across = Across(qkv_low, qkv_in, across_sems.at[1])
+    small = Doubling(held, small_landing, small_sems, partners, sum_or_top)
     first, second = (
         Scatter(ref, landing.at[k], passing.at[k], last.at[k], sems.at[k], near)
         for k, ref in enumerate((first_ref, output_ref))
@@ -524,41 +558,56 @@
         total = second.total(path, step)
         output_out[rows] = (hidden_ref[rows] + total + params_ref[1:2]).astype(BF16)
 
+    def paths(act):
+        each_step(lambda step: [act(path, step) for path in range(2)])
+
+    paths(first.begin)
     for line in lines:
         line.begin()
-    for job in (first, second):
-        each_step(lambda step, job=job: [job.begin(path, step) for path in range(2)])
-    for chunk in range(dp):
-        up_across.send(chunk)
+    for copy in copies:
+        copy.start()
     sums[...] = jnp.zeros_like(sums)
     for line in lines:
         line.merge()
-    for step in range(1, fsdp // 2):
+    for step in range(1, chips):
         for line in lines:
             line.open(step)
-    each_step(lambda step: [first.relay(path, step) for path in range(2)])
+    for copy in copies:
+        copy.wait()
+    paths(first.relay)
+    paths(second.begin)
     for line in lines:
         line.relay(1)
-    each_step(lambda step: [second.relay(path, step) for path in range(2)])
-    for step in range(2, fsdp // 2 - 1):
+    paths(first_rows)
+    held[0, :8] = small_ref[:8]
+    held[0, 8:] = small_ref[8:] + sums[...]
+    small.start(0)
+    paths(second.relay)
+    small.end(0)
+    small.start(1)
+    for chunk in range(dp):
+        up_across.send(chunk)
+    for step in range(2, chips - 1):
         for line in lines:
             line.relay(step)
-    each_step(lambda step: [first_rows(path, step) for path in range(2)])
-    each_step(lambda step: [second_rows(path, step) for path in range(2)])
-    held[0, :8] = small_ref[:8]
-    held[0, 8:] = small_ref[8:] + sums[...]
-    double_all(held, small_landing, small_sems, partners, sum_or_top, range(2))
+    small.end(1)
+    small.start(2)
+    paths(second_rows)
+    small.end(2)
+    small.start(3)
     for chunk in range(dp):
         lines[0].total(qkv_total, chunk)
         qkv_low[chunk] = qkv_total[chunk].astype(BF16)
         qkv_across.send(chunk)
+    small.end(3)
+    small.start(4)
     lines[1].total(out_out, 0)
-    double_all(held, small_landing, small_sems, partners, sum_or_top, range(2, len(partners)))
-    small_out[...] = held[len(partners)]
     columns = up_ref.shape[2]
     for slot in range(dp):
         up_across.receive(slot)
         up_out[:, slot * columns : (slot + 1) * columns] = up_in[slot].astype(F32)
+    small.end(4)
+    small_out[...] = held[len(partners)]
     for slot in range(dp):
         qkv_across.receive(slot)
         for third in range(3):
@@ -566,8 +615,8 @@
             qkv_out[:, start : start + part] = qkv_in[
                 slot, :, third * part : (third + 1) * part
             ].astype(F32)
-    for job in (first, second):
-        each_step(lambda step, job=job: [job.finish(path, step) for path in range(2)])
+    paths(first.finish)
+    paths(second.finish)
     for line in lines:
         line.finish()
     for chunk in range(dp):
@@ -887,7 +936,7 @@
         def room(grad):
             chips, piece = fsdp // 2, (grad.shape[0],) + grad.shape[2:]
             return tuple(
-                pltpu.VMEM((count,) + piece, BF16) for count in (chips, chips - 1, chips - 1)
+                pltpu.VMEM((count,) + piece, BF16) for count in (chips, chips, chips - 1, chips - 1)
             )
 
         def line_sems(grad):
@@ -900,18 +949,22 @@
             functools.partial(last_kernel, fsdp), 4, 2, 2,
             [(narrow, BF16), (narrow, BF16), (small.shape, F32), (w_qkv.shape, F32),
              ((1, shard, width), F32), (w_up.shape, F32)],
-            [first_part, output_part, tokens, hidden, grad_hidden,
-             jnp.concatenate([gain1, down_b], 0), small, qkv_grad, out_grad,
-             scattered_up.reshape(dp, shard, ff_part)],
+            [first_part, jnp.concatenate([gain1, down_b], 0), small,
+             scattered_up.reshape(dp, shard, ff_part), output_part, tokens, hidden, grad_hidden,
+             qkv_grad, out_grad],
             (
                 pltpu.VMEM((stages + 1,) + small.shape, F32),
                 pltpu.VMEM((stages,) + small.shape, F32), pltpu.VMEM((8, width), F32),
+                pltpu.VMEM(wide, BF16), pltpu.VMEM(narrow, BF16), pltpu.VMEM(narrow, F32),
+                pltpu.VMEM(narrow, F32),
                 *room(qkv_grad), *room(out_grad),
                 pltpu.VMEM((dp, shard, 3 * part), F32), pltpu.VMEM((dp, shard, 3 * part), BF16),
                 pltpu.VMEM((dp, shard, 3 * part), BF16), pltpu.VMEM((dp, shard, ff_part), BF16),
-                line_sems(qkv_grad), line_sems(out_grad), pltpu.SemaphoreType.DMA((2, 2, dp)),
+                pltpu.SemaphoreType.DMA((4,)), pltpu.SemaphoreType.DMA((fsdp // 2,)),
+                pltpu.SemaphoreType.DMA((fsdp // 2,)), line_sems(qkv_grad), line_sems(out_grad),
+                pltpu.SemaphoreType.DMA((2, 2, dp)),
             ),
-            (2, stages),
+            (2, stages), 6,
         )
         grad_w_out = grad_w_out[0]
     else:

time: 613 us -> 599 us (0.977)
  Pallas kernels: 386 us -> 371 us
    pallas_call x4, Pallas kernels: 352 us -> 338 us  [call_exchange(): pl.pallas_call(kernel, in_specs=[pl.BlockSpec(memory_space=pltpu.VMEM)] *...]
  transfers between devices with their start and end apart: 6 -> 6, of which waited for: 1 -> 1; matrix products, arithmetic and copies ran while one was open for 21% -> 22% of each run, Pallas kernels for 63% -> 62%
where the time goes in v4:
time: 599 us; the launch traced here: 595 us
  Pallas kernels  371 us (62%)
  matrix products  122 us (20%)
  local copies, waits for them, and re-layouts  34.3 us (6%)
  blocking collectives  31.8 us (5%)
  between operations  14.8 us (2%)
  other arithmetic  13.7 us (2%)
  waiting for transfers between devices  6.98 us (1%)
    pallas_call x4, Pallas kernels, call_exchange(): pl.pallas_call(kernel, in_specs=[pl.BlockSpec(memory_space=pltpu.VMEM)] *...  338 us
    dot_general x4, matrix products, dot_nt(): lax.dot_general(a, b, (((1,), (1,)), ((), ())), preferred_element_type=F32)  44.7 us
    dot_general x4, matrix products, dot_tn(): lax.dot_general(a, b, (((0,), (0,)), ((), ())), preferred_element_type=F32)  42.1 us
    dot_general x3, matrix products, dot(): return jnp.dot(a, b, preferred_element_type=F32)  34.9 us
    pallas_call x1, Pallas kernels, attend_back(): pl.pallas_call(attend_back_kernel, grid=(rows // length,), in_specs=[pl.B...  22.2 us
    all_to_all x1, blocking collectives, layer(): lax.all_to_all(cols, 'dp', 1, 0, tiled=True).reshape(dp, shard, 3 * part)  16.4 us
    all_to_all x1, blocking collectives, layer(): lax.all_to_all(w_up, 'dp', 1, 0, tiled=True).reshape(dp, shard, ff_part)  15.4 us
  transfers between devices with their start and end apart: 6, of which 1 were waited for; matrix products, arithmetic and copies ran while one was open for 22% of the time, Pallas kernels for 62%

profile of v4, /device:TPU:0, one launch (start us, length us, event | category | flops | bytes accessed | tf_op | source)
XLA Modules:
  0.0 594.8 jit_solution(2799712390380533703)
XLA Ops:
  11.2 16.4 %all_to_all.32 = bf16[64,4,1536]{2,0,1:T(8,128)(2,1)} all-to-all(bf16[64,4,1536]{2,0,1:T(8,128)(2,1)S(1)} %all_to_all.24), channel_id=1, replica_groups=mesh['dp'=4,'fsdp'=8] {'dp'}, dimensions={1} | all-to-all | bytes 1572864 | tf_op jit(solution)/shard_map/all_to_all | solution.py:803
  28.6 15.4 %all_to_all.33 = bf16[64,4,2048]{2,0,1:T(8,128)(2,1)S(1)} all-to-all(bf16[64,4,2048]{2,0,1:T(8,128)(2,1)S(1)} %bitcast.70), channel_id=1, replica_groups=mesh['dp'=4,'fsdp'=8] {'dp'}, dimensions={1} | all-to-all | bytes 2097152 | tf_op jit(solution)/shard_map/all_to_all | solution.py:806
  48.2 81.4 %shard_map.270 = (bf16[1024,2048]{1,0:T(8,128)(2,1)}, bf16[1024,2048]{1,0:T(8,128)(2,1)}, bf16[32,768]{1,0:T(8,128)(2,1)}) custom-call(bf16[256,2048]{1,0:T(8,128)(2,1)} %tokens_any.1, bf16[256,2048]{1,0:T(8,128)(2,1)} %cotangent_ref.1, bf16[32,768]{1,0:T(8,128)(2,1)} %copy-done.9), custom_call_target="tpu_custom_call" | custom-call | flops 2097152 | bytes 209715200 | tf_op jit(solution)/shard_map/pallas_call | solution.py:635
  132.6 3.6 convert_reduce_fusion
  138.9 11.9 %add_convert_fusion.qkv_ref = bf16[1024,1536]{1,0:T(8,128)(2,1)} fusion(bf16[2048,1536]{1,0:T(8,128)(2,1)} %bitcast.78, f32[1536]{0:T(1024)S(1)} %fusion.13, bf16[1024,2048]{1,0:T(8,128)(2,1)} %get-tuple-element.45, f32[2048]{0:T(1024)S(1)} %add.95, f32[2048]{0:T(1024)S(1)} %mul.93, f32[1024]{0:T(1024)S(1)} %add_rsqrt_fusion, ...), kind=kOutput, calls=%fused_computation.21 | convolution fusion | flops 6458179584 | bytes 13662208 | tf_op jit(solution)/shard_map/dot_general | solution.py:784
  150.7 11.6 %attend.1 = (bf16[1024,512]{1,0:T(8,128)(2,1)}, f32[32,128]{1,0:T(8,128)}) custom-call(f32[8]{0:T(128)} %exponential_multiply_fusion.slope_ref, f32[256,256]{1,0:T(8,128)} %convert_select_fusion.distance_ref, bf16[1024,1536]{1,0:T(8,128)(2,1)} %add_convert_fusion.qkv_ref), custom_call_target="tpu_custom_call" | custom-call | flops 536870912 | bytes 4194304 | tf_op jit(solution)/shard_map/attend/pallas_call | solution.py:721
  162.3 6.3 %convolution_convert_fusion.5.partial_ref = bf16[1024,2048]{1,0:T(8,128)(2,1)} fusion(bf16[1024,512]{1,0:T(8,128)(2,1)} %get-tuple-element.47, bf16[512,2048]{1,0:T(8,128)(2,1)} %all-gather.7.cloned.1.call-done), kind=kOutput, calls=%fused_computation.24 | convolution fusion | flops 2149580800 | bytes 7340032 | tf_op jit(solution)/shard_map/dot_general | solution.py:784
  168.6 73.5 %shard_map.271 = (bf16[1024,2048]{1,0:T(8,128)(2,1)}, f32[256,2048]{1,0:T(8,128)}) custom-call(bf16[1024,2048]{1,0:T(8,128)(2,1)} %convolution_convert_fusion.5.partial_ref, bf16[256,2048]{1,0:T(8,128)(2,1)} %tokens_any.1, f32[3,2048]{1,0:T(4,128)} %pad_maximum_fusion.params_ref), custom_call_target="tpu_custom_call" | custom-call | flops 2097152 | bytes 209715200 | tf_op jit(solution)/shard_map/pallas_call | solution.py:635
  242.1 11.3 %copy.37 = bf16[4,512,2048]{2,1,0:T(8,128)(2,1)} copy(bf16[4,512,2048]{2,0,1:T(4,128)(2,1)} %all-gather.9.cloned.1.call-done) | data formatting | bytes 16777216 | tf_op jit(solution)/shard_map/all_gather | solution.py:807
  253.5 16.7 %fusion.10 = (bf16[1024,2048]{1,0:T(8,128)(2,1)}, bf16[1024,2048]{1,0:T(8,128)(2,1)S(1)}) fusion(f32[2048]{0:T(1024)S(1)} %bitcast.77, bf16[1024,2048]{1,0:T(8,128)(2,1)} %get-tuple-element.48, bf16[2048,2048]{1,0:T(8,128)(2,1)} %bitcast.65), kind=kOutput, calls=%fused_computation.13 | convolution fusion | flops 8615100416 | bytes 20979712 | tf_op jit(solution)/shard_map/dot_general | solution.py:784
  272.2 11.9 %convolution_convert_fusion.2 = bf16[2048,2048]{1,0:T(8,128)(2,1)} fusion(bf16[1024,2048]{1,0:T(8,128)(2,1)S(1)} %get-tuple-element.50.active_ref, bf16[1024,2048]{1,0:T(8,128)(2,1)S(1)} %copy-done.21), kind=kOutput, calls=%fused_computation.20 | convolution fusion | flops 8594128896 | bytes 16777216 | tf_op jit(solution)/shard_map/dot_general | solution.py:670
  284.1 5.2 all-gather.11.cloned.1.call-done.weight_ref
  289.3 13.3 %convert_reduce_fusion.1 = (f32[2048]{0:T(1024)S(1)}, bf16[1024,2048]{1,0:T(8,128)(2,1)S(1)}) fusion(bf16[1024,2048]{1,0:T(8,128)(2,1)} %get-tuple-element.52, bf16[1024,2048]{1,0:T(8,128)(2,1)} %get-tuple-element.51, bf16[2048,2048]{1,0:T(8,128)(2,1)} %all-gather.11.cloned.1.call-done.weight_ref), kind=kOutput, calls=%fused_computation.14 | convolution fusion | flops 8600418304 | bytes 20979712 | tf_op jit(solution)/shard_map/dot_general | solution.py:666
  302.6 11.5 %convolution_convert_fusion.1 = bf16[2048,2048]{1,0:T(8,128)(2,1)} fusion(bf16[1024,2048]{1,0:T(8,128)(2,1)S(1)} %copy-done.22, bf16[1024,2048]{1,0:T(8,128)(2,1)S(1)} %get-tuple-element.53), kind=kOutput, calls=%fused_computation.19 | convolution fusion | flops 8594128896 | bytes 16777216 | tf_op jit(solution)/shard_map/dot_general | solution.py:670
  316.3 14.8 %convolution_convert_fusion.4.partial_ref = bf16[1024,2048]{1,0:T(8,128)(2,1)} fusion(bf16[1024,2048]{1,0:T(8,128)(2,1)} %copy-done.24, bf16[2048,2048]{1,0:T(8,128)(2,1)} %bitcast.66), kind=kOutput, calls=%fused_computation.23 | convolution fusion | flops 8592031744 | bytes 16777216 | tf_op jit(solution)/shard_map/dot_general | solution.py:666
  331.2 79.5 %shard_map.272 = (bf16[1024,2048]{1,0:T(8,128)(2,1)}, f32[256,2048]{1,0:T(8,128)}, f32[8,2048]{1,0:T(8,128)}, bf16[1024,2048]{1,0:T(8,128)(2,1)}) custom-call(bf16[1024,2048]{1,0:T(8,128)(2,1)} %convolution_convert_fusion.4.partial_ref, f32[256,2048]{1,0:T(8,128)} %get-tuple-element.54.hidden_ref.hidden_any, bf16[256,2048]{1,0:T(8,128)(2,1)} %cotangent_ref.1, ...), custom_call_target="tpu_custom_call" | custom-call | flops 2097152 | bytes 209715200 | tf_op jit(solution)/shard_map/pallas_call | solution.py:635
  410.6 5.5 convolution_convert_fusion.7.grad_ref
  416.2 22.2 %attend_back.1 = bf16[1024,1536]{1,0:T(8,128)(2,1)} custom-call(f32[8]{0:T(128)} %exponential_multiply_fusion.slope_ref, f32[256,256]{1,0:T(8,128)} %convert_select_fusion.distance_ref, bf16[1024,1536]{1,0:T(8,128)(2,1)} %add_convert_fusion.qkv_ref, bf16[1024,512]{1,0:T(8,128)(2,1)} %convolution_convert_fusion.7.grad_ref), custom_call_target="tpu_custom_call" | custom-call | flops 1342177280 | bytes 7340032 | tf_op jit(solution)/shard_map/attend_back/pallas_call | solution.py:748
  438.4 12.4 %convolution_convert_fusion = bf16[2048,1536]{1,0:T(8,128)(2,1)} fusion(bf16[1024,1536]{1,0:T(8,128)(2,1)} %attend_back.1, bf16[1024,2048]{1,0:T(8,128)(2,1)} %get-tuple-element.45, f32[2048]{0:T(1024)S(1)} %add.95, f32[2048]{0:T(1024)S(1)} %mul.93, f32[1024]{0:T(1024)S(1)} %add_rsqrt_fusion, f32[1024]{0:T(1024)S(1)} %broadcast_multiply_fusion), kind=kOutput, calls=%fused_computation.18 | convolution fusion | flops 6458179584 | bytes 13656064 | tf_op jit(solution)/shard_map/dot_general | solution.py:670
  452.8 6.2 %convolution_convert_fusion.6 = bf16[512,2048]{1,0:T(8,128)(2,1)} fusion(bf16[1024,512]{1,0:T(8,128)(2,1)} %get-tuple-element.47, bf16[1024,2048]{1,0:T(8,128)(2,1)} %get-tuple-element.61), kind=kOutput, calls=%fused_computation.25 | convolution fusion | flops 2148532224 | bytes 7340032 | tf_op jit(solution)/shard_map/dot_general | solution.py:670
  459.1 11.0 %convolution_convert_fusion.3.first_ref = bf16[1024,2048]{1,0:T(8,128)(2,1)} fusion(bf16[1024,1536]{1,0:T(8,128)(2,1)S(1)} %copy-done.1, bf16[2048,1536]{1,0:T(8,128)(2,1)} %bitcast.79), kind=kOutput, calls=%fused_computation.22 | convolution fusion | flops 6444548096 | bytes 13631488 | tf_op jit(solution)/shard_map/dot_general | solution.py:666
  470.1 103.2 %shard_map.273 = (bf16[256,2048]{1,0:T(8,128)(2,1)}, bf16[256,2048]{1,0:T(8,128)(2,1)}, f32[16,2048]{1,0:T(8,128)}, f32[64,6144]{1,0:T(8,128)}, f32[1,64,2048]{2,1,0:T(8,128)}, /*index=5*/f32[64,8192]{1,0:T(8,128)}) custom-call(bf16[1024,2048]{1,0:T(8,128)(2,1)} %convolution_convert_fusion.3.first_ref, f32[2,2048]{1,0:T(2,128)} %pad_maximum_fusion.3.params_ref, ...), custom_call_target="tpu_custom_call" | custom-call | flops 2097152 | bytes 209715200 | tf_op jit(solution)/shard_map/pallas_call | solution.py:635
  578.2 2.8 convert_element_type.95
  581.0 2.5 copy.61
  (134 shorter events, 29.9 us)
Async XLA Ops:
  7.2 21.2 %copy-start.6 = (bf16[64,8192]{1,0:T(8,128)(2,1)S(1)}, bf16[64,8192]{1,0:T(8,128)(2,1)}, u32[]{:S(2)}) copy-start(bf16[64,8192]{1,0:T(8,128)(2,1)} %param.24) | copy-start | bytes 3145732
  7.2 131.7 %all-gather.5.cloned.1.call-start = ((), (), s32[]{:S(2)}) async-start(), calls=%async_computation.4 | async-start | bytes 7077888 | tf_op jit(solution)/shard_map/all_gather | solution.py:804
  27.6 134.7 %all-gather.7.cloned.1.call-start = ((), (), s32[]{:S(2)}) async-start(), calls=%async_computation.5 | async-start | bytes 2359296 | tf_op jit(solution)/shard_map/all_gather | solution.py:801
  28.4 213.8 %all-gather.9.cloned.1.call-start = ((), (), s32[]{:S(2)}) async-start(), calls=%async_computation.6 | async-start | bytes 9437184 | tf_op jit(solution)/shard_map/all_gather | solution.py:807
  28.4 18.0 %copy-start.12 = (bf16[64]{0:T(256)(128)(2,1)S(1)}, bf16[64]{0:T(256)(128)(2,1)}, u32[]{:S(2)}) copy-start(bf16[64]{0:T(256)(128)(2,1)} %param.21) | copy-start | bytes 388
  28.4 18.0 %copy-start.13 = (bf16[64]{0:T(256)(128)(2,1)S(1)}, bf16[64]{0:T(256)(128)(2,1)}, u32[]{:S(2)}) copy-start(bf16[64]{0:T(256)(128)(2,1)} %param.22) | copy-start | bytes 388
  28.4 18.0 %copy-start.14 = (bf16[64]{0:T(256)(128)(2,1)S(1)}, bf16[64]{0:T(256)(128)(2,1)}, u32[]{:S(2)}) copy-start(bf16[64]{0:T(256)(128)(2,1)} %param.23) | copy-start | bytes 388
  28.5 18.0 %copy-start.15 = (bf16[64]{0:T(256)(128)(2,1)S(1)}, bf16[64]{0:T(256)(128)(2,1)}, u32[]{:S(2)}) copy-start(bf16[64]{0:T(256)(128)(2,1)} %param.27) | copy-start | bytes 388
  28.5 18.0 %copy-start.16 = (bf16[64]{0:T(256)(128)(2,1)S(1)}, bf16[64]{0:T(256)(128)(2,1)}, u32[]{:S(2)}) copy-start(bf16[64]{0:T(256)(128)(2,1)} %param.28) | copy-start | bytes 388
  28.5 18.0 %copy-start.17 = (bf16[64]{0:T(256)(128)(2,1)S(1)}, bf16[64]{0:T(256)(128)(2,1)}, u32[]{:S(2)}) copy-start(bf16[64]{0:T(256)(128)(2,1)} %param.29) | copy-start | bytes 388
  28.5 18.0 %copy-start.18 = (bf16[64]{0:T(256)(128)(2,1)S(1)}, bf16[64]{0:T(256)(128)(2,1)}, u32[]{:S(2)}) copy-start(bf16[64]{0:T(256)(128)(2,1)} %param.18) | copy-start | bytes 388
  28.5 18.0 %copy-start.19 = (bf16[64]{0:T(256)(128)(2,1)S(1)}, bf16[64]{0:T(256)(128)(2,1)}, u32[]{:S(2)}) copy-start(bf16[64]{0:T(256)(128)(2,1)} %param.19) | copy-start | bytes 388
  28.5 18.0 %copy-start.20 = (bf16[256]{0:T(256)(128)(2,1)S(1)}, bf16[256]{0:T(256)(128)(2,1)}, u32[]{:S(2)}) copy-start(bf16[256]{0:T(256)(128)(2,1)} %param.25) | copy-start | bytes 1540
  45.8 243.5 %all-gather.11.cloned.1.call-start = ((), (), s32[]{:S(2)}) async-start(), calls=%async_computation.7 | async-start | bytes 9437184 | tf_op jit(solution)/shard_map/all_gather | solution.py:808
  46.4 423.7 %reduce-scatter.3.cloned.1.call-start = ((), (), s32[]{:S(2)}) async-start(), calls=%async_computation.8 | async-start | bytes 9437184 | tf_op jit(solution)/shard_map/reduce_scatter | solution.py:870
  253.5 18.7 %copy-start.21 = (bf16[1024,2048]{1,0:T(8,128)(2,1)S(1)}, bf16[1024,2048]{1,0:T(8,128)(2,1)}, u32[]{:S(2)}) copy-start(bf16[1024,2048]{1,0:T(8,128)(2,1)} %get-tuple-element.51) | copy-start | bytes 12582916
  289.3 13.4 %copy-start.22 = (bf16[1024,2048]{1,0:T(8,128)(2,1)S(1)}, bf16[1024,2048]{1,0:T(8,128)(2,1)}, u32[]{:S(2)}) copy-start(bf16[1024,2048]{1,0:T(8,128)(2,1)} %get-tuple-element.48) | copy-start | bytes 12582916
  302.6 11.5 %copy-start.24 = (bf16[1024,2048]{1,0:T(8,128)(2,1)}, bf16[1024,2048]{1,0:T(8,128)(2,1)S(1)}, u32[]{:S(2)}) copy-start(bf16[1024,2048]{1,0:T(8,128)(2,1)S(1)} %get-tuple-element.53) | copy-start | bytes 12582916
  314.2 264.1 %reduce-scatter.5.cloned.1.call-start = ((), (), s32[]{:S(2)}) async-start(), calls=%async_computation.9 | async-start | bytes 9437184 | tf_op jit(solution)/shard_map/reduce_scatter | solution.py:866
  331.2 79.5 %copy-start.23 = (bf16[512,2048]{1,0:T(8,128)(2,1)S(1)}, bf16[512,2048]{1,0:T(8,128)(2,1)}, u32[]{:S(2)}) copy-start(bf16[512,2048]{1,0:T(8,128)(2,1)} %all-gather.7.cloned.1.call-done) | copy-start | bytes 6291460
  438.4 12.4 %copy-start.10 = (f32[8,2048]{1,0:T(8,128)S(1)}, f32[8,2048]{1,0:T(8,128)}, u32[]{:S(2)}) copy-start(f32[8,2048]{1,0:T(8,128)} %get-tuple-element.57) | copy-start | bytes 196612
  438.4 12.5 %copy-start.1 = (bf16[1024,1536]{1,0:T(8,128)(2,1)S(1)}, bf16[1024,1536]{1,0:T(8,128)(2,1)}, u32[]{:S(2)}) copy-start(bf16[1024,1536]{1,0:T(8,128)(2,1)} %attend_back.1) | copy-start | bytes 9437188
  470.1 107.1 %copy-start.3 = (bf16[64,6144]{1,0:T(8,128)(2,1)S(1)}, bf16[64,6144]{1,0:T(8,128)(2,1)}, u32[]{:S(2)}) copy-start(bf16[64,6144]{1,0:T(8,128)(2,1)} %param.17) | copy-start | bytes 2359300
  573.3 10.2 %copy-start.7 = (bf16[256,2048]{1,0:T(8,128)(2,1)S(1)}, bf16[256,2048]{1,0:T(8,128)(2,1)}, u32[]{:S(2)}) copy-start(bf16[256,2048]{1,0:T(8,128)(2,1)} %get-tuple-element.107) | copy-start | bytes 3145732
  (7 other events, 26.9 us)
Sparse Core Ops, SparseCore 0:
  27.7 66.4 all-gather.4
  95.8 27.7 all-gather.6
  125.8 81.4 all-gather.8
  208.7 80.5 all-gather.10
  314.3 88.0 reduce-scatter.2
  404.5 93.6 reduce-scatter.4

commit v5 on v4

--- a/solution.py
+++ b/solution.py
@@ -214,6 +214,12 @@
         self.closing(path, step).wait_send()
 
 
+def regroup(values, outer, inner):
+    piece = values.shape[1] // (outer * inner)
+    starts = [(o * inner + i) * piece for i in range(inner) for o in range(outer)]
+    return jnp.concatenate([values[:, start : start + piece] for start in starts], 1)
+
+
 def row_norm(values):
     centred = values - jnp.mean(values, axis=-1, keepdims=True)
     inverse_std = lax.rsqrt(jnp.mean(centred * centred, axis=-1, keepdims=True) + EPS)
@@ -261,16 +267,23 @@
         out[: source.shape[0]] = source[...]
         jobs.append(Gather(out, sems.at[k], near))
     held[0] = table_ref[...]
-    small = Doubling(held, landing, small_sems, partners, jnp.add)
-    small.run(0, 1)
+    small = Doubling(held, landing, small_sems, partners[2:] + partners[:2], jnp.add)
+
+    def paths(act):
+        each_step(lambda step: [act(path, step) for path in range(2)])
+
+    paths(jobs[0].send)
+    small.run(*range(len(partners) - 2))
+    small.start(len(partners) - 2)
+    paths(jobs[0].forward)
+    small.end(len(partners) - 2)
+    small.start(len(partners) - 1)
+    paths(jobs[1].send)
+    small.end(len(partners) - 1)
+    table_out[...] = held[len(partners)]
+    paths(jobs[1].forward)
     for job in jobs:
-        each_step(lambda step, job=job: [job.send(path, step) for path in range(2)])
-    small.run(*range(2, len(partners)))
-    table_out[...] = held[len(partners)]
-    for job in jobs:
-        each_step(lambda step, job=job: [job.forward(path, step) for path in range(2)])
-    for job in jobs:
-        each_step(lambda step, job=job: [job.finish(path, step) for path in range(2)])
+        paths(job.finish)
 
 
 def exchange(scatter, gather, rows_of, beside=None):
@@ -304,7 +317,7 @@
 
 
 def hidden_kernel(
-    partial_ref, tokens_ref, params_ref, out_ref, hidden_ref, landing, passing, last, sems
+    fsdp, partial_ref, tokens_ref, params_ref, out_ref, hidden_ref, landing, passing, last, sems
 ):
     near, _ = neighbours()
 
@@ -312,7 +325,7 @@
         hidden = tokens_ref[rows].astype(F32) + total + params_ref[0:1]
         hidden_ref[rows] = hidden
         normed, _ = row_norm(hidden)
-        return (normed * params_ref[1:2] + params_ref[2:3]).astype(BF16)
+        return regroup(normed * params_ref[1:2] + params_ref[2:3], 4, fsdp).astype(BF16)
 
     exchange(
         Scatter(partial_ref, landing, passing, last, sems.at[0], near),
@@ -321,7 +334,7 @@
 
 
 def branch_kernel(
-    partial_ref, hidden_ref, cotangent_ref, params_ref, active_ref, weight_ref, out_ref, grad_ref,
+    fsdp, partial_ref, hidden_ref, cotangent_ref, params_ref, active_ref, weight_ref, out_ref, grad_ref,
     sums_ref, output_ref, landing, passing, last, active, weight, copy_sems, sems,
 ):
     copies = [
@@ -334,6 +347,7 @@
     sums_ref[...] = jnp.zeros_like(sums_ref)
 
     def rows_of(rows, total):
+        total = regroup(total, fsdp, 4)
         normed, inverse_std = row_norm(hidden_ref[rows])
         upper = cotangent_ref[rows].astype(F32)
         grad = upper + row_back(total, normed, inverse_std, params_ref[1:2])
@@ -605,7 +619,7 @@
     columns = up_ref.shape[2]
     for slot in range(dp):
         up_across.receive(slot)
-        up_out[:, slot * columns : (slot + 1) * columns] = up_in[slot].astype(F32)
+        up_out[:, slot * columns : (slot + 1) * columns] = up_in[slot]
     small.end(4)
     small_out[...] = held[len(partners)]
     for slot in range(dp):
@@ -614,7 +628,7 @@
             start = (third * dp + slot) * part
             qkv_out[:, start : start + part] = qkv_in[
                 slot, :, third * part : (third + 1) * part
-            ].astype(F32)
+            ]
     paths(first.finish)
     paths(second.finish)
     for line in lines:
@@ -803,8 +817,8 @@
     cols = lax.all_to_all(cols, "dp", 1, 0, tiled=True).reshape(dp, shard, 3 * part)
     qkv_w = lax.all_gather(cols, "fsdp", axis=1, tiled=True).reshape(width, 3 * part)
     w_up, cols = lax.optimization_barrier((w_up, cols))
-    ups = lax.all_to_all(w_up, "dp", 1, 0, tiled=True).reshape(dp, shard, ff_part)
-    up_w = lax.all_gather(ups, "fsdp", axis=1, tiled=True).reshape(width, ff_part)
+    ups = lax.all_to_all(w_up, "dp", 1, 0, tiled=True)
+    up_w = lax.all_gather(ups, "fsdp", axis=0, tiled=True)
     down_w = lax.all_gather(w_down, "fsdp", axis=0, tiled=True)
     late_tokens, _ = lax.optimization_barrier((tokens, ups))
 
@@ -848,13 +862,14 @@
     out_part = dot(mixed, out_w).astype(BF16)
     if kernels:
         second_in, hidden = call_exchange(
-            hidden_kernel, 2, 2, 1, [(wide, BF16), (narrow, F32)],
+            functools.partial(hidden_kernel, fsdp), 2, 2, 1, [(wide, BF16), (narrow, F32)],
             [out_part, tokens, jnp.concatenate([out_b, gain2, shift2], 0)],
         )
     else:
         hidden = inputs + scatter_dp(out_part, dp) + out_b
         normed2, inverse2 = norm_stats(hidden)
-        second_in = gather_dp((normed2 * gain2 + shift2).astype(BF16), dp)
+        second_in = regroup(normed2 * gain2 + shift2, dp, fsdp).astype(BF16)
+        second_in = gather_dp(second_in, dp)
 
     upward = dot(second_in, up_w) + up_b
     cumulative = 0.5 * (1.0 + lax.erf(upward * (0.5**0.5)))
@@ -870,9 +885,8 @@
         return lax.psum_scatter(grad, "fsdp", scatter_dimension=1, tiled=True)
 
     def exchange_columns(grad):
-        return lax.all_to_all(
-            grad.reshape(dp * shard, grad.shape[2]), "dp", 0, 1, tiled=True
-        ).astype(F32)
+        grad = grad.reshape(dp * shard, grad.shape[-1])
+        return lax.all_to_all(grad, "dp", 0, 1, tiled=True).astype(F32)
 
     local_down = dot_tn(active, grad_y).astype(BF16)
     late_y, slope, _ = lax.optimization_barrier((grad_y, slope, local_down))
@@ -881,10 +895,10 @@
     local_up = dot_tn(second_in, grad_upward).astype(BF16)
     late_upward, _ = lax.optimization_barrier((grad_upward, local_up))
     second_part = dot_nt(late_upward, up_w).astype(BF16)
-    scattered_up = reduce_columns(local_up)
+    scattered_up = lax.psum_scatter(local_up, "fsdp", scatter_dimension=0, tiled=True)
     if kernels:
         branch_all, grad_hidden, branch_sums, output_part = call_exchange(
-            branch_kernel, 3, 2, 1,
+            functools.partial(branch_kernel, fsdp), 3, 2, 1,
             [(wide, BF16), (narrow, F32), ((8, width), F32), (wide, BF16)],
             [second_part, hidden, cotangent, jnp.concatenate([out_b, gain2], 0), active, down_w],
             (pltpu.VMEM(active.shape, BF16), pltpu.VMEM(down_w.shape, BF16),
@@ -892,7 +906,7 @@
             unplaced=2,
         )
     else:
-        grad_second = scatter_dp(second_part, dp)
+        grad_second = regroup(scatter_dp(second_part, dp), fsdp, dp)
         grad_hidden = cotangent.astype(F32) + norm_back(grad_second, normed2, inverse2, gain2)
         grad_branch = grad_hidden.astype(BF16)
         branch_all = gather_dp(grad_branch, dp)
@@ -947,8 +961,8 @@
         out_grad = local_out.reshape(1, fsdp, shard, width)
         grad_tokens, output, small, grad_w_qkv, grad_w_out, grad_w_up = call_exchange(
             functools.partial(last_kernel, fsdp), 4, 2, 2,
-            [(narrow, BF16), (narrow, BF16), (small.shape, F32), (w_qkv.shape, F32),
-             ((1, shard, width), F32), (w_up.shape, F32)],
+            [(narrow, BF16), (narrow, BF16), (small.shape, F32), (w_qkv.shape, BF16),
+             ((1, shard, width), F32), (w_up.shape, BF16)],
             [first_part, jnp.concatenate([gain1, down_b], 0), small,
              scattered_up.reshape(dp, shard, ff_part), output_part, tokens, hidden, grad_hidden,
              qkv_grad, out_grad],
@@ -967,6 +981,7 @@
             (2, stages), 6,
         )
         grad_w_out = grad_w_out[0]
+        grad_w_qkv, grad_w_up = grad_w_qkv.astype(F32), grad_w_up.astype(F32)
     else:
         grad_first = scatter_dp(first_part, dp)
         normed1, inverse1 = norm_stats(inputs)

time: 599 us -> 601 us (level)
  waiting for transfers between devices: 6.98 us -> 23.3 us
  local copies, waits for them, and re-layouts: 34.3 us -> 18.9 us
    all_gather x1, waiting for transfers between devices: 5.17 us -> 21.5 us  [layer(): down_w = lax.all_gather(w_down, 'fsdp', axis=0, tiled=True)]
    all_gather x1 -> x0, local copies, waits for them, and re-layouts: 11.3 us -> none  [layer(): lax.all_gather(ups, 'fsdp', axis=1, tiled=True).reshape(width, ff_part)]
  transfers between devices with their start and end apart: 6 -> 6, of which waited for: 1 -> 1; matrix products, arithmetic and copies ran while one was open for 22% -> 20% of each run, Pallas kernels for 62% -> 61%
where the time goes in v5:
time: 601 us; the launch traced here: 598 us
  Pallas kernels  367 us (61%)
  matrix products  123 us (20%)
  blocking collectives  32.6 us (5%)
  waiting for transfers between devices  23.3 us (4%)
  local copies, waits for them, and re-layouts  18.9 us (3%)
  other arithmetic  18.3 us (3%)
  between operations  14.8 us (2%)
    pallas_call x4, Pallas kernels, call_exchange(): pl.pallas_call(kernel, in_specs=[pl.BlockSpec(memory_space=pltpu.VMEM)] *...  333 us
    dot_general x4, matrix products, dot_nt(): lax.dot_general(a, b, (((1,), (1,)), ((), ())), preferred_element_type=F32)  45.2 us
    dot_general x4, matrix products, dot_tn(): lax.dot_general(a, b, (((0,), (0,)), ((), ())), preferred_element_type=F32)  41.6 us
    dot_general x3, matrix products, dot(): return jnp.dot(a, b, preferred_element_type=F32)  35.9 us
    pallas_call x1, Pallas kernels, attend_back(): pl.pallas_call(attend_back_kernel, grid=(rows // length,), in_specs=[pl.B...  22.2 us
    all_gather x1, waiting for transfers between devices, layer(): down_w = lax.all_gather(w_down, 'fsdp', axis=0, tiled=True)  21.5 us
    all_to_all x1, blocking collectives, layer(): lax.all_to_all(cols, 'dp', 1, 0, tiled=True).reshape(dp, shard, 3 * part)  16.6 us
    all_to_all x1, blocking collectives, layer(): ups = lax.all_to_all(w_up, 'dp', 1, 0, tiled=True)  16.1 us
  transfers between devices with their start and end apart: 6, of which 1 were waited for; matrix products, arithmetic and copies ran while one was open for 20% of the time, Pallas kernels for 61%

profile of v5, /device:TPU:0, one launch (start us, length us, event | category | flops | bytes accessed | tf_op | source)
XLA Modules:
  0.0 597.6 jit_solution(3398964529868153285)
XLA Ops:
  11.3 16.6 %all_to_all.35 = bf16[64,4,1536]{2,0,1:T(8,128)(2,1)} all-to-all(bf16[64,4,1536]{2,0,1:T(8,128)(2,1)S(1)} %all_to_all.26), channel_id=1, replica_groups=mesh['dp'=4,'fsdp'=8] {'dp'}, dimensions={1} | all-to-all | bytes 1572864 | tf_op jit(solution)/shard_map/all_to_all | solution.py:817
  28.8 16.1 %all_to_all.36 = bf16[64,4,2048]{2,0,1:T(8,128)(2,1)} all-to-all(bf16[64,4,2048]{2,0,1:T(8,128)(2,1)S(1)} %bitcast.68), channel_id=1, replica_groups=mesh['dp'=4,'fsdp'=8] {'dp'}, dimensions={1} | all-to-all | bytes 2097152 | tf_op jit(solution)/shard_map/all_to_all | solution.py:820
  47.2 76.7 %shard_map.270 = (bf16[1024,2048]{1,0:T(8,128)(2,1)}, bf16[1024,2048]{1,0:T(8,128)(2,1)}, bf16[32,768]{1,0:T(8,128)(2,1)}) custom-call(bf16[256,2048]{1,0:T(8,128)(2,1)} %tokens_any.1, bf16[256,2048]{1,0:T(8,128)(2,1)} %cotangent_ref.1, bf16[32,768]{1,0:T(8,128)(2,1)} %copy-done.8), custom_call_target="tpu_custom_call" | custom-call | flops 2097152 | bytes 209715200 | tf_op jit(solution)/shard_map/pallas_call | solution.py:649
  127.2 3.0 convert_reduce_fusion
  132.4 12.7 %add_convert_fusion.qkv_ref = bf16[1024,1536]{1,0:T(8,128)(2,1)} fusion(bf16[2048,1536]{1,0:T(8,128)(2,1)} %bitcast.77, f32[1536]{0:T(1024)S(1)} %fusion.13, bf16[1024,2048]{1,0:T(8,128)(2,1)} %get-tuple-element.45, f32[2048]{0:T(1024)S(1)} %add.95, f32[2048]{0:T(1024)S(1)} %mul.93, f32[1024]{0:T(1024)S(1)} %add_rsqrt_fusion, ...), kind=kOutput, calls=%fused_computation.21 | convolution fusion | flops 6458179584 | bytes 13662208 | tf_op jit(solution)/shard_map/dot_general | solution.py:798
  145.1 11.6 %attend.1 = (bf16[1024,512]{1,0:T(8,128)(2,1)}, f32[32,128]{1,0:T(8,128)}) custom-call(f32[8]{0:T(128)} %exponential_multiply_fusion.slope_ref, f32[256,256]{1,0:T(8,128)} %convert_select_fusion.distance_ref, bf16[1024,1536]{1,0:T(8,128)(2,1)} %add_convert_fusion.qkv_ref), custom_call_target="tpu_custom_call" | custom-call | flops 536870912 | bytes 4194304 | tf_op jit(solution)/shard_map/attend/pallas_call | solution.py:735
  156.7 6.3 %convolution_convert_fusion.5.partial_ref = bf16[1024,2048]{1,0:T(8,128)(2,1)} fusion(bf16[1024,512]{1,0:T(8,128)(2,1)} %get-tuple-element.47, bf16[512,2048]{1,0:T(8,128)(2,1)} %all-gather.7.cloned.1.call-done), kind=kOutput, calls=%fused_computation.24 | convolution fusion | flops 2149580800 | bytes 7340032 | tf_op jit(solution)/shard_map/dot_general | solution.py:798
  162.9 74.0 %shard_map.271 = (bf16[1024,2048]{1,0:T(8,128)(2,1)}, f32[256,2048]{1,0:T(8,128)}) custom-call(bf16[1024,2048]{1,0:T(8,128)(2,1)} %convolution_convert_fusion.5.partial_ref, bf16[256,2048]{1,0:T(8,128)(2,1)} %tokens_any.1, f32[3,2048]{1,0:T(4,128)} %pad_maximum_fusion.params_ref), custom_call_target="tpu_custom_call" | custom-call | flops 2097152 | bytes 209715200 | tf_op jit(solution)/shard_map/pallas_call | solution.py:649
  237.0 16.9 %fusion.10 = (bf16[1024,2048]{1,0:T(8,128)(2,1)}, bf16[1024,2048]{1,0:T(8,128)(2,1)S(1)}) fusion(f32[2048]{0:T(1024)S(1)} %bitcast.76, bf16[1024,2048]{1,0:T(8,128)(2,1)} %get-tuple-element.48, bf16[2048,2048]{1,0:T(8,128)(2,1)} %all-gather.9.cloned.1.call-done), kind=kOutput, calls=%fused_computation.13 | convolution fusion | flops 8615100416 | bytes 20979712 | tf_op jit(solution)/shard_map/dot_general | solution.py:798
  256.0 11.5 %convolution_convert_fusion.2 = bf16[2048,2048]{1,0:T(8,128)(2,1)} fusion(bf16[1024,2048]{1,0:T(8,128)(2,1)S(1)} %get-tuple-element.50.active_ref, bf16[1024,2048]{1,0:T(8,128)(2,1)S(1)} %copy-done.20), kind=kOutput, calls=%fused_computation.20 | convolution fusion | flops 8594128896 | bytes 16777216 | tf_op jit(solution)/shard_map/dot_general | solution.py:684
  267.5 21.5 %all-gather.11.cloned.1.call-done.weight_ref = bf16[2048,2048]{1,0:T(8,128)(2,1)} async-done(((bf16[256,2048]{1,0:T(8,128)(2,1)}), bf16[2048,2048]{1,0:T(8,128)(2,1)}) %all-gather.11.cloned.1.call-update) | async-done | bytes 8388624 | tf_op jit(solution)/shard_map/all_gather | solution.py:822
  289.0 13.8 %convert_reduce_fusion.1 = (f32[2048]{0:T(1024)S(1)}, bf16[1024,2048]{1,0:T(8,128)(2,1)S(1)}) fusion(bf16[1024,2048]{1,0:T(8,128)(2,1)} %get-tuple-element.52, bf16[1024,2048]{1,0:T(8,128)(2,1)} %get-tuple-element.51, bf16[2048,2048]{1,0:T(8,128)(2,1)} %all-gather.11.cloned.1.call-done.weight_ref), kind=kOutput, calls=%fused_computation.14 | convolution fusion | flops 8600418304 | bytes 20979712 | tf_op jit(solution)/shard_map/dot_general | solution.py:680
  304.8 11.4 %convolution_convert_fusion.1 = bf16[2048,2048]{1,0:T(8,128)(2,1)} fusion(bf16[1024,2048]{1,0:T(8,128)(2,1)S(1)} %copy-done.21, bf16[1024,2048]{1,0:T(8,128)(2,1)S(1)} %get-tuple-element.53), kind=kOutput, calls=%fused_computation.19 | convolution fusion | flops 8594128896 | bytes 16777216 | tf_op jit(solution)/shard_map/dot_general | solution.py:684
  318.4 14.8 %convolution_convert_fusion.4.partial_ref = bf16[1024,2048]{1,0:T(8,128)(2,1)} fusion(bf16[1024,2048]{1,0:T(8,128)(2,1)} %copy-done.23, bf16[2048,2048]{1,0:T(8,128)(2,1)} %all-gather.9.cloned.1.call-done), kind=kOutput, calls=%fused_computation.23 | convolution fusion | flops 8592031744 | bytes 16777216 | tf_op jit(solution)/shard_map/dot_general | solution.py:680
  333.2 79.5 %shard_map.272 = (bf16[1024,2048]{1,0:T(8,128)(2,1)}, f32[256,2048]{1,0:T(8,128)}, f32[8,2048]{1,0:T(8,128)}, bf16[1024,2048]{1,0:T(8,128)(2,1)}) custom-call(bf16[1024,2048]{1,0:T(8,128)(2,1)} %convolution_convert_fusion.4.partial_ref, f32[256,2048]{1,0:T(8,128)} %get-tuple-element.54.hidden_ref.hidden_any, bf16[256,2048]{1,0:T(8,128)(2,1)} %cotangent_ref.1, ...), custom_call_target="tpu_custom_call" | custom-call | flops 2097152 | bytes 209715200 | tf_op jit(solution)/shard_map/pallas_call | solution.py:649
  412.7 5.5 convolution_convert_fusion.7.grad_ref
  418.2 22.2 %attend_back.1 = bf16[1024,1536]{1,0:T(8,128)(2,1)} custom-call(f32[8]{0:T(128)} %exponential_multiply_fusion.slope_ref, f32[256,256]{1,0:T(8,128)} %convert_select_fusion.distance_ref, bf16[1024,1536]{1,0:T(8,128)(2,1)} %add_convert_fusion.qkv_ref, bf16[1024,512]{1,0:T(8,128)(2,1)} %convolution_convert_fusion.7.grad_ref), custom_call_target="tpu_custom_call" | custom-call | flops 1342177280 | bytes 7340032 | tf_op jit(solution)/shard_map/attend_back/pallas_call | solution.py:762
  440.5 12.5 %convolution_convert_fusion = bf16[2048,1536]{1,0:T(8,128)(2,1)} fusion(bf16[1024,1536]{1,0:T(8,128)(2,1)} %attend_back.1, bf16[1024,2048]{1,0:T(8,128)(2,1)} %get-tuple-element.45, f32[2048]{0:T(1024)S(1)} %add.95, f32[2048]{0:T(1024)S(1)} %mul.93, f32[1024]{0:T(1024)S(1)} %add_rsqrt_fusion, f32[1024]{0:T(1024)S(1)} %broadcast_multiply_fusion), kind=kOutput, calls=%fused_computation.18 | convolution fusion | flops 6458179584 | bytes 13656064 | tf_op jit(solution)/shard_map/dot_general | solution.py:684
  454.9 6.2 %convolution_convert_fusion.6 = bf16[512,2048]{1,0:T(8,128)(2,1)} fusion(bf16[1024,512]{1,0:T(8,128)(2,1)} %get-tuple-element.47, bf16[1024,2048]{1,0:T(8,128)(2,1)} %get-tuple-element.61), kind=kOutput, calls=%fused_computation.25 | convolution fusion | flops 2148532224 | bytes 7340032 | tf_op jit(solution)/shard_map/dot_general | solution.py:684
  461.2 11.1 %convolution_convert_fusion.3.first_ref = bf16[1024,2048]{1,0:T(8,128)(2,1)} fusion(bf16[1024,1536]{1,0:T(8,128)(2,1)S(1)} %copy-done.1, bf16[2048,1536]{1,0:T(8,128)(2,1)} %bitcast.78), kind=kOutput, calls=%fused_computation.22 | convolution fusion | flops 6444548096 | bytes 13631488 | tf_op jit(solution)/shard_map/dot_general | solution.py:680
  472.3 102.5 %shard_map.273 = (bf16[256,2048]{1,0:T(8,128)(2,1)}, bf16[256,2048]{1,0:T(8,128)(2,1)}, f32[16,2048]{1,0:T(8,128)}, bf16[64,6144]{1,0:T(8,128)(2,1)}, f32[1,64,2048]{2,1,0:T(8,128)}, /*index=5*/bf16[64,8192]{1,0:T(8,128)(2,1)}) custom-call(bf16[1024,2048]{1,0:T(8,128)(2,1)} %convolution_convert_fusion.3.first_ref, f32[2,2048]{1,0:T(2,128)} %pad_maximum_fusion.3.params_ref, ...), custom_call_target="tpu_custom_call" | custom-call | flops 2097152 | bytes 209715200 | tf_op jit(solution)/shard_map/pallas_call | solution.py:649
  574.8 2.8 convert_element_type.102
  577.6 2.5 convert_element_type.101
  585.0 2.8 convert_element_type.103
  (130 shorter events, 28.2 us)
Async XLA Ops:
  7.2 21.5 %copy-start.4 = (bf16[64,8192]{1,0:T(8,128)(2,1)S(1)}, bf16[64,8192]{1,0:T(8,128)(2,1)}, u32[]{:S(2)}) copy-start(bf16[64,8192]{1,0:T(8,128)(2,1)} %param.24) | copy-start | bytes 3145732
  7.2 125.2 %all-gather.5.cloned.1.call-start = ((), (), s32[]{:S(2)}) async-start(), calls=%async_computation.4 | async-start | bytes 7077888 | tf_op jit(solution)/shard_map/all_gather | solution.py:818
  11.2 34.4 %copy-start.11 = (bf16[64]{0:T(256)(128)(2,1)S(1)}, bf16[64]{0:T(256)(128)(2,1)}, u32[]{:S(2)}) copy-start(bf16[64]{0:T(256)(128)(2,1)} %param.21) | copy-start | bytes 388
  11.2 34.4 %copy-start.12 = (bf16[64]{0:T(256)(128)(2,1)S(1)}, bf16[64]{0:T(256)(128)(2,1)}, u32[]{:S(2)}) copy-start(bf16[64]{0:T(256)(128)(2,1)} %param.22) | copy-start | bytes 388
  11.2 34.4 %copy-start.13 = (bf16[64]{0:T(256)(128)(2,1)S(1)}, bf16[64]{0:T(256)(128)(2,1)}, u32[]{:S(2)}) copy-start(bf16[64]{0:T(256)(128)(2,1)} %param.23) | copy-start | bytes 388
  11.2 34.4 %copy-start.14 = (bf16[64]{0:T(256)(128)(2,1)S(1)}, bf16[64]{0:T(256)(128)(2,1)}, u32[]{:S(2)}) copy-start(bf16[64]{0:T(256)(128)(2,1)} %param.27) | copy-start | bytes 388
  11.2 34.4 %copy-start.15 = (bf16[64]{0:T(256)(128)(2,1)S(1)}, bf16[64]{0:T(256)(128)(2,1)}, u32[]{:S(2)}) copy-start(bf16[64]{0:T(256)(128)(2,1)} %param.28) | copy-start | bytes 388
  11.2 34.3 %copy-start.16 = (bf16[64]{0:T(256)(128)(2,1)S(1)}, bf16[64]{0:T(256)(128)(2,1)}, u32[]{:S(2)}) copy-start(bf16[64]{0:T(256)(128)(2,1)} %param.29) | copy-start | bytes 388
  11.2 34.3 %copy-start.17 = (bf16[64]{0:T(256)(128)(2,1)S(1)}, bf16[64]{0:T(256)(128)(2,1)}, u32[]{:S(2)}) copy-start(bf16[64]{0:T(256)(128)(2,1)} %param.18) | copy-start | bytes 388
  11.2 34.3 %copy-start.18 = (bf16[64]{0:T(256)(128)(2,1)S(1)}, bf16[64]{0:T(256)(128)(2,1)}, u32[]{:S(2)}) copy-start(bf16[64]{0:T(256)(128)(2,1)} %param.19) | copy-start | bytes 388
  11.3 34.3 %copy-start.19 = (bf16[256]{0:T(256)(128)(2,1)S(1)}, bf16[256]{0:T(256)(128)(2,1)}, u32[]{:S(2)}) copy-start(bf16[256]{0:T(256)(128)(2,1)} %param.25) | copy-start | bytes 1540
  27.8 128.8 %all-gather.7.cloned.1.call-start = ((), (), s32[]{:S(2)}) async-start(), calls=%async_computation.5 | async-start | bytes 2359296 | tf_op jit(solution)/shard_map/all_gather | solution.py:815
  28.6 208.4 %all-gather.9.cloned.1.call-start = ((), (), s32[]{:S(2)}) async-start(), calls=%async_computation.6 | async-start | bytes 9437184 | tf_op jit(solution)/shard_map/all_gather | solution.py:821
  44.9 244.1 %all-gather.11.cloned.1.call-start = ((), (), s32[]{:S(2)}) async-start(), calls=%async_computation.7 | async-start | bytes 9437184 | tf_op jit(solution)/shard_map/all_gather | solution.py:822
  45.5 426.8 %reduce-scatter.3.cloned.1.call-start = ((), (), s32[]{:S(2)}) async-start(), calls=%async_computation.8 | async-start | bytes 9437184 | tf_op jit(solution)/shard_map/reduce_scatter | solution.py:898
  237.0 19.0 %copy-start.20 = (bf16[1024,2048]{1,0:T(8,128)(2,1)S(1)}, bf16[1024,2048]{1,0:T(8,128)(2,1)}, u32[]{:S(2)}) copy-start(bf16[1024,2048]{1,0:T(8,128)(2,1)} %get-tuple-element.51) | copy-start | bytes 12582916
  289.0 15.8 %copy-start.21 = (bf16[1024,2048]{1,0:T(8,128)(2,1)S(1)}, bf16[1024,2048]{1,0:T(8,128)(2,1)}, u32[]{:S(2)}) copy-start(bf16[1024,2048]{1,0:T(8,128)(2,1)} %get-tuple-element.48) | copy-start | bytes 12582916
  316.3 268.7 %reduce-scatter.5.cloned.1.call-start = ((), (), s32[]{:S(2)}) async-start(), calls=%async_computation.9 | async-start | bytes 9437184 | tf_op jit(solution)/shard_map/reduce_scatter | solution.py:881
  333.2 79.5 %copy-start.22 = (bf16[512,2048]{1,0:T(8,128)(2,1)S(1)}, bf16[512,2048]{1,0:T(8,128)(2,1)}, u32[]{:S(2)}) copy-start(bf16[512,2048]{1,0:T(8,128)(2,1)} %all-gather.7.cloned.1.call-done) | copy-start | bytes 6291460
  440.5 12.5 %copy-start.9 = (f32[8,2048]{1,0:T(8,128)S(1)}, f32[8,2048]{1,0:T(8,128)}, u32[]{:S(2)}) copy-start(f32[8,2048]{1,0:T(8,128)} %get-tuple-element.57) | copy-start | bytes 196612
  440.5 12.5 %copy-start.1 = (bf16[1024,1536]{1,0:T(8,128)(2,1)S(1)}, bf16[1024,1536]{1,0:T(8,128)(2,1)}, u32[]{:S(2)}) copy-start(bf16[1024,1536]{1,0:T(8,128)(2,1)} %attend_back.1) | copy-start | bytes 9437188
  574.8 9.1 %copy-start.3 = (bf16[64,6144]{1,0:T(8,128)(2,1)S(1)}, bf16[64,6144]{1,0:T(8,128)(2,1)}, u32[]{:S(2)}) copy-start(bf16[64,6144]{1,0:T(8,128)(2,1)} %param.17) | copy-start | bytes 2359300
  577.6 10.2 %copy-start.6 = (bf16[256,2048]{1,0:T(8,128)(2,1)S(1)}, bf16[256,2048]{1,0:T(8,128)(2,1)}, u32[]{:S(2)}) copy-start(bf16[256,2048]{1,0:T(8,128)(2,1)} %get-tuple-element.106) | copy-start | bytes 3145732
  577.6 11.1 %copy-start.5 = (bf16[256,2048]{1,0:T(8,128)(2,1)S(1)}, bf16[256,2048]{1,0:T(8,128)(2,1)}, u32[]{:S(2)}) copy-start(bf16[256,2048]{1,0:T(8,128)(2,1)} %get-tuple-element.107) | copy-start | bytes 3145732
  (6 other events, 16.5 us)
Sparse Core Ops, SparseCore 0:
  28.0 66.4 all-gather.4
  96.1 27.7 all-gather.6
  125.5 81.4 all-gather.8
  208.5 80.5 all-gather.10
  316.4 88.0 reduce-scatter.2
  406.6 93.6 reduce-scatter.4

commit v6 on v5

--- a/solution.py
+++ b/solution.py
@@ -220,6 +220,22 @@
     return jnp.concatenate([values[:, start : start + piece] for start in starts], 1)
 
 
+def regroup_pairs(values, outer, inner):
+    piece = values.shape[1] // (outer * inner)
+    pair = 2 * piece
+    left = lax.broadcasted_iota(jnp.int32, (values.shape[0], pair), 1) < piece
+    slabs = {}
+    for o in range(0, outer, 2):
+        for i in range(0, inner, 2):
+            one, two = (
+                values[:, (k * inner + i) * piece : (k * inner + i) * piece + pair]
+                for k in (o, o + 1)
+            )
+            slabs[i, o] = jnp.where(left, one, pltpu.roll(two, piece, 1))
+            slabs[i + 1, o] = jnp.where(left, pltpu.roll(one, piece, 1), two)
+    return jnp.concatenate([slabs[i, o] for i in range(inner) for o in range(0, outer, 2)], 1)
+
+
 def row_norm(values):
     centred = values - jnp.mean(values, axis=-1, keepdims=True)
     inverse_std = lax.rsqrt(jnp.mean(centred * centred, axis=-1, keepdims=True) + EPS)
@@ -325,7 +341,9 @@
         hidden = tokens_ref[rows].astype(F32) + total + params_ref[0:1]
         hidden_ref[rows] = hidden
         normed, _ = row_norm(hidden)
-        return regroup(normed * params_ref[1:2] + params_ref[2:3], 4, fsdp).astype(BF16)
+        return regroup_pairs(
+            normed * params_ref[1:2] + params_ref[2:3], 4, fsdp
+        ).astype(BF16)
 
     exchange(
         Scatter(partial_ref, landing, passing, last, sems.at[0], near),
@@ -347,7 +365,7 @@
     sums_ref[...] = jnp.zeros_like(sums_ref)
 
     def rows_of(rows, total):
-        total = regroup(total, fsdp, 4)
+        total = regroup_pairs(total, fsdp, 4)
         normed, inverse_std = row_norm(hidden_ref[rows])
         upper = cotangent_ref[rows].astype(F32)
         grad = upper + row_back(total, normed, inverse_std, params_ref[1:2])
@@ -619,7 +637,7 @@
     columns = up_ref.shape[2]
     for slot in range(dp):
         up_across.receive(slot)
-        up_out[:, slot * columns : (slot + 1) * columns] = up_in[slot]
+        up_out[:, slot * columns : (slot + 1) * columns] = up_in[slot].astype(F32)
     small.end(4)
     small_out[...] = held[len(partners)]
     for slot in range(dp):
@@ -628,7 +646,7 @@
             start = (third * dp + slot) * part
             qkv_out[:, start : start + part] = qkv_in[
                 slot, :, third * part : (third + 1) * part
-            ]
+            ].astype(F32)
     paths(first.finish)
     paths(second.finish)
     for line in lines:
@@ -828,7 +846,7 @@
     table = lax.dynamic_update_slice(table, row, (rank, 0))
     wide = (4 * length, width)
     narrow = (length, width)
-    kernels = dp == 4 and fsdp == 8 and length % (32 * STEPS) == 0 and ff == dp * width
+    kernels = dp == 4 and fsdp == 8 and length % (32 * STEPS) == 0 and ff == dp * width and shard == 64
     stages = len(bits_of(fsdp)) + 2
     if kernels:
         all_tokens, grad_y, table = call_exchange(
@@ -961,8 +979,8 @@
         out_grad = local_out.reshape(1, fsdp, shard, width)
         grad_tokens, output, small, grad_w_qkv, grad_w_out, grad_w_up = call_exchange(
             functools.partial(last_kernel, fsdp), 4, 2, 2,
-            [(narrow, BF16), (narrow, BF16), (small.shape, F32), (w_qkv.shape, BF16),
-             ((1, shard, width), F32), (w_up.shape, BF16)],
+            [(narrow, BF16), (narrow, BF16), (small.shape, F32), (w_qkv.shape, F32),
+             ((1, shard, width), F32), (w_up.shape, F32)],
             [first_part, jnp.concatenate([gain1, down_b], 0), small,
              scattered_up.reshape(dp, shard, ff_part), output_part, tokens, hidden, grad_hidden,
              qkv_grad, out_grad],
@@ -981,7 +999,6 @@
             (2, stages), 6,
         )
         grad_w_out = grad_w_out[0]
-        grad_w_qkv, grad_w_up = grad_w_qkv.astype(F32), grad_w_up.astype(F32)
     else:
         grad_first = scatter_dp(first_part, dp)
         normed1, inverse1 = norm_stats(inputs)

time: 601 us -> 600 us (level)
    unnamed x62 -> x66, local copies, waits for them, and re-layouts: 8.22 us -> 12.2 us
  transfers between devices with their start and end apart: 6 -> 6, of which waited for: 1 -> 1; matrix products, arithmetic and copies ran while one was open for 20% -> 19% of each run, Pallas kernels for 61% -> 62%
where the time goes in v6:
time: 600 us; the launch traced here: 597 us
  Pallas kernels  367 us (61%)
  matrix products  123 us (20%)
  blocking collectives  32.6 us (5%)
  waiting for transfers between devices  23.4 us (4%)
  local copies, waits for them, and re-layouts  22.8 us (4%)
  between operations  14.8 us (2%)
  other arithmetic  13.1 us (2%)
    pallas_call x4, Pallas kernels, call_exchange(): pl.pallas_call(kernel, in_specs=[pl.BlockSpec(memory_space=pltpu.VMEM)] *...  333 us
    dot_general x4, matrix products, dot_nt(): lax.dot_general(a, b, (((1,), (1,)), ((), ())), preferred_element_type=F32)  45.2 us
    dot_general x4, matrix products, dot_tn(): lax.dot_general(a, b, (((0,), (0,)), ((), ())), preferred_element_type=F32)  41.6 us
    dot_general x3, matrix products, dot(): return jnp.dot(a, b, preferred_element_type=F32)  35.9 us
    pallas_call x1, Pallas kernels, attend_back(): pl.pallas_call(attend_back_kernel, grid=(rows // length,), in_specs=[pl.B...  22.2 us
    all_gather x1, waiting for transfers between devices, layer(): down_w = lax.all_gather(w_down, 'fsdp', axis=0, tiled=True)  21.6 us
    all_to_all x1, blocking collectives, layer(): lax.all_to_all(cols, 'dp', 1, 0, tiled=True).reshape(dp, shard, 3 * part)  16.6 us
    all_to_all x1, blocking collectives, layer(): ups = lax.all_to_all(w_up, 'dp', 1, 0, tiled=True)  16.1 us
  transfers between devices with their start and end apart: 6, of which 1 were waited for; matrix products, arithmetic and copies ran while one was open for 19% of the time, Pallas kernels for 62%

profile of v6, /device:TPU:0, one launch (start us, length us, event | category | flops | bytes accessed | tf_op | source)
XLA Modules:
  0.0 596.8 jit_solution(11898244601610461528)
XLA Ops:
  7.2 2.4 reshape.113
  11.3 16.6 %all_to_all.35 = bf16[64,4,1536]{2,0,1:T(8,128)(2,1)} all-to-all(bf16[64,4,1536]{2,0,1:T(8,128)(2,1)S(1)} %all_to_all.26), channel_id=1, replica_groups=mesh['dp'=4,'fsdp'=8] {'dp'}, dimensions={1} | all-to-all | bytes 1572864 | tf_op jit(solution)/shard_map/all_to_all | solution.py:835
  28.8 16.1 %all_to_all.36 = bf16[64,4,2048]{2,0,1:T(8,128)(2,1)} all-to-all(bf16[64,4,2048]{2,0,1:T(8,128)(2,1)S(1)} %bitcast.68), channel_id=1, replica_groups=mesh['dp'=4,'fsdp'=8] {'dp'}, dimensions={1} | all-to-all | bytes 2097152 | tf_op jit(solution)/shard_map/all_to_all | solution.py:838
  47.2 76.7 %shard_map.270 = (bf16[1024,2048]{1,0:T(8,128)(2,1)}, bf16[1024,2048]{1,0:T(8,128)(2,1)}, bf16[32,768]{1,0:T(8,128)(2,1)}) custom-call(bf16[256,2048]{1,0:T(8,128)(2,1)} %tokens_any.1, bf16[256,2048]{1,0:T(8,128)(2,1)} %cotangent_ref.1, bf16[32,768]{1,0:T(8,128)(2,1)} %copy-done.9), custom_call_target="tpu_custom_call" | custom-call | flops 2097152 | bytes 209715200 | tf_op jit(solution)/shard_map/pallas_call | solution.py:667
  127.1 3.0 convert_reduce_fusion
  132.3 12.7 %add_convert_fusion.qkv_ref = bf16[1024,1536]{1,0:T(8,128)(2,1)} fusion(bf16[2048,1536]{1,0:T(8,128)(2,1)} %bitcast.77, f32[1536]{0:T(1024)S(1)} %fusion.13, bf16[1024,2048]{1,0:T(8,128)(2,1)} %get-tuple-element.45, f32[2048]{0:T(1024)S(1)} %add.95, f32[2048]{0:T(1024)S(1)} %mul.93, f32[1024]{0:T(1024)S(1)} %add_rsqrt_fusion, ...), kind=kOutput, calls=%fused_computation.21 | convolution fusion | flops 6458179584 | bytes 13662208 | tf_op jit(solution)/shard_map/dot_general | solution.py:816
  145.0 11.6 %attend.1 = (bf16[1024,512]{1,0:T(8,128)(2,1)}, f32[32,128]{1,0:T(8,128)}) custom-call(f32[8]{0:T(128)} %exponential_multiply_fusion.slope_ref, f32[256,256]{1,0:T(8,128)} %convert_select_fusion.distance_ref, bf16[1024,1536]{1,0:T(8,128)(2,1)} %add_convert_fusion.qkv_ref), custom_call_target="tpu_custom_call" | custom-call | flops 536870912 | bytes 4194304 | tf_op jit(solution)/shard_map/attend/pallas_call | solution.py:753
  156.6 6.3 %convolution_convert_fusion.5.partial_ref = bf16[1024,2048]{1,0:T(8,128)(2,1)} fusion(bf16[1024,512]{1,0:T(8,128)(2,1)} %get-tuple-element.47, bf16[512,2048]{1,0:T(8,128)(2,1)} %all-gather.7.cloned.1.call-done), kind=kOutput, calls=%fused_computation.24 | convolution fusion | flops 2149580800 | bytes 7340032 | tf_op jit(solution)/shard_map/dot_general | solution.py:816
  162.9 74.0 %shard_map.271 = (bf16[1024,2048]{1,0:T(8,128)(2,1)}, f32[256,2048]{1,0:T(8,128)}) custom-call(bf16[1024,2048]{1,0:T(8,128)(2,1)} %convolution_convert_fusion.5.partial_ref, bf16[256,2048]{1,0:T(8,128)(2,1)} %tokens_any.1, f32[3,2048]{1,0:T(4,128)} %pad_maximum_fusion.params_ref), custom_call_target="tpu_custom_call" | custom-call | flops 2097152 | bytes 209715200 | tf_op jit(solution)/shard_map/pallas_call | solution.py:667
  236.9 16.9 %fusion.10 = (bf16[1024,2048]{1,0:T(8,128)(2,1)}, bf16[1024,2048]{1,0:T(8,128)(2,1)S(1)}) fusion(f32[2048]{0:T(1024)S(1)} %bitcast.76, bf16[1024,2048]{1,0:T(8,128)(2,1)} %get-tuple-element.48, bf16[2048,2048]{1,0:T(8,128)(2,1)} %all-gather.9.cloned.1.call-done), kind=kOutput, calls=%fused_computation.13 | convolution fusion | flops 8615100416 | bytes 20979712 | tf_op jit(solution)/shard_map/dot_general | solution.py:816
  255.9 11.5 %convolution_convert_fusion.2 = bf16[2048,2048]{1,0:T(8,128)(2,1)} fusion(bf16[1024,2048]{1,0:T(8,128)(2,1)S(1)} %get-tuple-element.50.active_ref, bf16[1024,2048]{1,0:T(8,128)(2,1)S(1)} %copy-done.21), kind=kOutput, calls=%fused_computation.20 | convolution fusion | flops 8594128896 | bytes 16777216 | tf_op jit(solution)/shard_map/dot_general | solution.py:702
  267.4 21.6 %all-gather.11.cloned.1.call-done.weight_ref = bf16[2048,2048]{1,0:T(8,128)(2,1)} async-done(((bf16[256,2048]{1,0:T(8,128)(2,1)}), bf16[2048,2048]{1,0:T(8,128)(2,1)}) %all-gather.11.cloned.1.call-update) | async-done | bytes 8388624 | tf_op jit(solution)/shard_map/all_gather | solution.py:840
  289.0 13.8 %convert_reduce_fusion.1 = (f32[2048]{0:T(1024)S(1)}, bf16[1024,2048]{1,0:T(8,128)(2,1)S(1)}) fusion(bf16[1024,2048]{1,0:T(8,128)(2,1)} %get-tuple-element.52, bf16[1024,2048]{1,0:T(8,128)(2,1)} %get-tuple-element.51, bf16[2048,2048]{1,0:T(8,128)(2,1)} %all-gather.11.cloned.1.call-done.weight_ref), kind=kOutput, calls=%fused_computation.14 | convolution fusion | flops 8600418304 | bytes 20979712 | tf_op jit(solution)/shard_map/dot_general | solution.py:698
  304.8 11.4 %convolution_convert_fusion.1 = bf16[2048,2048]{1,0:T(8,128)(2,1)} fusion(bf16[1024,2048]{1,0:T(8,128)(2,1)S(1)} %copy-done.22, bf16[1024,2048]{1,0:T(8,128)(2,1)S(1)} %get-tuple-element.53), kind=kOutput, calls=%fused_computation.19 | convolution fusion | flops 8594128896 | bytes 16777216 | tf_op jit(solution)/shard_map/dot_general | solution.py:702
  318.4 14.8 %convolution_convert_fusion.4.partial_ref = bf16[1024,2048]{1,0:T(8,128)(2,1)} fusion(bf16[1024,2048]{1,0:T(8,128)(2,1)} %copy-done.24, bf16[2048,2048]{1,0:T(8,128)(2,1)} %all-gather.9.cloned.1.call-done), kind=kOutput, calls=%fused_computation.23 | convolution fusion | flops 8592031744 | bytes 16777216 | tf_op jit(solution)/shard_map/dot_general | solution.py:698
  333.2 79.5 %shard_map.272 = (bf16[1024,2048]{1,0:T(8,128)(2,1)}, f32[256,2048]{1,0:T(8,128)}, f32[8,2048]{1,0:T(8,128)}, bf16[1024,2048]{1,0:T(8,128)(2,1)}) custom-call(bf16[1024,2048]{1,0:T(8,128)(2,1)} %convolution_convert_fusion.4.partial_ref, f32[256,2048]{1,0:T(8,128)} %get-tuple-element.54.hidden_ref.hidden_any, bf16[256,2048]{1,0:T(8,128)(2,1)} %cotangent_ref.1, ...), custom_call_target="tpu_custom_call" | custom-call | flops 2097152 | bytes 209715200 | tf_op jit(solution)/shard_map/pallas_call | solution.py:667
  412.7 5.5 convolution_convert_fusion.7.grad_ref
  418.2 22.2 %attend_back.1 = bf16[1024,1536]{1,0:T(8,128)(2,1)} custom-call(f32[8]{0:T(128)} %exponential_multiply_fusion.slope_ref, f32[256,256]{1,0:T(8,128)} %convert_select_fusion.distance_ref, bf16[1024,1536]{1,0:T(8,128)(2,1)} %add_convert_fusion.qkv_ref, bf16[1024,512]{1,0:T(8,128)(2,1)} %convolution_convert_fusion.7.grad_ref), custom_call_target="tpu_custom_call" | custom-call | flops 1342177280 | bytes 7340032 | tf_op jit(solution)/shard_map/attend_back/pallas_call | solution.py:780
  440.4 12.4 %convolution_convert_fusion = bf16[2048,1536]{1,0:T(8,128)(2,1)} fusion(bf16[1024,1536]{1,0:T(8,128)(2,1)} %attend_back.1, bf16[1024,2048]{1,0:T(8,128)(2,1)} %get-tuple-element.45, f32[2048]{0:T(1024)S(1)} %add.95, f32[2048]{0:T(1024)S(1)} %mul.93, f32[1024]{0:T(1024)S(1)} %add_rsqrt_fusion, f32[1024]{0:T(1024)S(1)} %broadcast_multiply_fusion), kind=kOutput, calls=%fused_computation.18 | convolution fusion | flops 6458179584 | bytes 13656064 | tf_op jit(solution)/shard_map/dot_general | solution.py:702
  454.9 6.2 %convolution_convert_fusion.6 = bf16[512,2048]{1,0:T(8,128)(2,1)} fusion(bf16[1024,512]{1,0:T(8,128)(2,1)} %get-tuple-element.47, bf16[1024,2048]{1,0:T(8,128)(2,1)} %get-tuple-element.61), kind=kOutput, calls=%fused_computation.25 | convolution fusion | flops 2148532224 | bytes 7340032 | tf_op jit(solution)/shard_map/dot_general | solution.py:702
  461.1 11.1 %convolution_convert_fusion.3.first_ref = bf16[1024,2048]{1,0:T(8,128)(2,1)} fusion(bf16[1024,1536]{1,0:T(8,128)(2,1)S(1)} %copy-done.1, bf16[2048,1536]{1,0:T(8,128)(2,1)} %bitcast.78), kind=kOutput, calls=%fused_computation.22 | convolution fusion | flops 6444548096 | bytes 13631488 | tf_op jit(solution)/shard_map/dot_general | solution.py:698
  472.2 103.2 %shard_map.273 = (bf16[256,2048]{1,0:T(8,128)(2,1)}, bf16[256,2048]{1,0:T(8,128)(2,1)}, f32[16,2048]{1,0:T(8,128)}, f32[64,6144]{1,0:T(8,128)}, f32[1,64,2048]{2,1,0:T(8,128)}, /*index=5*/f32[64,8192]{1,0:T(8,128)}) custom-call(bf16[1024,2048]{1,0:T(8,128)(2,1)} %convolution_convert_fusion.3.first_ref, f32[2,2048]{1,0:T(2,128)} %pad_maximum_fusion.3.params_ref, ...), custom_call_target="tpu_custom_call" | custom-call | flops 2097152 | bytes 209715200 | tf_op jit(solution)/shard_map/pallas_call | solution.py:667
  580.3 2.8 convert_element_type.95
  583.1 2.5 copy.59
  (132 shorter events, 27.3 us)
Async XLA Ops:
  7.2 21.5 %copy-start.6 = (bf16[64,8192]{1,0:T(8,128)(2,1)S(1)}, bf16[64,8192]{1,0:T(8,128)(2,1)}, u32[]{:S(2)}) copy-start(bf16[64,8192]{1,0:T(8,128)(2,1)} %param.24) | copy-start | bytes 3145732
  7.2 125.1 %all-gather.5.cloned.1.call-start = ((), (), s32[]{:S(2)}) async-start(), calls=%async_computation.4 | async-start | bytes 7077888 | tf_op jit(solution)/shard_map/all_gather | solution.py:836
  11.2 34.4 %copy-start.12 = (bf16[64]{0:T(256)(128)(2,1)S(1)}, bf16[64]{0:T(256)(128)(2,1)}, u32[]{:S(2)}) copy-start(bf16[64]{0:T(256)(128)(2,1)} %param.21) | copy-start | bytes 388
  11.2 34.4 %copy-start.13 = (bf16[64]{0:T(256)(128)(2,1)S(1)}, bf16[64]{0:T(256)(128)(2,1)}, u32[]{:S(2)}) copy-start(bf16[64]{0:T(256)(128)(2,1)} %param.22) | copy-start | bytes 388
  11.2 34.3 %copy-start.14 = (bf16[64]{0:T(256)(128)(2,1)S(1)}, bf16[64]{0:T(256)(128)(2,1)}, u32[]{:S(2)}) copy-start(bf16[64]{0:T(256)(128)(2,1)} %param.23) | copy-start | bytes 388
  11.2 34.3 %copy-start.15 = (bf16[64]{0:T(256)(128)(2,1)S(1)}, bf16[64]{0:T(256)(128)(2,1)}, u32[]{:S(2)}) copy-start(bf16[64]{0:T(256)(128)(2,1)} %param.27) | copy-start | bytes 388
  11.2 34.3 %copy-start.16 = (bf16[64]{0:T(256)(128)(2,1)S(1)}, bf16[64]{0:T(256)(128)(2,1)}, u32[]{:S(2)}) copy-start(bf16[64]{0:T(256)(128)(2,1)} %param.28) | copy-start | bytes 388
  11.2 34.3 %copy-start.17 = (bf16[64]{0:T(256)(128)(2,1)S(1)}, bf16[64]{0:T(256)(128)(2,1)}, u32[]{:S(2)}) copy-start(bf16[64]{0:T(256)(128)(2,1)} %param.29) | copy-start | bytes 388
  11.2 34.3 %copy-start.18 = (bf16[64]{0:T(256)(128)(2,1)S(1)}, bf16[64]{0:T(256)(128)(2,1)}, u32[]{:S(2)}) copy-start(bf16[64]{0:T(256)(128)(2,1)} %param.18) | copy-start | bytes 388
  11.2 34.3 %copy-start.19 = (bf16[64]{0:T(256)(128)(2,1)S(1)}, bf16[64]{0:T(256)(128)(2,1)}, u32[]{:S(2)}) copy-start(bf16[64]{0:T(256)(128)(2,1)} %param.19) | copy-start | bytes 388
  11.3 34.3 %copy-start.20 = (bf16[256]{0:T(256)(128)(2,1)S(1)}, bf16[256]{0:T(256)(128)(2,1)}, u32[]{:S(2)}) copy-start(bf16[256]{0:T(256)(128)(2,1)} %param.25) | copy-start | bytes 1540
  27.8 128.8 %all-gather.7.cloned.1.call-start = ((), (), s32[]{:S(2)}) async-start(), calls=%async_computation.5 | async-start | bytes 2359296 | tf_op jit(solution)/shard_map/all_gather | solution.py:833
  28.6 208.3 %all-gather.9.cloned.1.call-start = ((), (), s32[]{:S(2)}) async-start(), calls=%async_computation.6 | async-start | bytes 9437184 | tf_op jit(solution)/shard_map/all_gather | solution.py:839
  44.9 244.1 %all-gather.11.cloned.1.call-start = ((), (), s32[]{:S(2)}) async-start(), calls=%async_computation.7 | async-start | bytes 9437184 | tf_op jit(solution)/shard_map/all_gather | solution.py:840
  45.5 426.7 %reduce-scatter.3.cloned.1.call-start = ((), (), s32[]{:S(2)}) async-start(), calls=%async_computation.8 | async-start | bytes 9437184 | tf_op jit(solution)/shard_map/reduce_scatter | solution.py:916
  236.9 19.0 %copy-start.21 = (bf16[1024,2048]{1,0:T(8,128)(2,1)S(1)}, bf16[1024,2048]{1,0:T(8,128)(2,1)}, u32[]{:S(2)}) copy-start(bf16[1024,2048]{1,0:T(8,128)(2,1)} %get-tuple-element.51) | copy-start | bytes 12582916
  289.0 15.8 %copy-start.22 = (bf16[1024,2048]{1,0:T(8,128)(2,1)S(1)}, bf16[1024,2048]{1,0:T(8,128)(2,1)}, u32[]{:S(2)}) copy-start(bf16[1024,2048]{1,0:T(8,128)(2,1)} %get-tuple-element.48) | copy-start | bytes 12582916
  316.2 264.1 %reduce-scatter.5.cloned.1.call-start = ((), (), s32[]{:S(2)}) async-start(), calls=%async_computation.9 | async-start | bytes 9437184 | tf_op jit(solution)/shard_map/reduce_scatter | solution.py:899
  333.2 79.5 %copy-start.23 = (bf16[512,2048]{1,0:T(8,128)(2,1)S(1)}, bf16[512,2048]{1,0:T(8,128)(2,1)}, u32[]{:S(2)}) copy-start(bf16[512,2048]{1,0:T(8,128)(2,1)} %all-gather.7.cloned.1.call-done) | copy-start | bytes 6291460
  440.4 12.4 %copy-start.10 = (f32[8,2048]{1,0:T(8,128)S(1)}, f32[8,2048]{1,0:T(8,128)}, u32[]{:S(2)}) copy-start(f32[8,2048]{1,0:T(8,128)} %get-tuple-element.57) | copy-start | bytes 196612
  440.4 12.5 %copy-start.1 = (bf16[1024,1536]{1,0:T(8,128)(2,1)S(1)}, bf16[1024,1536]{1,0:T(8,128)(2,1)}, u32[]{:S(2)}) copy-start(bf16[1024,1536]{1,0:T(8,128)(2,1)} %attend_back.1) | copy-start | bytes 9437188
  472.2 107.1 %copy-start.3 = (bf16[64,6144]{1,0:T(8,128)(2,1)S(1)}, bf16[64,6144]{1,0:T(8,128)(2,1)}, u32[]{:S(2)}) copy-start(bf16[64,6144]{1,0:T(8,128)(2,1)} %param.17) | copy-start | bytes 2359300
  575.4 10.2 %copy-start.7 = (bf16[256,2048]{1,0:T(8,128)(2,1)S(1)}, bf16[256,2048]{1,0:T(8,128)(2,1)}, u32[]{:S(2)}) copy-start(bf16[256,2048]{1,0:T(8,128)(2,1)} %get-tuple-element.107) | copy-start | bytes 3145732
  579.3 7.2 %copy-start.5 = (f32[64,6144]{1,0:T(8,128)S(1)}, f32[64,6144]{1,0:T(8,128)}, u32[]{:S(2)}) copy-start(f32[64,6144]{1,0:T(8,128)} %get-tuple-element.108) | copy-start | bytes 4718596
  (7 other events, 20.7 us)
Sparse Core Ops, SparseCore 0:
  28.0 66.4 all-gather.4
  96.1 27.7 all-gather.6
  125.5 81.4 all-gather.8
  208.4 80.5 all-gather.10
  316.3 88.0 reduce-scatter.2
  406.5 93.6 reduce-scatter.4
